TPU v7x, 128 devices: a whole 4x4x4 slice. The times are simulated.
128 devices in a mesh: gx: 16 (over y, z), gy: 8 (over x, core).
Axes of the slice: x: 4, y: 4, z: 4, core: 2. Of those that a mesh axis runs over, the one named last changes fastest.
Arguments:
- snapshots: bfloat16 [16, 16, 4, 2048, 512], P('gx', 'gy'), may hold values from -120 to 120
- basis: bfloat16 [16, 16, 4, 24, 2048], P('gx', 'gy'), may hold values from -0.0625 to 0.0625
- node_counts: int32 [16, 16], P('gx', 'gy'), may hold values from 1024 to 2048, as said below
- adjacency: int32 [16, 16, 3], P('gx', 'gy'), may hold values from 0 to 255, as said below
Outputs:
- operator: float32 [16, 16, 397, 24], P('gx', 'gy')
- reduced_states: float32 [16, 16, 24, 512], P('gx', 'gy')
Inputs may be any that keep to these rules, and one draw needn't show every extreme that they name: Node slot n of subdomain g is live iff n < node_counts[g]; at least 1024 slots are live, and one subdomain has all 2048 live. Subdomain (row, col) has id row * 16 + col. Each row of adjacency holds 3 distinct ids other than its own subdomain's, each within one subdomain row and one subdomain column of it.
All inputs are finite; a program needn't handle non-finite values.
Results may differ from a plain program's by a relative error of at most 0.0003.
Values sent between devices are 32-bit elements; how exact they have to be, the bound alone decides.
No kernel may reach another device: no remote copies, remote signals or barrier semaphores. Data moves between devices by JAX's collectives and lax.ppermute only.
A program may use at most 64 MiB of HBM per device.

v0:
```python
import jax
import jax.numpy as jnp
from jax import lax
from jax.sharding import Mesh
from jax.sharding import PartitionSpec as P

GX = ("gx_0", "gx_1")
GY = ("gy_0", "gy_1")
GX_GY = ("gx_0", "gx_1", "gy_0", "gy_1")


beta_linear = 0.5
beta_quad = 0.5


def one_axis_at_a_time(x, axes):
    for axis in axes:
        x = lax.psum(x, axis)
    return x


def padded_2(cells, sides, width):
    for axis, dim in sides:
        count = lax.axis_size(axis)
        ends = count - 1
        head = lax.slice_in_dim(cells, 0, width, axis=dim)
        tail = lax.slice_in_dim(cells, cells.shape[dim] - width, cells.shape[dim], axis=dim)
        cells = jnp.concatenate(
            [
                lax.ppermute(tail, axis, [(i, (i + 1) % count) for i in range(ends)]),
                cells,
                lax.ppermute(head, axis, [((i + 1) % count, i) for i in range(ends)]),
            ],
            axis=dim,
        )
    return cells


def build_features(state, near):
    ranks = state.shape[1]
    steps = state.shape[2]
    pieces = [
        jnp.ones((state.shape[0], 1, steps), jnp.float32),
        state,
        near.reshape(state.shape[0], -1, steps),
    ]
    for first in range(ranks):
        pieces.append(state[:, first : first + 1] * state[:, first:])
    return jnp.concatenate(pieces, axis=1)


def pick_rows(pieces, links):
    ids = jnp.arange(pieces.shape[0], dtype=jnp.int32)
    hits = (links[:, :, None] == ids[None, None, :]).astype(jnp.float32)
    return jnp.einsum("sbn,nrk->sbrk", hits, pieces, precision=lax.Precision.HIGHEST)


def solve_one(gram, rhs):
    factor = jnp.linalg.cholesky(gram)
    middle = jax.scipy.linalg.solve_triangular(factor, rhs, lower=True)
    return jax.scipy.linalg.solve_triangular(factor, middle, lower=True, trans=1)


def body(snapshots, basis, node_counts, adjacency):
    values = snapshots[0]
    modes = basis[0]
    counts = node_counts[0]
    links = adjacency[0]
    columns = values.shape[0]
    slots = values.shape[2]
    steps = values.shape[3]
    ranks = modes.shape[2]
    live = jnp.arange(slots, dtype=jnp.int32)[None, :] < counts[:, None]
    masked = modes * live.astype(jnp.bfloat16)[:, None, None, :]
    proj = jnp.einsum("svrp,svpk->svrk", masked, values, preferred_element_type=jnp.float32)
    slotsq = jnp.einsum("svpk,svpk->svp", values, values, preferred_element_type=jnp.float32)
    squares = jnp.sum(slotsq * live.astype(jnp.float32)[:, None, :], axis=(0, 2))
    nodes = jnp.sum(counts.astype(jnp.float32))
    total_subs = lax.axis_size(GX) * lax.axis_size(GY) * columns
    grid_cols = columns * lax.axis_size(GY)
    near_row = links // grid_cols
    near_col = links % grid_cols
    local = (near_row - lax.axis_index(GX) + 1) * (columns + 2) + (
        near_col - lax.axis_index(GY) * columns + 1
    )
    cross = jnp.einsum("svrk,swrk->vw", proj, proj, precision=lax.Precision.HIGHEST)
    sq_all, nodes_all, cross_all = (
        one_axis_at_a_time(squares, GX_GY),
        one_axis_at_a_time(nodes, GX_GY),
        one_axis_at_a_time(cross, GX_GY),
    )
    scale = jnp.sqrt(sq_all / (nodes_all * steps) + 1e-06)
    states = jnp.sum(proj / scale[None, :, None, None], axis=1)
    gnorm = jnp.sum(cross_all / (scale[:, None] * scale[None, :])) / (total_subs * ranks * steps)
    padded = padded_2(states[None], ((GX, 0), (GY, 1)), 1)
    flat = padded.reshape(-1, ranks, steps)
    near = pick_rows(flat, local)
    nbrs = links.shape[1]
    feats = build_features(states, near)
    past = feats[:, :, :-1]
    nlin = 1 + ranks + nbrs * ranks
    nquad = ranks * (ranks + 1) // 2
    reg_diag = steps * jnp.concatenate(
        [
            jnp.full((nlin,), beta_linear, jnp.float32) * gnorm,
            jnp.full((nquad,), beta_quad, jnp.float32) * gnorm * gnorm,
        ]
    )
    gram = (
        jnp.einsum("sfk,sgk->sfg", past, past, precision=lax.Precision.HIGHEST)
        + jnp.diag(reg_diag)[None]
    )
    rhs = jnp.einsum("sfk,srk->sfr", past, states[:, :, 1:], precision=lax.Precision.HIGHEST)
    operator = jax.vmap(solve_one)(gram, rhs)
    return (operator[None], states[None])


def solution(mesh):
    split = Mesh(mesh.devices.reshape(4, 4, 4, 2), ("gx_0", "gx_1", "gy_0", "gy_1"))
    placed = (P(GX, GY, None, None, None), P(GX, GY, None, None, None), P(GX, GY), P(GX, GY, None))
    return jax.shard_map(
        body,
        mesh=split,
        in_specs=placed,
        out_specs=(P(GX, GY, None, None), P(GX, GY, None, None)),
        check_vma=False,
    )
```

profile of v0, /device:TPU:1, one launch (start us, length us, event | category | flops | bytes accessed | tf_op | source)
XLA Modules:
  0.0 333.4 jit_solution(6899208880659183131)
XLA Ops:
  1.4 7.5 %fusion = f32[2,4,2048]{2,1,0:T(4,128)S(1)} fusion(bf16[1,2,4,2048,512]{4,3,2,1,0:T(8,128)(2,1)} %param.4), kind=kLoop, calls=%fused_computation.3 | loop fusion | flops 25149440 | bytes 16842752 | tf_op jit(solution)/shard_map/svpk,svpk->svp/dot_general | solution.py:76
  8.9 3.2 copy-done
  12.0 3.4 %fusion.1 = f32[2,4,24,512]{3,2,1,0:T(8,128)S(1)} fusion(bf16[1,2,4,2048,512]{4,3,2,1,0:T(8,128)(2,1)S(1)} %copy-done, bf16[1,2,4,24,2048]{4,3,2,1,0:T(8,128)(2,1)} %param.5, bf16[2,2048]{1,0:T(2,128)(2,1)S(1)} %get-tuple-element.70), kind=kOutput, calls=%fused_computation.4 | convolution fusion | flops 403046400 | bytes 17965056 | tf_op jit(solution)/shard_map/svrp,svpk->svrk/dot_general | solution.py:75
  15.5 1.9 convolution_bitcast_fusion
  18.1 10.1 %all-reduce.6 = (f32[4]{0:T(128)S(1)}, f32[]{:T(128)}, f32[4,4]{1,0:T(4,128)S(1)}) all-reduce(f32[4]{0:T(128)S(1)} %multiply_reduce_fusion, f32[]{:T(128)} %convert_reduce_fusion, f32[4,4]{1,0:T(4,128)S(1)} %convolution_bitcast_fusion), channel_id=1, replica_groups=mesh['gx_0'=4,'gx_1'=4,'gy_0'=4,'gy_1'=2] {'gx_0'}, use_global_device_ids=true, to_apply=%region_1.0 | all-reduce | flops 21 | bytes 168 | tf_op jit(solution)/shard_map/psum | solution.py:18
  28.3 10.4 %all-reduce.5 = (f32[4]{0:T(128)S(1)}, f32[]{:T(128)}, f32[4,4]{1,0:T(4,128)S(1)}) all-reduce(f32[4]{0:T(128)S(1)} %get-tuple-element.27, f32[]{:T(128)} %get-tuple-element.28, f32[4,4]{1,0:T(4,128)S(1)} %get-tuple-element.29), channel_id=1, replica_groups=mesh['gx_0'=4,'gx_1'=4,'gy_0'=4,'gy_1'=2] {'gx_1'}, use_global_device_ids=true, to_apply=%region_2.3 | all-reduce | flops 21 | bytes 168 | tf_op jit(solution)/shard_map/psum | solution.py:18
  38.6 9.1 %all-reduce.4 = (f32[4]{0:T(128)S(1)}, f32[]{:T(128)}, f32[4,4]{1,0:T(4,128)S(1)}) all-reduce(f32[4]{0:T(128)S(1)} %get-tuple-element.24, f32[]{:T(128)} %get-tuple-element.25, f32[4,4]{1,0:T(4,128)S(1)} %get-tuple-element.26), channel_id=1, replica_groups=mesh['gx_0'=4,'gx_1'=4,'gy_0'=4,'gy_1'=2] {'gy_0'}, use_global_device_ids=true, to_apply=%region_3.4 | all-reduce | flops 21 | bytes 168 | tf_op jit(solution)/shard_map/psum | solution.py:18
  47.7 9.5 %all-reduce.7 = (f32[4]{0:T(128)S(1)}, f32[]{:T(128)}, f32[4,4]{1,0:T(4,128)S(1)}) all-reduce(f32[4]{0:T(128)S(1)} %get-tuple-element.21, f32[]{:T(128)} %get-tuple-element.22, f32[4,4]{1,0:T(4,128)S(1)} %get-tuple-element.23), channel_id=1, replica_groups=mesh['gx_0'=4,'gx_1'=4,'gy_0'=4,'gy_1'=2] {'gy_1'}, use_global_device_ids=true, to_apply=%region_4.5 | all-reduce | flops 21 | bytes 168 | tf_op jit(solution)/shard_map/psum | solution.py:18
  59.3 4.0 %collective-permute-start = (f32[1,2,24,512]{3,2,1,0:T(8,128)S(1)}, f32[1,2,24,512]{3,2,1,0:T(8,128)S(1)}, u32[]{:S(2)}, u32[]{:S(2)}) collective-permute-start(f32[1,2,24,512]{3,2,1,0:T(8,128)S(1)} %bitcast.156), channel_id=1, source_target_pairs={{0,8},{8,16},{16,24},{24,32},{32,40},{40,48},{48,56},{56,64},{64,7... | collective-permute-start | bytes 294920 | tf_op jit(solution)/shard_map/ppermute | solution.py:30
  72.9 1.4 fusion.9
  74.9 2.0 collective-permute-start.2
  77.0 2.5 collective-permute-start.3
  80.8 2.7 collective-permute-done.3
  84.3 8.0 %concatenate.48 = f32[2,397,512]{2,1,0:T(8,128)S(1)} concatenate(f32[2,1,512]{2,1,0:T(1,128)S(1)} %broadcast_in_dim.45, f32[2,24,512]{2,1,0:T(8,128)S(1)} %divide_reduce_fusion, f32[2,72,512]{2,1,0:T(8,128)S(1)} %bitcast.161, f32[2,24,512]{2,1,0:T(8,128)S(1)} %broadcast_multiply_fusion, f32[2,23,512]{2,1,0:T(8,128)S(1)} %slice_multiply_fusion.6, ...), dimensions={1} | concatenate | bytes 3252224 | tf_op jit(solution)/shard_map/concatenate | solution.py:49
  92.4 1.5 fusion.5
  93.9 2.8 fusion.7
  97.4 2.0 fusion.4
  100.6 23.5 %custom-call.38 = f32[2,128,128]{2,1,0:T(8,128)S(1)} custom-call(f32[2,128,128]{2,1,0:T(8,128)S(1)} %cholesky.281), custom_call_target="Cholesky" | custom-call | tf_op jit(solution)/shard_map/vmap(jit(cholesky))/cholesky | solution.py:59
  124.1 19.9 %custom-call.39 = f32[2,1,128,128]{2,3,1,0:T(8,128)S(1)} custom-call(f32[2,1,128,128]{3,2,1,0:T(8,128)S(1)} %select_bitcast_fusion.2), custom_call_target="InvertDiagBlocksLowerTriangular" | custom-call | tf_op jit(solution)/shard_map/vmap(jit(cholesky))/cholesky | solution.py:59
  144.2 1.4 constant_dynamic-update-slice_fusion.3
  145.6 1.4 convolution_subtract_fusion
  147.0 23.5 %custom-call.40 = f32[2,128,128]{2,1,0:T(8,128)S(1)} custom-call(f32[2,128,128]{2,1,0:T(8,128)S(1)} %cholesky.285), custom_call_target="Cholesky" | custom-call | tf_op jit(solution)/shard_map/vmap(jit(cholesky))/cholesky | solution.py:59
  170.5 19.7 %custom-call.41 = f32[2,1,128,128]{2,3,1,0:T(8,128)S(1)} custom-call(f32[2,1,128,128]{3,2,1,0:T(8,128)S(1)} %get-tuple-element.39), custom_call_target="InvertDiagBlocksLowerTriangular" | custom-call | tf_op jit(solution)/shard_map/vmap(jit(cholesky))/cholesky | solution.py:59
  190.5 1.3 convolution_subtract_fusion.1
  191.8 23.7 %custom-call.42 = f32[2,128,128]{2,1,0:T(8,128)S(1)} custom-call(f32[2,128,128]{2,1,0:T(8,128)S(1)} %cholesky.290), custom_call_target="Cholesky" | custom-call | tf_op jit(solution)/shard_map/vmap(jit(cholesky))/cholesky | solution.py:59
  215.9 19.7 %custom-call.43 = f32[2,1,128,128]{2,3,1,0:T(8,128)S(1)} custom-call(f32[2,1,128,128]{3,2,1,0:T(8,128)S(1)} %get-tuple-element.37), custom_call_target="InvertDiagBlocksLowerTriangular" | custom-call | tf_op jit(solution)/shard_map/vmap(jit(cholesky))/cholesky | solution.py:59
  236.8 2.4 custom-call.44
  240.7 7.9 %while.1 = (s32[]{:T(128)}, f32[2,397,397]{2,1,0:T(8,128)S(1)}, s32[3,2]{0,1:T(2,128)S(1)}, f32[3,2,128,128]{3,2,0,1:T(8,128)}, s32[]{:T(128)}) while((s32[]{:T(128)}, f32[2,397,397]{2,1,0:T(8,128)S(1)}, s32[3,2]{0,1:T(2,128)S(1)}, f32[3,2,128,128]{3,2,0,1:T(8,128)}, s32[]{:T(128)}) %tuple.67), condition=%wide.while_cond, body=%wide.while_body.sunk | while | flops 2 | bytes 263277 | solution.py:61
  241.3 2.0 bitcast_dynamic-update-slice_fusion.2
  244.0 2.0 bitcast_dynamic-update-slice_fusion.2
  246.6 2.0 bitcast_dynamic-update-slice_fusion.2
  249.7 78.6 %custom-call.45 = f32[2,4,128,128]{2,3,1,0:T(8,128)S(1)} custom-call(f32[2,4,128,128]{3,2,1,0:T(8,128)S(1)} %pad_maximum_fusion.1), custom_call_target="InvertDiagBlocksLowerTriangular" | custom-call | tf_op jit(solution)/shard_map/vmap(jit(_solve_triangular))/triangular_solve | solution.py:61
  (125 shorter events, 26.2 us)
Async XLA Ops:
  1.4 10.7 %copy-start = (bf16[1,2,4,2048,512]{4,3,2,1,0:T(8,128)(2,1)S(1)}, bf16[1,2,4,2048,512]{4,3,2,1,0:T(8,128)(2,1)}, u32[]{:S(2)}) copy-start(bf16[1,2,4,2048,512]{4,3,2,1,0:T(8,128)(2,1)} %param.4) | copy-start | bytes 50331652
  12.0 5.5 %copy-start.7 = (s32[1,2]{1,0:T(1,128)S(1)}, s32[1,2]{1,0:T(1,128)}, u32[]{:S(2)}) copy-start(s32[1,2]{1,0:T(1,128)} %param.6) | copy-start | bytes 28
  58.0 34.4 %copy-start.1 = (f32[2,24,512]{2,1,0:T(8,128)}, f32[2,24,512]{2,1,0:T(8,128)S(1)}, u32[]{:S(2)}) copy-start(f32[2,24,512]{2,1,0:T(8,128)S(1)} %divide_reduce_fusion) | copy-start | bytes 294916
  58.0 16.9 %collective-permute-start.1 = (f32[1,2,24,512]{3,2,1,0:T(8,128)S(1)}, f32[1,2,24,512]{3,2,1,0:T(8,128)S(1)}, u32[]{:S(2)}, u32[]{:S(2)}) collective-permute-start(f32[1,2,24,512]{3,2,1,0:T(8,128)S(1)} %bitcast.155), channel_id=1, source_target_pairs={{8,0},{16,8},{24,16},{32,24},{40,32},{48,40},{56,48},{64,56},{72,6... | collective-permute-start | bytes 294920 | tf_op jit(solution)/shard_map/ppermute | solution.py:32
  59.3 15.6 %collective-permute-start = (f32[1,2,24,512]{3,2,1,0:T(8,128)S(1)}, f32[1,2,24,512]{3,2,1,0:T(8,128)S(1)}, u32[]{:S(2)}, u32[]{:S(2)}) collective-permute-start(f32[1,2,24,512]{3,2,1,0:T(8,128)S(1)} %bitcast.156), channel_id=1, source_target_pairs={{0,8},{8,16},{16,24},{24,32},{32,40},{40,48},{48,56},{56,64},{64,7... | collective-permute-start | bytes 294920 | tf_op jit(solution)/shard_map/ppermute | solution.py:30
  72.6 1.7 copy-start.6
  74.9 5.8 %collective-permute-start.2 = (f32[3,1,24,512]{3,2,1,0:T(8,128)S(1)}, f32[3,1,24,512]{3,2,1,0:T(8,128)S(1)}, u32[]{:S(2)}, u32[]{:S(2)}) collective-permute-start(f32[3,1,24,512]{3,2,1,0:T(8,128)S(1)} %get-tuple-element.35), channel_id=1, source_target_pairs={{0,1},{1,2},{2,3},{3,4},{4,5},{5,6},{6,7},{8,9},{9,10},{10,11},{11... | collective-permute-start | bytes 442376 | tf_op jit(solution)/shard_map/ppermute | solution.py:30
  77.0 6.5 %collective-permute-start.3 = (f32[3,1,24,512]{3,2,1,0:T(8,128)S(1)}, f32[3,1,24,512]{3,2,1,0:T(8,128)S(1)}, u32[]{:S(2)}, u32[]{:S(2)}) collective-permute-start(f32[3,1,24,512]{3,2,1,0:T(8,128)S(1)} %get-tuple-element.36), channel_id=1, source_target_pairs={{1,0},{2,1},{3,2},{4,3},{5,4},{6,5},{7,6},{9,8},{10,9},{11,10},{12... | collective-permute-start | bytes 442376 | tf_op jit(solution)/shard_map/ppermute | solution.py:32
  99.4 1.2 copy-start.2
  145.6 69.9 %copy-start.4 = (pred[128,128]{1,0:T(8,128)(4,1)S(1)}, pred[128,128]{1,0:T(8,128)(4,1)}, u32[]{:S(2)}) copy-start(pred[128,128]{1,0:T(8,128)(4,1)} %get-tuple-element.96) | copy-start | bytes 49156
  147.0 92.2 %copy-start.5 = (pred[13,13]{1,0:T(8,128)(4,1)S(1)}, pred[13,13]{1,0:T(8,128)(4,1)}, u32[]{:S(2)}) copy-start(pred[13,13]{1,0:T(8,128)(4,1)} %iota_compare_fusion.8) | copy-start | bytes 511
  239.3 1.3 copy-start.8
  239.3 9.2 %copy-start.3 = (f32[128,115]{1,0:T(8,128)S(1)}, f32[128,115]{1,0:T(8,128)}, u32[]{:S(2)}) copy-start(f32[128,115]{1,0:T(8,128)} %pad_convert_fusion) | copy-start | bytes 176644
where the time goes:
time: 338 us; the launch traced here: 333 us
  other arithmetic  236 us (70%)
  blocking collectives  39 us (12%)
  local copies, waits for them, and re-layouts  21.6 us (6%)
  matrix products  19.6 us (6%)
  starting transfers between devices  9.79 us (3%)
  between operations  4.41 us (1%)
    another operation x18, other arithmetic, solve_one(): factor = jnp.linalg.cholesky(gram)  134 us
    another operation x8, other arithmetic, solve_one(): jax.scipy.linalg.solve_triangular(factor, middle, lower=True, trans=1)  83 us
    psum x4, blocking collectives, one_axis_at_a_time(): x = lax.psum(x, axis)  39 us
    concatenate x1, local copies, waits for them, and re-layouts, build_features(): return jnp.concatenate(pieces, axis=1)  8.01 us
    another operation x9, local copies, waits for them, and re-layouts  7.89 us
    dot_general x1, other arithmetic, body(): jnp.einsum('svpk,svpk->svp', values, values, preferred_element_type=jnp.f...  7.47 us
  transfers between devices with their start and end apart: 4, of which 1 were waited for; matrix products, arithmetic and copies ran while one was open for 3% of the time, Pallas kernels for 0%

commit v1 on v0

v1 whole, which is shorter than its diff:
```python
import jax
import jax.numpy as jnp
from jax import lax
from jax.experimental import pallas as pl
from jax.experimental.pallas import tpu as pltpu
from jax.sharding import Mesh
from jax.sharding import PartitionSpec as P

GX = ("gx_0", "gx_1")
GY = ("gy_0", "gy_1")
GX_GY = ("gx_0", "gx_1", "gy_0", "gy_1")

R = 24
NVAR = 4
K = 512
SLOTS = 2048
COLS = 2
NB = 3
NF = 397
HALF = 0.5
F32 = jnp.float32
HI = lax.Precision.HIGHEST


def iotas(shape):
    return lax.broadcasted_iota(jnp.int32, shape, 0), lax.broadcasted_iota(jnp.int32, shape, 1)


def local_kernel(counts, basis, snaps, proj, stats, acc):
    s = pl.program_id(0)
    v = pl.program_id(1)
    count = counts[s]

    @pl.when((s == 0) & (v == 0))
    def _():
        acc[...] = jnp.zeros_like(acc)

    lane = lax.broadcasted_iota(jnp.int32, (R, SLOTS), 1)
    modes = jnp.where(lane < count, basis[0, 0], jnp.zeros((), jnp.bfloat16))
    proj[s, v] = jnp.dot(modes, snaps[0, 0], preferred_element_type=F32)

    step = 64

    def tile_sum(x):
        x = x * x
        return jnp.sum(x.reshape(step // 8, 8, K), axis=0)

    def full(i, part):
        return part + tile_sum(snaps[0, 0, pl.ds(i * step, step), :].astype(F32))

    whole = count // step
    part = lax.fori_loop(0, whole, full, jnp.zeros((8, K), F32))
    edge = jnp.minimum(whole, SLOTS // step - 1)
    row = lax.broadcasted_iota(jnp.int32, (step, K), 0) + edge * step
    keep = (row < count) & (row >= whole * step)
    last = snaps[0, 0, pl.ds(pl.multiple_of(edge * step, step), step), :].astype(F32)
    part = part + tile_sum(jnp.where(keep, last, 0.0))
    part = part[:, 0:128] + part[:, 128:256] + part[:, 256:384] + part[:, 384:512]
    acc[v] += part

    @pl.when(v == NVAR - 1)
    def _():
        q = NVAR
        for a in range(NVAR):
            pa = proj[s, a]
            for b in range(a, NVAR):
                prod = pa * proj[s, b]
                t = prod[:, 0:128] + prod[:, 128:256] + prod[:, 256:384] + prod[:, 384:512]
                acc[q] += t[0:8] + t[8:16] + t[16:24]
                q += 1

    @pl.when((s == COLS - 1) & (v == NVAR - 1))
    def _():
        rows = jnp.sum(acc[...], axis=1)
        total = jnp.sum(rows, axis=1, keepdims=True)
        i, j = iotas((16, 128))
        flat = jnp.sum(jnp.where(i == j, total, 0.0), axis=0, keepdims=True)
        nodes = (counts[0] + counts[1]).astype(F32)
        _, lane1 = iotas((1, 128))
        stats[...] = jnp.where(lane1 == 14, nodes, flat)


def local_pass(snapshots, basis, counts):
    return pl.pallas_call(
        local_kernel,
        grid_spec=pltpu.PrefetchScalarGridSpec(
            num_scalar_prefetch=1,
            grid=(COLS, NVAR),
            in_specs=[
                pl.BlockSpec((1, 1, R, SLOTS), lambda s, v, c: (s, v, 0, 0)),
                pl.BlockSpec((1, 1, SLOTS, K), lambda s, v, c: (s, v, 0, 0)),
            ],
            out_specs=[
                pl.BlockSpec((COLS, NVAR, R, K), lambda s, v, c: (0, 0, 0, 0)),
                pl.BlockSpec((1, 128), lambda s, v, c: (0, 0)),
            ],
            scratch_shapes=[pltpu.VMEM((16, 8, 128), F32)],
        ),
        out_shape=[
            jax.ShapeDtypeStruct((COLS, NVAR, R, K), F32),
            jax.ShapeDtypeStruct((1, 128), F32),
        ],
        compiler_params=pltpu.CompilerParams(dimension_semantics=("arbitrary", "arbitrary")),
        name="local",
    )(counts, basis, snapshots)


def states_kernel(everyone, proj, states, gnorm):
    total = jnp.sum(everyone[...], axis=0, keepdims=True)
    nodes = total[:, 14:15]
    inv = []
    for v in range(NVAR):
        scale = jnp.sqrt(total[:, v : v + 1] / (nodes * K) + 1e-06)
        inv.append(1.0 / scale)
    g = jnp.zeros((1, 1), F32)
    q = NVAR
    for a in range(NVAR):
        for b in range(a, NVAR):
            term = total[:, q : q + 1] * inv[a] * inv[b]
            g = g + (term if a == b else 2.0 * term)
            q += 1
    gnorm[...] = jnp.broadcast_to(g * (1.0 / (256 * R * K)), (1, 128))
    for s in range(COLS):
        t = proj[s, 0] * inv[0]
        for v in range(1, NVAR):
            t = t + proj[s, v] * inv[v]
        states[s] = t


def global_states(everyone, proj):
    return pl.pallas_call(
        states_kernel,
        out_shape=[
            jax.ShapeDtypeStruct((COLS, R, K), F32),
            jax.ShapeDtypeStruct((1, 128), F32),
        ],
        name="states",
    )(everyone, proj)


LAST = 16
PADDED = 400
NQ = 288
FUT = 384
TAIL = FUT + R
WIDTH = 512


def place(row):
    return row if row < FUT else row + R


def invert_rows(block, tiles, first):
    sub, lane = iotas((8, 128))
    for p in range(tiles):
        base = first + 8 * p
        inside = (lane >= base) & (lane < base + 8)
        unit = jnp.where(lane - base == sub, 1.0, 0.0)
        for m in range(COLS):
            tile = block[m, 8 * p : 8 * p + 8, :]
            col = [jnp.broadcast_to(tile[:, base + k : base + k + 1], (8, 128)) for k in range(8)]
            x = jnp.where(inside, unit, tile)
            recips = jnp.zeros((8, 128), F32)
            for j in range(8):
                r = 1.0 / jnp.broadcast_to(col[j][j : j + 1, :], (8, 128))
                mult = jnp.where(sub == j, 0.0, col[j] * r)
                recips = jnp.where(sub == j, r, recips)
                for k in range(j + 1, 8):
                    col[k] = col[k] - mult * jnp.broadcast_to(col[k][j : j + 1, :], (8, 128))
                x = x - mult * jnp.broadcast_to(x[j : j + 1, :], (8, 128))
            w = x * recips
            block[m, 8 * p : 8 * p + 8, :] = w
            wb = [jnp.broadcast_to(w[j : j + 1, :], (8, 128)) for j in range(8)]
            for t in [t % tiles for t in range(p + 1, p + tiles)]:
                a = block[m, 8 * t : 8 * t + 8, :]
                terms = [jnp.broadcast_to(a[:, base + j : base + j + 1], (8, 128)) * wb[j] for j in range(8)]
                while len(terms) > 1:
                    terms = [terms[i] + terms[i + 1] for i in range(0, len(terms), 2)]
                block[m, 8 * t : 8 * t + 8, :] = jnp.where(inside, 0.0, a) - terms[0]


def mm(a, b):
    return lax.dot_general(a, b, (((1,), (0,)), ((), ())), precision=HI, preferred_element_type=F32)


def fit_kernel(links, gnorm, own, up, down, left, right, out, near, twice, feats, h, block):
    near[0, 1] = up[0]
    near[0, 2] = up[1]
    near[1, 1] = own[0]
    near[1, 2] = own[1]
    near[2, 1] = down[0]
    near[2, 2] = down[1]
    for i in range(3):
        near[i, 0] = left[i]
        near[i, 3] = right[i]
    _, lane = iotas((8, K))
    keep = lane < K - 1
    keep24 = jnp.concatenate([keep] * 3, axis=0)
    for m in range(COLS):
        s = own[m]
        past = jnp.where(keep24, s, 0.0)
        twice[0:R] = past
        twice[R : 2 * R] = past
        for d in range(12):
            feats[m, R * d : R * d + R] = past * twice[d : d + R]
        feats[m, NQ : NQ + R] = past
        row, lane16 = iotas((16, K))
        one = jnp.where((row == 12) & (lane16 < K - 1), 1.0, 0.0)
        feats[m, 312:328] = jnp.where(row < 12, twice[0:16] * twice[12:28], one)
        for b in range(NB):
            block_id = links[m * NB + b]
            v = jnp.where(keep24, near[block_id // 4, block_id % 4], 0.0)
            if b < 2:
                feats[m, 328 + R * b : 328 + R * b + R] = v
            else:
                feats[m, 376:384] = v[0:8]
                feats[m, TAIL : TAIL + 16] = v[8:24]
        feats[m, FUT:TAIL] = pltpu.roll(s, K - 1, 1)
    g = gnorm[...]
    lin = K * (HALF * g)
    quad = K * (HALF * g * g)
    sub, lane = iotas((8, 128))
    for m in range(COLS):
        rhs = feats[m]
        for lo, size, dst in ((0, 384, 0), (TAIL, LAST, FUT)):
            prod = lax.dot_general(
                feats[m, lo : lo + size], rhs, (((1,), (1,)), ((), ())), precision=HI, preferred_element_type=F32
            )
            h[m, dst : dst + size, 0:424] = prod
            h[m, dst : dst + size, 424:512] = jnp.zeros((size, 88), F32)
        for t in range(PADDED // 8):
            row = 8 * t
            if row < NQ:
                reg = quad
            elif row == 312:
                reg = quad
            elif row == 320:
                reg = jnp.where(sub < 4, quad, jnp.where(sub == 4, lin, 1.0))
            else:
                reg = lin
            where = place(row)
            cb = where // 128 * 128
            cell = h[m, row : row + 8, cb : cb + 128]
            h[m, row : row + 8, cb : cb + 128] = cell + jnp.where(lane == sub + (where - cb), reg, 0.0)
        block[m] = h[m, 0:128, 0:128]

    def step(p, carry):
        invert_rows(block, 16, 0)
        for k in range(3):

            @pl.when(p == k)
            def _():
                lo = 128 * k
                hi = lo + 128
                for m in range(COLS):
                    w = mm(block[m], h[m, lo:hi, hi:WIDTH])
                    for a, b in ((0, lo), (hi, PADDED)):
                        if a < b:
                            h[m, a:b, hi:WIDTH] = h[m, a:b, hi:WIDTH] - mm(h[m, a:b, lo:hi], w)
                    h[m, lo:hi, hi:WIDTH] = w
                    if k < 2:
                        block[m] = h[m, hi : hi + 128, hi : hi + 128]
                    else:
                        block[m, 0:LAST] = h[m, FUT:PADDED, FUT:WIDTH]

        return carry

    lax.fori_loop(0, 3, step, 0)
    invert_rows(block, 2, R)
    for m in range(COLS):
        x = block[m, 0:LAST]
        top = h[m, 0:FUT, FUT:WIDTH]
        h[m, 0:FUT, FUT:WIDTH] = top - mm(top[:, R : R + LAST], x)
        h[m, FUT:PADDED, FUT:WIDTH] = x
        out[m, 0:1] = h[m, 324:325, FUT : FUT + R]
        out[m, 1:25] = h[m, NQ : NQ + R, FUT : FUT + R]
        out[m, 25:97] = h[m, 328:400, FUT : FUT + R]
        dst = 97
        for a in range(R):
            for b in range(a, R):
                d = b - a
                if d == 12:
                    src = 312 + a
                elif d < 12:
                    src = R * d + a
                else:
                    src = R * (R - d) + b
                out[m, dst : dst + 1] = h[m, src : src + 1, FUT : FUT + R]
                dst += 1


def fit(links, gnorm, own, up, down, left, right):
    vm = pl.BlockSpec(memory_space=pltpu.VMEM)
    return pl.pallas_call(
        fit_kernel,
        in_specs=[pl.BlockSpec(memory_space=pltpu.SMEM)] + [vm] * 6,
        out_specs=vm,
        out_shape=jax.ShapeDtypeStruct((COLS, NF, R), F32),
        scratch_shapes=[
            pltpu.VMEM((3, 4, R, K), F32),
            pltpu.VMEM((2 * R, K), F32),
            pltpu.VMEM((COLS, 424, K), F32),
            pltpu.VMEM((COLS, PADDED, WIDTH), F32),
            pltpu.VMEM((COLS, 128, 128), F32),
        ],
        name="fit",
    )(links, gnorm, own, up, down, left, right)


def shifts(axis, x, y):
    n = lax.axis_size(axis)
    return (
        lax.ppermute(x, axis, [(i, i + 1) for i in range(n - 1)]),
        lax.ppermute(y, axis, [(i + 1, i) for i in range(n - 1)]),
    )


def body(snapshots, basis, node_counts, adjacency):
    counts = node_counts[0]
    links = adjacency[0]
    proj, stats = local_pass(snapshots[0], basis[0], counts)
    near_row = links // 16
    near_col = links % 16
    local = (near_row - lax.axis_index(GX) + 1) * 4 + (near_col - lax.axis_index(GY) * COLS + 1)
    everyone = lax.all_to_all(jnp.broadcast_to(stats[None], (128, 1, 128)), GX_GY, 0, 0)
    states, gnorm = global_states(everyone.reshape(128, 128), proj)
    up, down = shifts(GX, states, states)
    right_edge = jnp.stack([up[1], states[1], down[1]])
    left_edge = jnp.stack([up[0], states[0], down[0]])
    left, right = shifts(GY, right_edge, left_edge)
    operator = fit(local.reshape(-1), gnorm, states, up, down, left, right)
    return (operator[None], states[None])


def solution(mesh):
    split = Mesh(mesh.devices.reshape(4, 4, 4, 2), ("gx_0", "gx_1", "gy_0", "gy_1"))
    placed = (P(GX, GY, None, None, None), P(GX, GY, None, None, None), P(GX, GY), P(GX, GY, None))
    return jax.shard_map(
        body,
        mesh=split,
        in_specs=placed,
        out_specs=(P(GX, GY, None, None), P(GX, GY, None, None)),
        check_vma=False,
    )
```

time: 338 us -> 96.3 us (0.28)
  the two profiles are of different devices: /device:TPU:1 before, /device:TPU:9 now
where the time goes in v1:
time: 96.3 us; the launch traced here: 95.7 us
  Pallas kernels  48.6 us (50%)
  starting transfers between devices  22.3 us (23%)
  waiting for transfers between devices  18 us (19%)
  local copies, waits for them, and re-layouts  5.38 us (6%)
    pallas_call x1, Pallas kernels, fit(): pl.pallas_call(fit_kernel, in_specs=[pl.BlockSpec(memory_space=pltpu.SMEM...  34 us
    pallas_call x1, Pallas kernels, local_pass(): pl.pallas_call(local_kernel, grid_spec=pltpu.PrefetchScalarGridSpec(num_s...  12.6 us
    all_to_all x1, starting transfers between devices, body(): lax.all_to_all(jnp.broadcast_to(stats[None], (128, 1, 128)), GX_GY, 0, 0)  10.8 us
    all_to_all x1, waiting for transfers between devices, body(): lax.all_to_all(jnp.broadcast_to(stats[None], (128, 1, 128)), GX_GY, 0, 0)  8.34 us
    ppermute x2, starting transfers between devices, shifts(): lax.ppermute(x, axis, [(i, i + 1) for i in range(n - 1)])  6.04 us
    ppermute x2, waiting for transfers between devices, shifts(): lax.ppermute(x, axis, [(i, i + 1) for i in range(n - 1)])  5.72 us
    ppermute x2, starting transfers between devices, shifts(): lax.ppermute(y, axis, [(i + 1, i) for i in range(n - 1)])  5.44 us
    ppermute x2, waiting for transfers between devices, shifts(): lax.ppermute(y, axis, [(i + 1, i) for i in range(n - 1)])  3.94 us
  transfers between devices with their start and end apart: 5, of which 3 were waited for; matrix products, arithmetic and copies ran while one was open for 2% of the time, Pallas kernels for 0%

profile of v1, /device:TPU:9, one launch (start us, length us, event | category | flops | bytes accessed | tf_op | source)
XLA Modules:
  0.0 95.7 jit_solution(12896654370852590431)
XLA Ops:
  0.6 0.0 copy-start.5
  0.6 12.6 %local.1 = (f32[2,4,24,512]{3,2,1,0:T(8,128)}, f32[1,128]{1,0:T(1,128)}) custom-call(s32[2]{0:T(128)} %bitcast.12, bf16[2,4,24,2048]{3,2,1,0:T(8,128)(2,1)} %bitcast.9, bf16[2,4,2048,512]{3,2,1,0:T(8,128)(2,1)} %bitcast.7), custom_call_target="tpu_custom_call" | custom-call | tf_op jit(solution)/shard_map/local/pallas_call | solution.py:84
  13.3 1.3 %broadcast_in_dim.15 = f32[128,1,128]{2,1,0:T(1,128)} broadcast(f32[128]{0:T(128)} %bitcast.13), dimensions={2} | broadcast | bytes 66048 | tf_op jit(solution)/shard_map/broadcast_in_dim | solution.py:325
  14.6 10.8 %all-to-all-start = ((f32[128,1,128]{2,1,0:T(1,128)}), f32[128,1,128]{2,1,0:T(1,128)S(1)}, u32[]{:S(2)}, u32[]{:S(2)}) async-start(f32[128,1,128]{2,1,0:T(1,128)} %broadcast_in_dim.15), calls=%async_computation | async-start | bytes 131072 | tf_op jit(solution)/shard_map/all_to_all | solution.py:325
  25.5 0.0 copy-done.5
  25.5 0.1 squeeze.12
  25.5 8.3 %all-to-all-done = f32[128,1,128]{2,1,0:T(1,128)S(1)} async-done(((f32[128,1,128]{2,1,0:T(1,128)}), f32[128,1,128]{2,1,0:T(1,128)S(1)}, u32[]{:S(2)}, u32[]{:S(2)}) %all-to-all-start) | async-done | bytes 65568 | tf_op jit(solution)/shard_map/all_to_all | solution.py:325
  33.9 0.0 copy-start.2
  33.9 0.6 copy-done.2
  34.5 2.0 %states.1 = (f32[2,24,512]{2,1,0:T(8,128)}, f32[1,128]{1,0:T(1,128)}) custom-call(f32[128,128]{1,0:T(8,128)} %bitcast.11, f32[2,4,24,512]{3,2,1,0:T(8,128)} %get-tuple-element.7.proj), custom_call_target="tpu_custom_call" | custom-call | tf_op jit(solution)/shard_map/states/pallas_call | solution.py:131
  36.5 3.5 %collective-permute-start.1 = (f32[2,24,512]{2,1,0:T(8,128)}, f32[2,24,512]{2,1,0:T(8,128)S(1)}, u32[]{:S(2)}, u32[]{:S(2)}) collective-permute-start(f32[2,24,512]{2,1,0:T(8,128)} %get-tuple-element.9.own), channel_id=1, source_target_pairs={{8,0},{16,8},{24,16},{32,24},{40,32},{48,40},{56,48},{64,56},{72,6... | collective-permute-start | bytes 294920 | tf_op jit(solution)/shard_map/ppermute | solution.py:314
  40.0 0.9 fusion.4
  40.9 1.9 %collective-permute-start = (f32[2,24,512]{2,1,0:T(8,128)}, f32[2,24,512]{2,1,0:T(8,128)S(1)}, u32[]{:S(2)}, u32[]{:S(2)}) collective-permute-start(f32[2,24,512]{2,1,0:T(8,128)} %get-tuple-element.9.own), channel_id=1, source_target_pairs={{0,8},{8,16},{16,24},{24,32},{32,40},{40,48},{48,56},{56,64},{64,7... | collective-permute-start | bytes 294920 | tf_op jit(solution)/shard_map/ppermute | solution.py:313
  42.8 0.0 collective-permute-done.1.down
  42.8 0.0 copy-start
  42.9 5.7 %collective-permute-done.up = f32[2,24,512]{2,1,0:T(8,128)S(1)} collective-permute-done((f32[2,24,512]{2,1,0:T(8,128)}, f32[2,24,512]{2,1,0:T(8,128)S(1)}, u32[]{:S(2)}, u32[]{:S(2)}) %collective-permute-start) | collective-permute-done | bytes 98336 | tf_op jit(solution)/shard_map/ppermute | solution.py:313
  48.6 0.0 copy-start.1
  48.6 4.1 %collective-permute-start.2 = (f32[3,24,512]{2,1,0:T(8,128)S(1)}, f32[3,24,512]{2,1,0:T(8,128)S(1)}, u32[]{:S(2)}, u32[]{:S(2)}) collective-permute-start(f32[3,24,512]{2,1,0:T(8,128)S(1)} %pad_maximum_fusion), channel_id=1, source_target_pairs={{0,1},{1,2},{2,3},{3,4},{4,5},{5,6},{6,7},{8,9},{9,10},{10,11},{11... | collective-permute-start | bytes 442376 | tf_op jit(solution)/shard_map/ppermute | solution.py:313
  52.8 1.9 %collective-permute-start.3 = (f32[3,24,512]{2,1,0:T(8,128)S(1)}, f32[3,24,512]{2,1,0:T(8,128)S(1)}, u32[]{:S(2)}, u32[]{:S(2)}) collective-permute-start(f32[3,24,512]{2,1,0:T(8,128)S(1)} %pad_maximum_fusion.1), channel_id=1, source_target_pairs={{1,0},{2,1},{3,2},{4,3},{5,4},{6,5},{7,6},{9,8},{10,9},{11,10},{12... | collective-permute-start | bytes 442376 | tf_op jit(solution)/shard_map/ppermute | solution.py:314
  54.7 0.6 fusion.2.links
  55.3 0.0 collective-permute-done.2.left
  55.3 0.0 copy-start.3
  55.3 3.9 %collective-permute-done.3.right = f32[3,24,512]{2,1,0:T(8,128)S(1)} collective-permute-done((f32[3,24,512]{2,1,0:T(8,128)S(1)}, f32[3,24,512]{2,1,0:T(8,128)S(1)}, u32[]{:S(2)}, u32[]{:S(2)}) %collective-permute-start.3) | collective-permute-done | bytes 147488 | tf_op jit(solution)/shard_map/ppermute | solution.py:314
  59.2 0.0 copy-start.4
  59.2 0.0 copy-done
  59.2 0.0 copy-done.1
  59.2 0.0 copy-done.3
  59.2 0.7 copy-done.4
  59.9 34.0 %fit.1 = f32[2,397,24]{2,1,0:T(8,128)} custom-call(s32[6]{0:T(128)} %fusion.2.links, f32[1,128]{1,0:T(1,128)} %get-tuple-element.8.gnorm, f32[2,24,512]{2,1,0:T(8,128)} %get-tuple-element.9.own, f32[2,24,512]{2,1,0:T(8,128)} %copy-done.1, f32[2,24,512]{2,1,0:T(8,128)} %copy-done, f32[3,24,512]{2,1,0:T(8,128)} %copy-done.3, f32[3,24,512]{2,1,0:T(8,128)} %copy-done.4), custom_call_target="tpu_custom_call" | custom-call | tf_op jit(solution)/shard_map/fit/pallas_call | solution.py:294
  93.9 1.8 %copy.7 = f32[1,2,397,24]{2,3,1,0:T(8,128)} copy(f32[1,2,397,24]{3,2,1,0:T(8,128)} %bitcast.8) | data formatting | bytes 152448
  (4 shorter events, 0.0 us)
Async XLA Ops:
  0.6 24.8 %copy-start.5 = (s32[1,2,3]{2,1,0:T(2,128)S(1)}, s32[1,2,3]{2,1,0:T(2,128)}, u32[]{:S(2)}) copy-start(s32[1,2,3]{2,1,0:T(2,128)} %param.7) | copy-start | bytes 76
  14.6 19.3 %all-to-all-start = ((f32[128,1,128]{2,1,0:T(1,128)}), f32[128,1,128]{2,1,0:T(1,128)S(1)}, u32[]{:S(2)}, u32[]{:S(2)}) async-start(f32[128,1,128]{2,1,0:T(1,128)} %broadcast_in_dim.15), calls=%async_computation | async-start | bytes 131072 | tf_op jit(solution)/shard_map/all_to_all | solution.py:325
  33.9 0.6 copy-start.2
  36.5 6.3 %collective-permute-start.1 = (f32[2,24,512]{2,1,0:T(8,128)}, f32[2,24,512]{2,1,0:T(8,128)S(1)}, u32[]{:S(2)}, u32[]{:S(2)}) collective-permute-start(f32[2,24,512]{2,1,0:T(8,128)} %get-tuple-element.9.own), channel_id=1, source_target_pairs={{8,0},{16,8},{24,16},{32,24},{40,32},{48,40},{56,48},{64,56},{72,6... | collective-permute-start | bytes 294920 | tf_op jit(solution)/shard_map/ppermute | solution.py:314
  40.9 7.7 %collective-permute-start = (f32[2,24,512]{2,1,0:T(8,128)}, f32[2,24,512]{2,1,0:T(8,128)S(1)}, u32[]{:S(2)}, u32[]{:S(2)}) collective-permute-start(f32[2,24,512]{2,1,0:T(8,128)} %get-tuple-element.9.own), channel_id=1, source_target_pairs={{0,8},{8,16},{16,24},{24,32},{32,40},{40,48},{48,56},{56,64},{64,7... | collective-permute-start | bytes 294920 | tf_op jit(solution)/shard_map/ppermute | solution.py:313
  42.8 16.4 %copy-start = (f32[2,24,512]{2,1,0:T(8,128)}, f32[2,24,512]{2,1,0:T(8,128)S(1)}, u32[]{:S(2)}) copy-start(f32[2,24,512]{2,1,0:T(8,128)S(1)} %collective-permute-done.1.down) | copy-start | bytes 294916
  48.6 10.7 %copy-start.1 = (f32[2,24,512]{2,1,0:T(8,128)}, f32[2,24,512]{2,1,0:T(8,128)S(1)}, u32[]{:S(2)}) copy-start(f32[2,24,512]{2,1,0:T(8,128)S(1)} %collective-permute-done.up) | copy-start | bytes 294916
  48.6 6.7 %collective-permute-start.2 = (f32[3,24,512]{2,1,0:T(8,128)S(1)}, f32[3,24,512]{2,1,0:T(8,128)S(1)}, u32[]{:S(2)}, u32[]{:S(2)}) collective-permute-start(f32[3,24,512]{2,1,0:T(8,128)S(1)} %pad_maximum_fusion), channel_id=1, source_target_pairs={{0,1},{1,2},{2,3},{3,4},{4,5},{5,6},{6,7},{8,9},{9,10},{10,11},{11... | collective-permute-start | bytes 442376 | tf_op jit(solution)/shard_map/ppermute | solution.py:313
  52.8 6.5 %collective-permute-start.3 = (f32[3,24,512]{2,1,0:T(8,128)S(1)}, f32[3,24,512]{2,1,0:T(8,128)S(1)}, u32[]{:S(2)}, u32[]{:S(2)}) collective-permute-start(f32[3,24,512]{2,1,0:T(8,128)S(1)} %pad_maximum_fusion.1), channel_id=1, source_target_pairs={{1,0},{2,1},{3,2},{4,3},{5,4},{6,5},{7,6},{9,8},{10,9},{11,10},{12... | collective-permute-start | bytes 442376 | tf_op jit(solution)/shard_map/ppermute | solution.py:314
  55.3 4.0 %copy-start.3 = (f32[3,24,512]{2,1,0:T(8,128)}, f32[3,24,512]{2,1,0:T(8,128)S(1)}, u32[]{:S(2)}) copy-start(f32[3,24,512]{2,1,0:T(8,128)S(1)} %collective-permute-done.2.left) | copy-start | bytes 442372
  59.2 0.7 copy-start.4

commit v2 on v1

v2 whole, which is shorter than its diff:
```python
import jax
import jax.numpy as jnp
from jax import lax
from jax.experimental import pallas as pl
from jax.experimental.pallas import tpu as pltpu
from jax.sharding import Mesh
from jax.sharding import PartitionSpec as P

GX = ("gx_0", "gx_1")
GY = ("gy_0", "gy_1")
GX_GY = ("gx_0", "gx_1", "gy_0", "gy_1")

R = 24
NVAR = 4
K = 512
SLOTS = 2048
COLS = 2
NB = 3
NF = 397
HALF = 0.5
F32 = jnp.float32
BF = jnp.bfloat16
HI = lax.Precision.HIGHEST


def iotas(shape):
    return lax.broadcasted_iota(jnp.int32, shape, 0), lax.broadcasted_iota(jnp.int32, shape, 1)


def fold_lanes(x):
    return (x[:, 0:128] + x[:, 128:256]) + (x[:, 256:384] + x[:, 384:512])


def local_kernel(counts, basis, snaps, proj0, proj1, stats, acc):
    s = pl.program_id(0)
    v = pl.program_id(1)
    count = counts[s]

    @pl.when((s == 0) & (v == 0))
    def _():
        acc[...] = jnp.zeros_like(acc)

    lane = lax.broadcasted_iota(jnp.int32, (R, SLOTS), 1)
    modes = jnp.where(lane < count, basis[0, 0], jnp.zeros((), BF))
    prod = jnp.dot(modes, snaps[0, 0], preferred_element_type=F32)
    step = 128
    row = lax.broadcasted_iota(jnp.int32, (step, 128), 0)
    part = jnp.zeros((8, 128), F32)
    for lo in range(0, SLOTS, step):
        x = snaps[0, 0, lo : lo + step, :].astype(F32)
        t = jnp.where(row < count - lo, fold_lanes(x * x), 0.0)
        part = part + jnp.sum(t.reshape(step // 8, 8, 128), axis=0)
    acc[v] += part

    @pl.when(s == 0)
    def _():
        proj0[v] = prod

    @pl.when(s == 1)
    def _():
        proj1[v] = prod

    for sub, proj in ((0, proj0), (1, proj1)):

        @pl.when((s == sub) & (v == NVAR - 1))
        def _():
            q = NVAR
            for a in range(NVAR):
                pa = proj[a]
                for b in range(a, NVAR):
                    t = fold_lanes(pa * proj[b])
                    acc[q] += t[0:8] + t[8:16] + t[16:24]
                    q += 1

    @pl.when((s == COLS - 1) & (v == NVAR - 1))
    def _():
        rows = jnp.sum(acc[...], axis=1)
        total = jnp.sum(rows, axis=1, keepdims=True)
        i, j = iotas((16, 128))
        flat = jnp.sum(jnp.where(i == j, total, 0.0), axis=0, keepdims=True)
        nodes = (counts[0] + counts[1]).astype(F32)
        _, lane1 = iotas((1, 128))
        stats[...] = jnp.broadcast_to(jnp.where(lane1 == 14, nodes, flat), (128, 128))


def local_pass(snapshots, basis, counts):
    return pl.pallas_call(
        local_kernel,
        grid_spec=pltpu.PrefetchScalarGridSpec(
            num_scalar_prefetch=1,
            grid=(COLS, NVAR),
            in_specs=[
                pl.BlockSpec((1, 1, R, SLOTS), lambda s, v, c: (s, v, 0, 0)),
                pl.BlockSpec((1, 1, SLOTS, K), lambda s, v, c: (s, v, 0, 0)),
            ],
            out_specs=[
                pl.BlockSpec((NVAR, R, K), lambda s, v, c: (0, 0, 0)),
                pl.BlockSpec((NVAR, R, K), lambda s, v, c: (0, 0, 0)),
                pl.BlockSpec((128, 128), lambda s, v, c: (0, 0)),
            ],
            scratch_shapes=[pltpu.VMEM((16, 8, 128), F32)],
        ),
        out_shape=[
            jax.ShapeDtypeStruct((NVAR, R, K), F32),
            jax.ShapeDtypeStruct((NVAR, R, K), F32),
            jax.ShapeDtypeStruct((128, 128), F32),
        ],
        compiler_params=pltpu.CompilerParams(dimension_semantics=("arbitrary", "arbitrary")),
        name="local",
    )(counts, basis, snapshots)


def states_kernel(everyone, left, proj0, proj1, right, own, patch, gnorm):
    total = jnp.sum(everyone[...], axis=0, keepdims=True)
    nodes = total[:, 14:15]
    inv = []
    for v in range(NVAR):
        scale = jnp.sqrt(total[:, v : v + 1] / (nodes * K) + 1e-06)
        inv.append(1.0 / scale)
    g = jnp.zeros((1, 1), F32)
    q = NVAR
    for a in range(NVAR):
        for b in range(a, NVAR):
            term = total[:, q : q + 1] * inv[a] * inv[b]
            g = g + (term if a == b else 2.0 * term)
            q += 1
    gnorm[...] = jnp.broadcast_to(g * (1.0 / (256 * R * K)), (1, 128))
    for c, proj in enumerate((left, proj0, proj1, right)):
        t = proj[0] * inv[0]
        for v in range(1, NVAR):
            t = t + proj[v] * inv[v]
        patch[c] = t
        if c in (1, 2):
            own[c - 1] = t


def global_states(everyone, left, proj0, proj1, right):
    return pl.pallas_call(
        states_kernel,
        out_shape=[
            jax.ShapeDtypeStruct((COLS, R, K), F32),
            jax.ShapeDtypeStruct((4, R, K), F32),
            jax.ShapeDtypeStruct((1, 128), F32),
        ],
        name="states",
    )(everyone, left, proj0, proj1, right)


OWN = 328
NQ = 288
MIXED = 312
FUT = OWN
NEAR = 72
LANES = 384


def lane_copy(x, at):
    return jnp.take_along_axis(x, jnp.full((8, 128), at, jnp.int32), axis=1)


def sub_copy(x, j):
    return jnp.broadcast_to(x[j : j + 1, :], (8, 128))


def split3(x):
    h = x.astype(BF)
    r = x - h.astype(F32)
    m = r.astype(BF)
    return h, m, (r - m.astype(F32)).astype(BF)


def dot(a, b):
    return jnp.dot(a, b, preferred_element_type=F32)


def mm(a, b):
    return jnp.dot(a, b, precision=HI, preferred_element_type=F32)


def tree(terms):
    while len(terms) > 1:
        terms = [terms[i] + terms[i + 1] for i in range(0, len(terms) - 1, 2)] + terms[len(terms) // 2 * 2 :]
    return terms[0]


def padded_dot(a, w, lo):
    ah, am, al = split3(a)
    n = w.shape[0]
    parts = [jnp.zeros((lo, 128), F32)] * (lo > 0) + [w] + [jnp.zeros((128 - lo - n, 128), F32)] * (lo + n < 128)
    wh, wm, wl = split3(jnp.concatenate(parts, axis=0) if len(parts) > 1 else w)
    pair = jnp.concatenate([wh, wm], axis=1)
    u = dot(jnp.concatenate([ah, am], axis=1), jnp.concatenate([pair, pair], axis=0))
    v = dot(jnp.concatenate([ah, al], axis=1), jnp.concatenate([wl, wh], axis=0))
    return u[:, :128] + (u[:, 128:] + v)


def invert(block, tiles, strip=4, look=2):
    sub, lane = iotas((8, 128))
    for s in range(0, tiles, strip):
        own = list(range(s, min(s + strip, tiles)))
        ahead = list(range(s + strip, min(s + strip + look, tiles)))
        for p in own:
            base = 8 * p
            inside = (lane >= base) & (lane < base + 8)
            unit = jnp.where(lane - base == sub, 1.0, 0.0)
            ws = []
            for m in range(COLS):
                tile = block[m, base : base + 8, :]
                col = [lane_copy(tile, base + k) for k in range(8)]
                x = jnp.where(inside, unit, tile)
                recips = jnp.zeros((8, 128), F32)
                for j in range(8):
                    r = 1.0 / sub_copy(col[j], j)
                    mult = jnp.where(sub == j, 0.0, col[j]) * r
                    recips = jnp.where(sub == j, r, recips)
                    for k in range(j + 1, 8):
                        col[k] = col[k] - mult * sub_copy(col[k], j)
                    x = x - mult * sub_copy(x, j)
                w = x * recips
                block[m, base : base + 8, :] = w
                ws.append([sub_copy(w, j) for j in range(8)])
            for t in [t for t in own + ahead if t > p] + [t for t in own if t < p]:
                for m in range(COLS):
                    a = block[m, 8 * t : 8 * t + 8, :]
                    delta = tree([lane_copy(a, base + j) * ws[m][j] for j in range(8)])
                    block[m, 8 * t : 8 * t + 8, :] = jnp.where(inside, 0.0, a) - delta
            yield
        lo, hi = 8 * s, 8 * (own[-1] + 1)
        ranges = [(a, b) for a, b in ((hi + 8 * len(ahead), 8 * tiles), (0, lo)) if a < b]
        if ranges:
            for m in range(COLS):
                rest = [block[m, a:b, :] for a, b in ranges]
                rest = jnp.concatenate(rest, axis=0) if len(rest) > 1 else rest[0]
                _, wide = iotas(rest.shape)
                kept = jnp.where((wide >= lo) & (wide < hi), 0.0, rest)
                new = kept - padded_dot(rest, block[m, lo:hi, :], lo)
                at = 0
                for a, b in ranges:
                    block[m, a:b, :] = new[at : at + b - a]
                    at += b - a


def spread(panels, count, work):
    work = list(work)
    done = 0
    for i, _ in enumerate(panels):
        want = (i + 1) * len(work) // count if i + 1 < count else len(work)
        while done < min(want, len(work)):
            work[done]()
            done += 1
    for f in work[done:]:
        f()


def own_features(feats, twice, m, state, keep):
    past = jnp.where(keep, state, 0.0)
    twice[m, 0:R] = past
    twice[m, R : 2 * R] = past
    for d in range(12):
        feats(R * d, past * twice[m, d : d + R])
    feats(NQ, past)
    row, lane = iotas((16, K))
    one = jnp.where((row == 12) & (lane < K - 1), 1.0, 0.0)
    feats(MIXED, jnp.where(row < 12, twice[m, 0:16] * twice[m, 12:28], one))
    feats(FUT, pltpu.roll(state, K - 1, 1))


def ridge(gnorm):
    g = gnorm[...]
    return K * (HALF * g), K * (HALF * g * g)


def past_mask():
    return lax.broadcasted_iota(jnp.int32, (R, K), 1) < K - 1


def nt(a, b):
    return lax.dot_general(a, b, (((1,), (1,)), ((), ())), preferred_element_type=F32)


def own_kernel(gnorm, own, out, twice, fh, fm, fl, h, block):
    keep = past_mask()
    for m in range(COLS):

        def put(at, x, m=m):
            a, b, c = split3(x)
            n = x.shape[0]
            fh[m, at : at + n], fm[m, at : at + n], fl[m, at : at + n] = a, b, c

        own_features(put, twice, m, own[m], keep)
    lin, quad = ridge(gnorm)
    sub, lane = iotas((8, 128))

    def gram(m, r0, r1, c0, c1):
        a = [f[m, r0:r1] for f in (fh, fm, fl)]
        b = [f[m, c0:c1] for f in (fh, fm, fl)]
        g = ((nt(a[1], b[1]) + nt(a[0], b[2])) + nt(a[2], b[0])) + (nt(a[0], b[1]) + nt(a[1], b[0]))
        return g + nt(a[0], b[0])

    def reg(row):
        if row < NQ or row == MIXED:
            return quad
        if row == MIXED + 8:
            return jnp.where(sub < 4, quad, jnp.where(sub == 4, lin, 1.0))
        return lin

    def ridged(x, row0):
        tiles = []
        for i in range(x.shape[0] // 8):
            tiles.append(x[8 * i : 8 * i + 8] + jnp.where(lane == sub + 8 * i, reg(row0 + 8 * i), 0.0))
        return jnp.concatenate(tiles, axis=0)

    for m in range(COLS):
        block[m] = ridged(gram(m, 0, 128, 0, 128), 0)

    def piece(m, kind):
        def go():
            if kind == 0:
                h[m, 0:128, 128:256] = gram(m, 0, 128, 128, 256)
            elif kind == 1:
                h[m, 128:OWN, 0:128] = gram(m, 128, OWN, 0, 128)
            elif kind == 2:
                h[m, 128:256, 128:256] = ridged(gram(m, 128, 256, 128, 256), 128)
            elif kind == 3:
                h[m, 256:OWN, 128:256] = gram(m, 256, OWN, 128, 256)
            else:
                h[m, :, 256:LANES] = jnp.zeros((OWN, 128), F32)
                h[m, 0:256, 256 : OWN + R] = gram(m, 0, 256, 256, OWN + R)
                h[m, 256:OWN, 256 : OWN + R] = gram(m, 256, OWN, 256, OWN + R)
                h[m, 256:OWN, 256:LANES] = ridged(h[m, 256:OWN, 256:LANES], 256)

        return go

    spread(invert(block, 16), 14, [piece(m, k) for k in range(5) for m in range(COLS)])
    inv0 = [block[m] for m in range(COLS)]
    for m in range(COLS):
        w = mm(inv0[m], h[m, 0:128, 128:256])
        block[m] = h[m, 128:256, 128:256] - mm(h[m, 128:256, 0:128], w)
        h[m, 0:128, 128:256] = w
        h[m, 0:128, 0:128] = inv0[m]

    def after0(m, kind):
        def go():
            if kind == 0:
                h[m, 0:128, 256:LANES] = mm(h[m, 0:128, 0:128], h[m, 0:128, 256:LANES])
            elif kind == 1:
                rows = slice(128, OWN)
                h[m, rows, 256:LANES] -= mm(h[m, rows, 0:128], h[m, 0:128, 256:LANES])
            elif kind == 2:
                rows = slice(256, OWN)
                h[m, rows, 128:256] -= mm(h[m, rows, 0:128], h[m, 0:128, 128:256])
            else:
                rows = slice(128, OWN)
                h[m, rows, 0:128] = -mm(h[m, rows, 0:128], h[m, 0:128, 0:128])

        return go

    spread(invert(block, 16), 14, [after0(m, k) for k in range(4) for m in range(COLS)])
    for m in range(COLS):
        h[m, 128:256, 128:256] = block[m]
        w = mm(block[m], h[m, 128:256, 256:LANES])
        block[m, 0:NEAR] = h[m, 256:OWN, 256:LANES] - mm(h[m, 256:OWN, 128:256], w)
        h[m, 128:256, 256:LANES] = w

    def after1(m, kind):
        def go():
            if kind == 0:
                h[m, 128:256, 0:128] = mm(h[m, 128:256, 128:256], h[m, 128:256, 0:128])
            elif kind == 1:
                h[m, 0:128, 256:LANES] -= mm(h[m, 0:128, 128:256], h[m, 128:256, 256:LANES])
            elif kind == 2:
                for rows in (slice(0, 128), slice(256, OWN)):
                    h[m, rows, 0:128] -= mm(h[m, rows, 128:256], h[m, 128:256, 0:128])
            else:
                for rows in (slice(0, 128), slice(256, OWN)):
                    h[m, rows, 128:256] = -mm(h[m, rows, 128:256], h[m, 128:256, 128:256])

        return go

    spread(invert(block, 9), 8, [after1(m, k) for k in range(4) for m in range(COLS)])
    _, wide = iotas((256, 128))
    for m in range(COLS):
        last = block[m, 0:NEAR]
        w = mm(last[:, 0:NEAR], h[m, 256:OWN, 0:256])
        part = h[m, 0:256, 256:LANES]
        out[m, 0:256, 0:256] = h[m, 0:256, 0:256] - mm(part[:, 0:NEAR], w)
        out[m, 0:256, 256:LANES] = jnp.where(wide < NEAR, 0.0, part) - mm(part[:, 0:NEAR], last)
        out[m, 256:OWN, 0:256] = w
        out[m, 256:OWN, 256:LANES] = last


def fit_own(gnorm, own):
    return pl.pallas_call(
        own_kernel,
        out_shape=jax.ShapeDtypeStruct((COLS, OWN, LANES), F32),
        scratch_shapes=[
            pltpu.VMEM((COLS, 2 * R, K), F32),
            pltpu.VMEM((COLS, OWN + R, K), BF),
            pltpu.VMEM((COLS, OWN + R, K), BF),
            pltpu.VMEM((COLS, OWN + R, K), BF),
            pltpu.VMEM((COLS, OWN, LANES), F32),
            pltpu.VMEM((COLS, 128, 128), F32),
        ],
        name="fit_own",
    )(gnorm, own)


def near_kernel(adjacency, gnorm, mid, up, down, solved, out, twice, fh, fm, fl, near, block, x, order):
    row0 = lax.axis_index("gx_0") * 4 + lax.axis_index("gx_1")
    col0 = (lax.axis_index("gy_0") * 2 + lax.axis_index("gy_1")) * COLS
    for c in range(4):
        near[c] = up[c]
        near[4 + c] = mid[c]
        near[8 + c] = down[c]
    keep = past_mask()
    lin, _ = ridge(gnorm)
    sub, lane = iotas((8, 128))
    for m in range(COLS):

        def put(at, v, m=m):
            n = v.shape[0]
            fh[m, at : at + n], fm[m, at : at + n], fl[m, at : at + n] = split3(v)

        own_features(put, twice, m, mid[1 + m], keep)
        rows = []
        for b in range(NB):
            link = adjacency[0, m, b]
            at = ((link >> 4) - row0 + 1) * 4 + ((link & 15) - col0 + 1)
            rows.append(jnp.where(keep, near[at], 0.0))
        nh, nm, nl = split3(jnp.concatenate(rows, axis=0))
        thirds = jnp.concatenate([nh, nm, nl], axis=0)
        p = nt(fh[m], thirds)
        q = nt(fm[m], thirds[0 : 2 * NEAR])
        g = (p[:, 2 * NEAR : 3 * NEAR] + q[:, NEAR : 2 * NEAR] + nt(fl[m], nh)) + (p[:, NEAR : 2 * NEAR] + q[:, 0:NEAR])
        cross = g + p[:, 0:NEAR]
        p = nt(nh, thirds)
        q = nt(nm, thirds[0 : 2 * NEAR])
        g = (p[:, 2 * NEAR : 3 * NEAR] + q[:, NEAR : 2 * NEAR] + nt(nl, nh)) + (p[:, NEAR : 2 * NEAR] + q[:, 0:NEAR])
        square = g + p[:, 0:NEAR]
        wide = jnp.concatenate([cross, jnp.zeros((LANES - OWN - R, NEAR), F32)], axis=0)
        wide = jnp.concatenate([wide, jnp.zeros((LANES, 128 - NEAR), F32)], axis=1)
        turned = wide.T[0:NEAR]
        z = mm(solved[m, :, 0:256], cross[0:256]) + mm(solved[m, :, 256:OWN], cross[256:OWN])
        tail = solved[m, :, 256:LANES]
        _, lane_o = iotas((OWN, 128))
        z = jnp.concatenate([z, jnp.zeros((OWN, 128 - NEAR), F32)], axis=1)
        both = jnp.where(lane_o < NEAR, z, tail)
        x[m, 0:OWN] = both
        _, lane_n = iotas((NEAR, 128))
        square = jnp.concatenate([square, jnp.zeros((NEAR, 128 - NEAR), F32)], axis=1)
        start = jnp.where(lane_n < NEAR, square, turned[:, 256:LANES])
        start = jnp.where(lane_n < NEAR + R, start, 0.0)
        for i in range(NEAR // 8):
            rows8 = slice(8 * i, 8 * i + 8)
            block[m, rows8] = start[rows8] + jnp.where(lane == sub + 8 * i, lin, 0.0)
        block[m, 0:NEAR] = block[m, 0:NEAR] - mm(turned[:, 0:OWN], both)
    for _ in invert(block, 9):
        pass
    for m in range(COLS):
        last = block[m, 0:NEAR]
        both = x[m, 0:OWN]
        x[m, 0:OWN] = both - mm(both[:, 0:NEAR], last)
        x[m, OWN : OWN + NEAR] = last
        order[m, 0:1] = x[m, MIXED + 12 : MIXED + 13]
        order[m, 1:25] = x[m, NQ : NQ + R]
        order[m, 25:97] = last
        dst = 97
        for a in range(R):
            for b in range(a, R):
                d = b - a
                if d == 12:
                    src = MIXED + a
                elif d < 12:
                    src = R * d + a
                else:
                    src = R * (R - d) + b
                order[m, dst : dst + 1] = x[m, src : src + 1]
                dst += 1
        flat = order[m].T
        out[m] = flat[NEAR : NEAR + R, 0:NF]


def fit_near(adjacency, gnorm, mid, up, down, solved):
    vm = pl.BlockSpec(memory_space=pltpu.VMEM)
    return pl.pallas_call(
        near_kernel,
        in_specs=[pl.BlockSpec(memory_space=pltpu.SMEM)] + [vm] * 5,
        out_specs=vm,
        out_shape=jax.ShapeDtypeStruct((COLS, R, NF), F32),
        scratch_shapes=[
            pltpu.VMEM((COLS, 2 * R, K), F32),
            pltpu.VMEM((COLS, OWN + R, K), BF),
            pltpu.VMEM((COLS, OWN + R, K), BF),
            pltpu.VMEM((COLS, OWN + R, K), BF),
            pltpu.VMEM((12, R, K), F32),
            pltpu.VMEM((COLS, 128, 128), F32),
            pltpu.VMEM((COLS, OWN + NEAR, 128), F32),
            pltpu.VMEM((COLS, 512, 128), F32),
        ],
        name="fit_near",
    )(adjacency, gnorm, mid, up, down, solved)


def shifts(axis, x, y):
    n = lax.axis_size(axis)
    return (
        lax.ppermute(x, axis, [(i, i + 1) for i in range(n - 1)]),
        lax.ppermute(y, axis, [(i + 1, i) for i in range(n - 1)]),
    )


def body(snapshots, basis, node_counts, adjacency):
    proj0, proj1, stats = local_pass(snapshots[0], basis[0], node_counts[0])
    everyone = lax.all_to_all(stats, GX_GY, 0, 0, tiled=True)
    left, right = shifts(GY, proj1, proj0)
    own, mid, gnorm = global_states(everyone, left, proj0, proj1, right)
    up, down = shifts(GX, mid, mid)
    solved = fit_own(gnorm, own)
    operator = fit_near(adjacency, gnorm, mid, up, down, solved)
    return (jnp.swapaxes(operator, 1, 2)[None], own[None])


def solution(mesh):
    split = Mesh(mesh.devices.reshape(4, 4, 4, 2), ("gx_0", "gx_1", "gy_0", "gy_1"))
    placed = (P(GX, GY, None, None, None), P(GX, GY, None, None, None), P(GX, GY), P(GX, GY, None))
    return jax.shard_map(
        body,
        mesh=split,
        in_specs=placed,
        out_specs=(P(GX, GY, None, None), P(GX, GY, None, None)),
        check_vma=False,
    )
```

time: 96.3 us -> 77.7 us (0.81)
  the two profiles are of different devices: /device:TPU:9 before, /device:TPU:1 now
where the time goes in v2:
time: 77.7 us; the launch traced here: 76.9 us
  Pallas kernels  42.2 us (54%)
  blocking collectives  20.3 us (26%)
  starting transfers between devices  11.7 us (15%)
  local copies, waits for them, and re-layouts  2.08 us (3%)
    all_to_all x1, blocking collectives, body(): everyone = lax.all_to_all(stats, GX_GY, 0, 0, tiled=True)  20.3 us
    pallas_call x1, Pallas kernels, fit_own(): pl.pallas_call(own_kernel, out_shape=jax.ShapeDtypeStruct((COLS, OWN, LAN...  16.7 us
    pallas_call x1, Pallas kernels, local_pass(): pl.pallas_call(local_kernel, grid_spec=pltpu.PrefetchScalarGridSpec(num_s...  13.2 us
    pallas_call x1, Pallas kernels, fit_near(): pl.pallas_call(near_kernel, in_specs=[pl.BlockSpec(memory_space=pltpu.SME...  10 us
    ppermute x2, starting transfers between devices, shifts(): lax.ppermute(x, axis, [(i, i + 1) for i in range(n - 1)])  8.48 us
    ppermute x2, starting transfers between devices, shifts(): lax.ppermute(y, axis, [(i + 1, i) for i in range(n - 1)])  3.2 us
    pallas_call x1, Pallas kernels, global_states(): pl.pallas_call(states_kernel, out_shape=[jax.ShapeDtypeStruct((COLS, R, K...  2.29 us
    unnamed x8, local copies, waits for them, and re-layouts  2.08 us
  transfers between devices with their start and end apart: 4, of which 0 were waited for; matrix products, arithmetic and copies ran while one was open for 0% of the time, Pallas kernels for 22%

profile of v2, /device:TPU:1, one launch (start us, length us, event | category | flops | bytes accessed | tf_op | source)
XLA Modules:
  0.0 76.9 jit_solution(16592954927436406566)
XLA Ops:
  0.6 13.2 %local.1 = (f32[4,24,512]{2,1,0:T(8,128)}, f32[4,24,512]{2,1,0:T(8,128)}, f32[128,128]{1,0:T(8,128)}) custom-call(s32[2]{0:T(128)} %bitcast.17, bf16[2,4,24,2048]{3,2,1,0:T(8,128)(2,1)} %bitcast.12, bf16[2,4,2048,512]{3,2,1,0:T(8,128)(2,1)} %bitcast.11), custom_call_target="tpu_custom_call" | custom-call | tf_op jit(solution)/shard_map/local/pallas_call | solution.py:87
  13.8 4.5 %collective-permute-start = (f32[4,24,512]{2,1,0:T(8,128)}, f32[4,24,512]{2,1,0:T(8,128)S(1)}, u32[]{:S(2)}, u32[]{:S(2)}) collective-permute-start(f32[4,24,512]{2,1,0:T(8,128)} %get-tuple-element.9.proj1), channel_id=1, source_target_pairs={{0,1},{1,2},{2,3},{3,4},{4,5},{5,6},{6,7},{8,9},{9,10},{10,11},{11... | collective-permute-start | bytes 589832 | tf_op jit(solution)/shard_map/ppermute | solution.py:507
  18.3 1.9 %collective-permute-start.1 = (f32[4,24,512]{2,1,0:T(8,128)}, f32[4,24,512]{2,1,0:T(8,128)S(1)}, u32[]{:S(2)}, u32[]{:S(2)}) collective-permute-start(f32[4,24,512]{2,1,0:T(8,128)} %get-tuple-element.10.proj0), channel_id=1, source_target_pairs={{1,0},{2,1},{3,2},{4,3},{5,4},{6,5},{7,6},{9,8},{10,9},{11,10},{12... | collective-permute-start | bytes 589832 | tf_op jit(solution)/shard_map/ppermute | solution.py:508
  20.2 20.3 %all_to_all.11 = f32[128,1,128]{2,1,0:T(1,128)} all-to-all(f32[128,1,128]{2,1,0:T(1,128)} %bitcast.16), channel_id=1, replica_groups=mesh['gx_0'=4,'gx_1'=4,'gy_0'=4,'gy_1'=2] {'gx_0','gx_1','gy_0','gy_1'}, dimensions={0} | all-to-all | bytes 131072 | tf_op jit(solution)/shard_map/all_to_all | solution.py:514
  40.5 0.0 collective-permute-done.left
  40.5 0.0 copy-start
  40.5 0.0 collective-permute-done.1.right
  40.5 0.0 copy-start.1
  40.5 0.7 copy-done
  41.2 0.1 copy-done.1
  41.3 2.3 %states.1 = (f32[2,24,512]{2,1,0:T(8,128)}, f32[4,24,512]{2,1,0:T(8,128)}, f32[1,128]{1,0:T(1,128)}) custom-call(f32[128,128]{1,0:T(8,128)} %bitcast.13, f32[4,24,512]{2,1,0:T(8,128)} %copy-done, f32[4,24,512]{2,1,0:T(8,128)} %get-tuple-element.10.proj0, f32[4,24,512]{2,1,0:T(8,128)} %get-tuple-element.9.proj1, f32[4,24,512]{2,1,0:T(8,128)} %copy-done.1), custom_call_target="tpu_custom_call" | custom-call | tf_op jit(solution)/shard_map/states/pallas_call | solution.py:138
  43.6 1.3 %collective-permute-start.3 = (f32[4,24,512]{2,1,0:T(8,128)}, f32[4,24,512]{2,1,0:T(8,128)S(1)}, u32[]{:S(2)}, u32[]{:S(2)}) collective-permute-start(f32[4,24,512]{2,1,0:T(8,128)} %get-tuple-element.12.mid), channel_id=1, source_target_pairs={{8,0},{16,8},{24,16},{32,24},{40,32},{48,40},{56,48},{64,56},{72,6... | collective-permute-start | bytes 589832 | tf_op jit(solution)/shard_map/ppermute | solution.py:508
  44.8 4.0 %collective-permute-start.2 = (f32[4,24,512]{2,1,0:T(8,128)}, f32[4,24,512]{2,1,0:T(8,128)S(1)}, u32[]{:S(2)}, u32[]{:S(2)}) collective-permute-start(f32[4,24,512]{2,1,0:T(8,128)} %get-tuple-element.12.mid), channel_id=1, source_target_pairs={{0,8},{8,16},{16,24},{24,32},{32,40},{40,48},{48,56},{56,64},{64,7... | collective-permute-start | bytes 589832 | tf_op jit(solution)/shard_map/ppermute | solution.py:507
  48.8 16.7 %fit_own.1.solved = f32[2,328,384]{2,1,0:T(8,128)} custom-call(f32[1,128]{1,0:T(1,128)} %get-tuple-element.11.gnorm, f32[2,24,512]{2,1,0:T(8,128)} %get-tuple-element.13.own), custom_call_target="tpu_custom_call" | custom-call | tf_op jit(solution)/shard_map/fit_own/pallas_call | solution.py:393
  65.6 0.0 collective-permute-done.3.down
  65.6 0.0 copy-start.2
  65.6 0.0 collective-permute-done.2.up
  65.6 0.7 copy-done.2
  66.2 0.0 copy-start.3
  66.2 0.7 copy-done.3
  66.9 10.0 %fit_near.1 = f32[2,24,397]{2,1,0:T(8,128)} custom-call(s32[1,2,3]{2,1,0:T(2,128)} %adjacency.1, f32[1,128]{1,0:T(1,128)} %get-tuple-element.11.gnorm, f32[4,24,512]{2,1,0:T(8,128)} %get-tuple-element.12.mid, f32[4,24,512]{2,1,0:T(8,128)} %copy-done.3, f32[4,24,512]{2,1,0:T(8,128)} %copy-done.2, f32[2,328,384]{2,1,0:T(8,128)} %fit_own.1.solved), custom_call_target="tpu_custom_call" | custom-call | tf_op jit(solution)/shard_map/fit_near/pallas_call | solution.py:485
Async XLA Ops:
  13.8 26.7 %collective-permute-start = (f32[4,24,512]{2,1,0:T(8,128)}, f32[4,24,512]{2,1,0:T(8,128)S(1)}, u32[]{:S(2)}, u32[]{:S(2)}) collective-permute-start(f32[4,24,512]{2,1,0:T(8,128)} %get-tuple-element.9.proj1), channel_id=1, source_target_pairs={{0,1},{1,2},{2,3},{3,4},{4,5},{5,6},{6,7},{8,9},{9,10},{10,11},{11... | collective-permute-start | bytes 589832 | tf_op jit(solution)/shard_map/ppermute | solution.py:507
  18.3 22.2 %collective-permute-start.1 = (f32[4,24,512]{2,1,0:T(8,128)}, f32[4,24,512]{2,1,0:T(8,128)S(1)}, u32[]{:S(2)}, u32[]{:S(2)}) collective-permute-start(f32[4,24,512]{2,1,0:T(8,128)} %get-tuple-element.10.proj0), channel_id=1, source_target_pairs={{1,0},{2,1},{3,2},{4,3},{5,4},{6,5},{7,6},{9,8},{10,9},{11,10},{12... | collective-permute-start | bytes 589832 | tf_op jit(solution)/shard_map/ppermute | solution.py:508
  40.5 0.7 copy-start
  40.5 0.7 copy-start.1
  43.6 22.0 %collective-permute-start.3 = (f32[4,24,512]{2,1,0:T(8,128)}, f32[4,24,512]{2,1,0:T(8,128)S(1)}, u32[]{:S(2)}, u32[]{:S(2)}) collective-permute-start(f32[4,24,512]{2,1,0:T(8,128)} %get-tuple-element.12.mid), channel_id=1, source_target_pairs={{8,0},{16,8},{24,16},{32,24},{40,32},{48,40},{56,48},{64,56},{72,6... | collective-permute-start | bytes 589832 | tf_op jit(solution)/shard_map/ppermute | solution.py:508
  44.8 20.7 %collective-permute-start.2 = (f32[4,24,512]{2,1,0:T(8,128)}, f32[4,24,512]{2,1,0:T(8,128)S(1)}, u32[]{:S(2)}, u32[]{:S(2)}) collective-permute-start(f32[4,24,512]{2,1,0:T(8,128)} %get-tuple-element.12.mid), channel_id=1, source_target_pairs={{0,8},{8,16},{16,24},{24,32},{32,40},{40,48},{48,56},{56,64},{64,7... | collective-permute-start | bytes 589832 | tf_op jit(solution)/shard_map/ppermute | solution.py:507
  65.6 0.7 copy-start.2
  66.2 0.7 copy-start.3

commit v3 on v2

--- a/solution.py
+++ b/solution.py
@@ -27,123 +27,100 @@
     return lax.broadcasted_iota(jnp.int32, shape, 0), lax.broadcasted_iota(jnp.int32, shape, 1)
 
 
+DEPTH = 3
+CUTS = 1
+BLOCK = 256
+
+
 def fold_lanes(x):
     return (x[:, 0:128] + x[:, 128:256]) + (x[:, 256:384] + x[:, 384:512])
 
 
-def local_kernel(counts, basis, snaps, proj0, proj1, stats, acc):
-    s = pl.program_id(0)
-    v = pl.program_id(1)
-    count = counts[s]
-
-    @pl.when((s == 0) & (v == 0))
-    def _():
-        acc[...] = jnp.zeros_like(acc)
-
-    lane = lax.broadcasted_iota(jnp.int32, (R, SLOTS), 1)
-    modes = jnp.where(lane < count, basis[0, 0], jnp.zeros((), BF))
-    prod = jnp.dot(modes, snaps[0, 0], preferred_element_type=F32)
-    step = 128
-    row = lax.broadcasted_iota(jnp.int32, (step, 128), 0)
-    part = jnp.zeros((8, 128), F32)
-    for lo in range(0, SLOTS, step):
-        x = snaps[0, 0, lo : lo + step, :].astype(F32)
-        t = jnp.where(row < count - lo, fold_lanes(x * x), 0.0)
-        part = part + jnp.sum(t.reshape(step // 8, 8, 128), axis=0)
-    acc[v] += part
-
-    @pl.when(s == 0)
-    def _():
-        proj0[v] = prod
-
-    @pl.when(s == 1)
-    def _():
-        proj1[v] = prod
-
-    for sub, proj in ((0, proj0), (1, proj1)):
-
-        @pl.when((s == sub) & (v == NVAR - 1))
+def local_kernel(counts, basis, snaps, proj0, proj1, stats, modes, data, proj, acc, basis_sem, sems):
+    steps = COLS * NVAR
+    rows = SLOTS // CUTS
+
+    def copy(i, c):
+        part = pl.ds(c * rows, rows)
+        return pltpu.make_async_copy(snaps.at[i // NVAR, i % NVAR, part], data.at[i, part], sems.at[i, c])
+
+    def modes_copy(i):
+        return pltpu.make_async_copy(basis.at[i // NVAR, i % NVAR], modes.at[i], basis_sem.at[i])
+
+    for i in range(DEPTH):
+        modes_copy(i).start()
+        for c in range(CUTS):
+            copy(i, c).start()
+    acc[...] = jnp.zeros_like(acc)
+
+    def step(i, carry):
+        count = counts[0, i // NVAR]
+        v = i % NVAR
+
+        @pl.when(i + DEPTH < steps)
         def _():
-            q = NVAR
-            for a in range(NVAR):
-                pa = proj[a]
-                for b in range(a, NVAR):
-                    t = fold_lanes(pa * proj[b])
-                    acc[q] += t[0:8] + t[8:16] + t[16:24]
-                    q += 1
-
-    @pl.when((s == COLS - 1) & (v == NVAR - 1))
-    def _():
-        rows = jnp.sum(acc[...], axis=1)
-        total = jnp.sum(rows, axis=1, keepdims=True)
-        i, j = iotas((16, 128))
-        flat = jnp.sum(jnp.where(i == j, total, 0.0), axis=0, keepdims=True)
-        nodes = (counts[0] + counts[1]).astype(F32)
-        _, lane1 = iotas((1, 128))
-        stats[...] = jnp.broadcast_to(jnp.where(lane1 == 14, nodes, flat), (128, 128))
+            modes_copy(i + DEPTH).start()
+            for c in range(CUTS):
+                copy(i + DEPTH, c).start()
+
+        modes_copy(i).wait()
+        for c in range(CUTS):
+            copy(i, c).wait()
+        lane = lax.broadcasted_iota(jnp.int32, (R, BLOCK), 1)
+        row = lax.broadcasted_iota(jnp.int32, (BLOCK, 128), 0)
+        parts = []
+        prods = []
+        for lo in range(0, SLOTS, BLOCK):
+            kept = jnp.where(lane < count - lo, modes[i, :, lo : lo + BLOCK], jnp.zeros((), BF))
+            prods.append(jnp.dot(kept, data[i, lo : lo + BLOCK], preferred_element_type=F32))
+            x = data[i, lo : lo + BLOCK, :].astype(F32)
+            t = jnp.where(row < count - lo, fold_lanes(x * x), 0.0)
+            parts.append(jnp.sum(t.reshape(BLOCK // 8, 8, 128), axis=0))
+        proj[i] = sum(prods)
+        part = sum(parts)
+        acc[v] += part
+        return carry
+
+    lax.fori_loop(0, steps, step, 0)
+    q = NVAR
+    for a in range(NVAR):
+        for b in range(a, NVAR):
+            t = fold_lanes(proj[a] * proj[b]) + fold_lanes(proj[NVAR + a] * proj[NVAR + b])
+            acc[q] = t[0:8] + t[8:16] + t[16:24]
+            q += 1
+    for v in range(NVAR):
+        proj0[v] = proj[v]
+        proj1[v] = proj[NVAR + v]
+    total = jnp.sum(jnp.sum(acc[...], axis=1), axis=1, keepdims=True)
+    i, j = iotas((16, 128))
+    flat = jnp.sum(jnp.where(i == j, total, 0.0), axis=0, keepdims=True)
+    nodes = (counts[0, 0] + counts[0, 1]).astype(F32)
+    _, lane1 = iotas((1, 128))
+    stats[...] = jnp.broadcast_to(jnp.where(lane1 == 14, nodes, flat), (128, 128))
 
 
 def local_pass(snapshots, basis, counts):
+    vm = pl.BlockSpec(memory_space=pltpu.VMEM)
+    hbm = pl.BlockSpec(memory_space=pl.ANY)
     return pl.pallas_call(
         local_kernel,
-        grid_spec=pltpu.PrefetchScalarGridSpec(
-            num_scalar_prefetch=1,
-            grid=(COLS, NVAR),
-            in_specs=[
-                pl.BlockSpec((1, 1, R, SLOTS), lambda s, v, c: (s, v, 0, 0)),
-                pl.BlockSpec((1, 1, SLOTS, K), lambda s, v, c: (s, v, 0, 0)),
-            ],
-            out_specs=[
-                pl.BlockSpec((NVAR, R, K), lambda s, v, c: (0, 0, 0)),
-                pl.BlockSpec((NVAR, R, K), lambda s, v, c: (0, 0, 0)),
-                pl.BlockSpec((128, 128), lambda s, v, c: (0, 0)),
-            ],
-            scratch_shapes=[pltpu.VMEM((16, 8, 128), F32)],
-        ),
+        in_specs=[pl.BlockSpec(memory_space=pltpu.SMEM), hbm, hbm],
+        out_specs=[vm, vm, vm],
         out_shape=[
             jax.ShapeDtypeStruct((NVAR, R, K), F32),
             jax.ShapeDtypeStruct((NVAR, R, K), F32),
             jax.ShapeDtypeStruct((128, 128), F32),
         ],
-        compiler_params=pltpu.CompilerParams(dimension_semantics=("arbitrary", "arbitrary")),
+        scratch_shapes=[
+            pltpu.VMEM((COLS * NVAR, R, SLOTS), BF),
+            pltpu.VMEM((COLS * NVAR, SLOTS, K), BF),
+            pltpu.VMEM((COLS * NVAR, R, K), F32),
+            pltpu.VMEM((16, 8, 128), F32),
+            pltpu.SemaphoreType.DMA((COLS * NVAR,)),
+            pltpu.SemaphoreType.DMA((COLS * NVAR, CUTS)),
+        ],
         name="local",
     )(counts, basis, snapshots)
-
-
-def states_kernel(everyone, left, proj0, proj1, right, own, patch, gnorm):
-    total = jnp.sum(everyone[...], axis=0, keepdims=True)
-    nodes = total[:, 14:15]
-    inv = []
-    for v in range(NVAR):
-        scale = jnp.sqrt(total[:, v : v + 1] / (nodes * K) + 1e-06)
-        inv.append(1.0 / scale)
-    g = jnp.zeros((1, 1), F32)
-    q = NVAR
-    for a in range(NVAR):
-        for b in range(a, NVAR):
-            term = total[:, q : q + 1] * inv[a] * inv[b]
-            g = g + (term if a == b else 2.0 * term)
-            q += 1
-    gnorm[...] = jnp.broadcast_to(g * (1.0 / (256 * R * K)), (1, 128))
-    for c, proj in enumerate((left, proj0, proj1, right)):
-        t = proj[0] * inv[0]
-        for v in range(1, NVAR):
-            t = t + proj[v] * inv[v]
-        patch[c] = t
-        if c in (1, 2):
-            own[c - 1] = t
-
-
-def global_states(everyone, left, proj0, proj1, right):
-    return pl.pallas_call(
-        states_kernel,
-        out_shape=[
-            jax.ShapeDtypeStruct((COLS, R, K), F32),
-            jax.ShapeDtypeStruct((4, R, K), F32),
-            jax.ShapeDtypeStruct((1, 128), F32),
-        ],
-        name="states",
-    )(everyone, left, proj0, proj1, right)
 
 
 OWN = 328
@@ -265,8 +242,30 @@
     feats(FUT, pltpu.roll(state, K - 1, 1))
 
 
-def ridge(gnorm):
-    g = gnorm[...]
+def global_scales(everyone):
+    total = jnp.sum(everyone[...], axis=0, keepdims=True)
+    nodes = total[:, 14:15]
+    inv = []
+    for v in range(NVAR):
+        inv.append(1.0 / jnp.sqrt(total[:, v : v + 1] / (nodes * K) + 1e-06))
+    g = jnp.zeros((1, 1), F32)
+    q = NVAR
+    for a in range(NVAR):
+        for b in range(a, NVAR):
+            term = total[:, q : q + 1] * inv[a] * inv[b]
+            g = g + (term if a == b else 2.0 * term)
+            q += 1
+    return [jnp.broadcast_to(x, (1, 128)) for x in inv + [g * (1.0 / (256 * R * K))]]
+
+
+def scaled_sum(proj, inv):
+    t = proj[0] * inv[0]
+    for v in range(1, NVAR):
+        t = t + proj[v] * inv[v]
+    return t
+
+
+def ridge(g):
     return K * (HALF * g), K * (HALF * g * g)
 
 
@@ -278,8 +277,12 @@
     return lax.dot_general(a, b, (((1,), (1,)), ((), ())), preferred_element_type=F32)
 
 
-def own_kernel(gnorm, own, out, twice, fh, fm, fl, h, block):
+def own_kernel(everyone, proj0, proj1, out, own, scales, twice, fh, fm, fl, h, block):
     keep = past_mask()
+    found = global_scales(everyone)
+    scales[...] = jnp.concatenate(found + [jnp.zeros((3, 128), F32)], axis=0)
+    for m, proj in enumerate((proj0, proj1)):
+        own[m] = scaled_sum(proj, [x[:, 0:1] for x in found])
     for m in range(COLS):
 
         def put(at, x, m=m):
@@ -288,7 +291,7 @@
             fh[m, at : at + n], fm[m, at : at + n], fl[m, at : at + n] = a, b, c
 
         own_features(put, twice, m, own[m], keep)
-    lin, quad = ridge(gnorm)
+    lin, quad = ridge(found[NVAR])
     sub, lane = iotas((8, 128))
 
     def gram(m, r0, r1, c0, c1):
@@ -389,10 +392,14 @@
         out[m, 256:OWN, 256:LANES] = last
 
 
-def fit_own(gnorm, own):
+def fit_own(everyone, proj0, proj1):
     return pl.pallas_call(
         own_kernel,
-        out_shape=jax.ShapeDtypeStruct((COLS, OWN, LANES), F32),
+        out_shape=[
+            jax.ShapeDtypeStruct((COLS, OWN, LANES), F32),
+            jax.ShapeDtypeStruct((COLS, R, K), F32),
+            jax.ShapeDtypeStruct((8, 128), F32),
+        ],
         scratch_shapes=[
             pltpu.VMEM((COLS, 2 * R, K), F32),
             pltpu.VMEM((COLS, OWN + R, K), BF),
@@ -402,18 +409,27 @@
             pltpu.VMEM((COLS, 128, 128), F32),
         ],
         name="fit_own",
-    )(gnorm, own)
-
-
-def near_kernel(adjacency, gnorm, mid, up, down, solved, out, twice, fh, fm, fl, near, block, x, order):
+    )(everyone, proj0, proj1)
+
+
+def near_kernel(adjacency, scales, own, mid, up, down, solved, out, twice, fh, fm, fl, near, block, x, order, sems):
     row0 = lax.axis_index("gx_0") * 4 + lax.axis_index("gx_1")
     col0 = (lax.axis_index("gy_0") * 2 + lax.axis_index("gy_1")) * COLS
-    for c in range(4):
-        near[c] = up[c]
-        near[4 + c] = mid[c]
-        near[8 + c] = down[c]
+    for m in range(COLS):
+        for b in range(NB):
+            link = adjacency[0, m, b]
+            row = (link >> 4) - row0 + 1
+            col = (link & 15) - col0 + 1
+            slot = m * NB + b
+            for r, source in enumerate((up, mid, down)):
+
+                @pl.when(row == r)
+                def _():
+                    pltpu.make_async_copy(source.at[col], near.at[slot], sems.at[slot]).start()
+
     keep = past_mask()
-    lin, _ = ridge(gnorm)
+    lin, _ = ridge(scales[NVAR : NVAR + 1, :])
+    inv = [scales[v : v + 1, 0:1] for v in range(NVAR)]
     sub, lane = iotas((8, 128))
     for m in range(COLS):
 
@@ -421,12 +437,13 @@
             n = v.shape[0]
             fh[m, at : at + n], fm[m, at : at + n], fl[m, at : at + n] = split3(v)
 
-        own_features(put, twice, m, mid[1 + m], keep)
+        own_features(put, twice, m, own[m], keep)
+    for m in range(COLS):
         rows = []
         for b in range(NB):
-            link = adjacency[0, m, b]
-            at = ((link >> 4) - row0 + 1) * 4 + ((link & 15) - col0 + 1)
-            rows.append(jnp.where(keep, near[at], 0.0))
+            slot = m * NB + b
+            pltpu.make_async_copy(mid.at[0], near.at[slot], sems.at[slot]).wait()
+            rows.append(jnp.where(keep, scaled_sum(near.at[slot], inv), 0.0))
         nh, nm, nl = split3(jnp.concatenate(rows, axis=0))
         thirds = jnp.concatenate([nh, nm, nl], axis=0)
         p = nt(fh[m], thirds)
@@ -480,11 +497,12 @@
         out[m] = flat[NEAR : NEAR + R, 0:NF]
 
 
-def fit_near(adjacency, gnorm, mid, up, down, solved):
+def fit_near(adjacency, scales, own, mid, up, down, solved):
     vm = pl.BlockSpec(memory_space=pltpu.VMEM)
+    far = pl.BlockSpec(memory_space=pl.ANY)
     return pl.pallas_call(
         near_kernel,
-        in_specs=[pl.BlockSpec(memory_space=pltpu.SMEM)] + [vm] * 5,
+        in_specs=[pl.BlockSpec(memory_space=pltpu.SMEM), vm, vm, far, far, far, vm],
         out_specs=vm,
         out_shape=jax.ShapeDtypeStruct((COLS, R, NF), F32),
         scratch_shapes=[
@@ -492,13 +510,14 @@
             pltpu.VMEM((COLS, OWN + R, K), BF),
             pltpu.VMEM((COLS, OWN + R, K), BF),
             pltpu.VMEM((COLS, OWN + R, K), BF),
-            pltpu.VMEM((12, R, K), F32),
+            pltpu.VMEM((COLS * NB, NVAR, R, K), F32),
             pltpu.VMEM((COLS, 128, 128), F32),
             pltpu.VMEM((COLS, OWN + NEAR, 128), F32),
             pltpu.VMEM((COLS, 512, 128), F32),
+            pltpu.SemaphoreType.DMA((COLS * NB,)),
         ],
         name="fit_near",
-    )(adjacency, gnorm, mid, up, down, solved)
+    )(adjacency, scales, own, mid, up, down, solved)
 
 
 def shifts(axis, x, y):
@@ -510,13 +529,13 @@
 
 
 def body(snapshots, basis, node_counts, adjacency):
-    proj0, proj1, stats = local_pass(snapshots[0], basis[0], node_counts[0])
+    proj0, proj1, stats = local_pass(snapshots[0], basis[0], node_counts)
     everyone = lax.all_to_all(stats, GX_GY, 0, 0, tiled=True)
     left, right = shifts(GY, proj1, proj0)
-    own, mid, gnorm = global_states(everyone, left, proj0, proj1, right)
+    mid = jnp.stack([left, proj0, proj1, right])
     up, down = shifts(GX, mid, mid)
-    solved = fit_own(gnorm, own)
-    operator = fit_near(adjacency, gnorm, mid, up, down, solved)
+    solved, own, scales = fit_own(everyone, proj0, proj1)
+    operator = fit_near(adjacency, scales, own, mid, up, down, solved)
     return (jnp.swapaxes(operator, 1, 2)[None], own[None])
 
 

time: 77.7 us -> 78 us (level)
  Pallas kernels: 42.2 us -> 37.7 us
  waiting for transfers between devices: 0.01 us -> 2.91 us
  blocking collectives: 20.3 us -> 22 us
  other arithmetic: 0 us -> 1.08 us
  local copies, waits for them, and re-layouts: 2.08 us -> 1.12 us
    pallas_call x3 -> x2, Pallas kernels: 32.2 us -> 26.2 us  [the longest x1 17.1 us: fit_own(): pl.pallas_call(own_kernel, out_shape=[jax.ShapeDtypeStruct((COLS, OWN, LA...]
    ppermute x2, starting transfers between devices: 8.48 us -> 6.72 us  [shifts(): lax.ppermute(x, axis, [(i, i + 1) for i in range(n - 1)])]
    all_to_all x1, blocking collectives: 20.3 us -> 22 us  [body(): everyone = lax.all_to_all(stats, GX_GY, 0, 0, tiled=True)]
    ppermute x2, waiting for transfers between devices: 0.01 us -> 1.62 us  [shifts(): lax.ppermute(y, axis, [(i + 1, i) for i in range(n - 1)])]
    pallas_call x1, Pallas kernels: 10 us -> 11.4 us  [fit_near(): pl.pallas_call(near_kernel, in_specs=[pl.BlockSpec(memory_space=pltpu.SME...]
    ppermute x2, starting transfers between devices: 3.2 us -> 4.58 us  [shifts(): lax.ppermute(y, axis, [(i + 1, i) for i in range(n - 1)])]
    ppermute x2, waiting for transfers between devices: 0.01 us -> 1.29 us  [shifts(): lax.ppermute(x, axis, [(i, i + 1) for i in range(n - 1)])]
    another operation x0 -> x1, other arithmetic: none -> 1.08 us  [body(): mid = jnp.stack([left, proj0, proj1, right])]
  transfers between devices with their start and end apart: 4 -> 4, of which waited for: 0 -> 2; matrix products, arithmetic and copies ran while one was open for 0% -> 0% of each run, Pallas kernels for 22% -> 22%
where the time goes in v3:
time: 78 us; the launch traced here: 77 us
  Pallas kernels  37.7 us (48%)
  blocking collectives  22 us (28%)
  starting transfers between devices  11.3 us (14%)
  waiting for transfers between devices  2.91 us (4%)
  local copies, waits for them, and re-layouts  1.12 us (1%)
  other arithmetic  1.08 us (1%)
  between operations  0.87 us (1%)
    all_to_all x1, blocking collectives, body(): everyone = lax.all_to_all(stats, GX_GY, 0, 0, tiled=True)  22 us
    pallas_call x1, Pallas kernels, fit_own(): pl.pallas_call(own_kernel, out_shape=[jax.ShapeDtypeStruct((COLS, OWN, LA...  17.1 us
    pallas_call x1, Pallas kernels, fit_near(): pl.pallas_call(near_kernel, in_specs=[pl.BlockSpec(memory_space=pltpu.SME...  11.4 us
    pallas_call x1, Pallas kernels, local_pass(): pl.pallas_call(local_kernel, in_specs=[pl.BlockSpec(memory_space=pltpu.SM...  9.16 us
    ppermute x2, starting transfers between devices, shifts(): lax.ppermute(x, axis, [(i, i + 1) for i in range(n - 1)])  6.72 us
    ppermute x2, starting transfers between devices, shifts(): lax.ppermute(y, axis, [(i + 1, i) for i in range(n - 1)])  4.58 us
    ppermute x2, waiting for transfers between devices, shifts(): lax.ppermute(y, axis, [(i + 1, i) for i in range(n - 1)])  1.62 us
  transfers between devices with their start and end apart: 4, of which 2 were waited for; matrix products, arithmetic and copies ran while one was open for 0% of the time, Pallas kernels for 22%

profile of v3, /device:TPU:1, one launch (start us, length us, event | category | flops | bytes accessed | tf_op | source)
XLA Modules:
  0.0 77.0 jit_solution(7402462566706082882)
XLA Ops:
  0.6 9.2 %local.1 = (f32[4,24,512]{2,1,0:T(8,128)}, f32[4,24,512]{2,1,0:T(8,128)}, f32[128,128]{1,0:T(8,128)}) custom-call(s32[1,2]{1,0:T(1,128)} %counts.1, bf16[2,4,24,2048]{3,2,1,0:T(8,128)(2,1)} %bitcast.15, bf16[2,4,2048,512]{3,2,1,0:T(8,128)(2,1)} %bitcast.14), custom_call_target="tpu_custom_call" | custom-call | tf_op jit(solution)/shard_map/local/pallas_call | solution.py:105
  9.8 3.3 %collective-permute-start.1 = (f32[4,24,512]{2,1,0:T(8,128)}, f32[4,24,512]{2,1,0:T(8,128)S(1)}, u32[]{:S(2)}, u32[]{:S(2)}) collective-permute-start(f32[4,24,512]{2,1,0:T(8,128)} %get-tuple-element.9.proj0), channel_id=1, source_target_pairs={{1,0},{2,1},{3,2},{4,3},{5,4},{6,5},{7,6},{9,8},{10,9},{11,10},{12... | collective-permute-start | bytes 589832 | tf_op jit(solution)/shard_map/ppermute | solution.py:527
  13.1 3.1 %collective-permute-start = (f32[4,24,512]{2,1,0:T(8,128)}, f32[4,24,512]{2,1,0:T(8,128)S(1)}, u32[]{:S(2)}, u32[]{:S(2)}) collective-permute-start(f32[4,24,512]{2,1,0:T(8,128)} %get-tuple-element.10.proj1), channel_id=1, source_target_pairs={{0,1},{1,2},{2,3},{3,4},{4,5},{5,6},{6,7},{8,9},{9,10},{10,11},{11... | collective-permute-start | bytes 589832 | tf_op jit(solution)/shard_map/ppermute | solution.py:526
  16.2 1.6 %collective-permute-done.1 = f32[4,24,512]{2,1,0:T(8,128)S(1)} collective-permute-done((f32[4,24,512]{2,1,0:T(8,128)}, f32[4,24,512]{2,1,0:T(8,128)S(1)}, u32[]{:S(2)}, u32[]{:S(2)}) %collective-permute-start.1) | collective-permute-done | bytes 196640 | tf_op jit(solution)/shard_map/ppermute | solution.py:527
  17.8 1.3 %collective-permute-done = f32[4,24,512]{2,1,0:T(8,128)S(1)} collective-permute-done((f32[4,24,512]{2,1,0:T(8,128)}, f32[4,24,512]{2,1,0:T(8,128)S(1)}, u32[]{:S(2)}, u32[]{:S(2)}) %collective-permute-start) | collective-permute-done | bytes 196640 | tf_op jit(solution)/shard_map/ppermute | solution.py:526
  19.1 1.1 %pad_maximum_fusion.mid = f32[4,4,24,512]{3,2,1,0:T(8,128)S(1)} fusion(f32[1,4,24,512]{3,2,1,0:T(8,128)S(1)} %bitcast.19, f32[1,4,24,512]{3,2,1,0:T(8,128)} %bitcast.17, f32[1,4,24,512]{3,2,1,0:T(8,128)} %bitcast.16, f32[1,4,24,512]{3,2,1,0:T(8,128)S(1)} %bitcast.20), kind=kLoop, calls=%fused_computation | loop fusion | flops 589824 | bytes 1572864 | tf_op jit(solution)/shard_map/stack | solution.py:535
  20.2 0.0 copy-start
  20.2 3.6 %collective-permute-start.2 = (f32[4,4,24,512]{3,2,1,0:T(8,128)S(1)}, f32[4,4,24,512]{3,2,1,0:T(8,128)S(1)}, u32[]{:S(2)}, u32[]{:S(2)}) collective-permute-start(f32[4,4,24,512]{3,2,1,0:T(8,128)S(1)} %pad_maximum_fusion.mid), channel_id=1, source_target_pairs={{0,8},{8,16},{16,24},{24,32},{32,40},{40,48},{48,56},{56,64},{64,7... | collective-permute-start | bytes 2359304 | tf_op jit(solution)/shard_map/ppermute | solution.py:526
  23.8 1.3 %collective-permute-start.3 = (f32[4,4,24,512]{3,2,1,0:T(8,128)S(1)}, f32[4,4,24,512]{3,2,1,0:T(8,128)S(1)}, u32[]{:S(2)}, u32[]{:S(2)}) collective-permute-start(f32[4,4,24,512]{3,2,1,0:T(8,128)S(1)} %pad_maximum_fusion.mid), channel_id=1, source_target_pairs={{8,0},{16,8},{24,16},{32,24},{40,32},{48,40},{56,48},{64,56},{72,6... | collective-permute-start | bytes 2359304 | tf_op jit(solution)/shard_map/ppermute | solution.py:527
  25.1 22.0 %all_to_all.11 = f32[128,1,128]{2,1,0:T(1,128)} all-to-all(f32[128,1,128]{2,1,0:T(1,128)} %bitcast.23), channel_id=1, replica_groups=mesh['gx_0'=4,'gx_1'=4,'gy_0'=4,'gy_1'=2] {'gx_0','gx_1','gy_0','gy_1'}, dimensions={0} | all-to-all | bytes 131072 | tf_op jit(solution)/shard_map/all_to_all | solution.py:533
  47.2 17.1 %fit_own.1 = (f32[2,328,384]{2,1,0:T(8,128)}, f32[2,24,512]{2,1,0:T(8,128)}, f32[8,128]{1,0:T(8,128)}) custom-call(f32[128,128]{1,0:T(8,128)} %bitcast.18, f32[4,24,512]{2,1,0:T(8,128)} %get-tuple-element.9.proj0, f32[4,24,512]{2,1,0:T(8,128)} %get-tuple-element.10.proj1), custom_call_target="tpu_custom_call" | custom-call | tf_op jit(solution)/shard_map/fit_own/pallas_call | solution.py:396
  64.3 0.0 collective-permute-done.2.up
  64.3 0.0 copy-start.1
  64.3 0.0 collective-permute-done.3.down
  64.3 0.0 copy-start.2
  64.3 0.0 copy-done
  64.3 0.9 %copy-done.1 = f32[4,4,24,512]{3,2,1,0:T(8,128)} copy-done((f32[4,4,24,512]{3,2,1,0:T(8,128)}, f32[4,4,24,512]{3,2,1,0:T(8,128)S(1)}, u32[]{:S(2)}) %copy-start.1) | copy-done | bytes 786456
  65.1 0.3 copy-done.2
  65.4 11.4 %fit_near.1 = f32[2,24,397]{2,1,0:T(8,128)} custom-call(s32[1,2,3]{2,1,0:T(2,128)} %adjacency.1, f32[8,128]{1,0:T(8,128)} %get-tuple-element.11.scales, f32[2,24,512]{2,1,0:T(8,128)} %get-tuple-element.12.own, f32[4,4,24,512]{3,2,1,0:T(8,128)} %copy-done, f32[4,4,24,512]{3,2,1,0:T(8,128)} %copy-done.1, f32[4,4,24,512]{3,2,1,0:T(8,128)} %copy-done.2, ...), custom_call_target="tpu_custom_call" | custom-call | tf_op jit(solution)/shard_map/fit_near/pallas_call | solution.py:503
Async XLA Ops:
  9.8 8.1 %collective-permute-start.1 = (f32[4,24,512]{2,1,0:T(8,128)}, f32[4,24,512]{2,1,0:T(8,128)S(1)}, u32[]{:S(2)}, u32[]{:S(2)}) collective-permute-start(f32[4,24,512]{2,1,0:T(8,128)} %get-tuple-element.9.proj0), channel_id=1, source_target_pairs={{1,0},{2,1},{3,2},{4,3},{5,4},{6,5},{7,6},{9,8},{10,9},{11,10},{12... | collective-permute-start | bytes 589832 | tf_op jit(solution)/shard_map/ppermute | solution.py:527
  13.1 6.0 %collective-permute-start = (f32[4,24,512]{2,1,0:T(8,128)}, f32[4,24,512]{2,1,0:T(8,128)S(1)}, u32[]{:S(2)}, u32[]{:S(2)}) collective-permute-start(f32[4,24,512]{2,1,0:T(8,128)} %get-tuple-element.10.proj1), channel_id=1, source_target_pairs={{0,1},{1,2},{2,3},{3,4},{4,5},{5,6},{6,7},{8,9},{9,10},{10,11},{11... | collective-permute-start | bytes 589832 | tf_op jit(solution)/shard_map/ppermute | solution.py:526
  20.2 44.1 %copy-start = (f32[4,4,24,512]{3,2,1,0:T(8,128)}, f32[4,4,24,512]{3,2,1,0:T(8,128)S(1)}, u32[]{:S(2)}) copy-start(f32[4,4,24,512]{3,2,1,0:T(8,128)S(1)} %pad_maximum_fusion.mid) | copy-start | bytes 2359300
  20.2 44.0 %collective-permute-start.2 = (f32[4,4,24,512]{3,2,1,0:T(8,128)S(1)}, f32[4,4,24,512]{3,2,1,0:T(8,128)S(1)}, u32[]{:S(2)}, u32[]{:S(2)}) collective-permute-start(f32[4,4,24,512]{3,2,1,0:T(8,128)S(1)} %pad_maximum_fusion.mid), channel_id=1, source_target_pairs={{0,8},{8,16},{16,24},{24,32},{32,40},{40,48},{48,56},{56,64},{64,7... | collective-permute-start | bytes 2359304 | tf_op jit(solution)/shard_map/ppermute | solution.py:526
  23.8 40.4 %collective-permute-start.3 = (f32[4,4,24,512]{3,2,1,0:T(8,128)S(1)}, f32[4,4,24,512]{3,2,1,0:T(8,128)S(1)}, u32[]{:S(2)}, u32[]{:S(2)}) collective-permute-start(f32[4,4,24,512]{3,2,1,0:T(8,128)S(1)} %pad_maximum_fusion.mid), channel_id=1, source_target_pairs={{8,0},{16,8},{24,16},{32,24},{40,32},{48,40},{56,48},{64,56},{72,6... | collective-permute-start | bytes 2359304 | tf_op jit(solution)/shard_map/ppermute | solution.py:527
  64.3 0.9 %copy-start.1 = (f32[4,4,24,512]{3,2,1,0:T(8,128)}, f32[4,4,24,512]{3,2,1,0:T(8,128)S(1)}, u32[]{:S(2)}) copy-start(f32[4,4,24,512]{3,2,1,0:T(8,128)S(1)} %collective-permute-done.2.up) | copy-start | bytes 2359300
  64.3 1.1 %copy-start.2 = (f32[4,4,24,512]{3,2,1,0:T(8,128)}, f32[4,4,24,512]{3,2,1,0:T(8,128)S(1)}, u32[]{:S(2)}) copy-start(f32[4,4,24,512]{3,2,1,0:T(8,128)S(1)} %collective-permute-done.3.down) | copy-start | bytes 2359300

commit v4 on v3

--- a/solution.py
+++ b/solution.py
@@ -99,6 +99,13 @@
     stats[...] = jnp.broadcast_to(jnp.where(lane1 == 14, nodes, flat), (128, 128))
 
 
+ROOM = 36 << 20
+
+
+def on_chip(*xs):
+    return [pltpu.with_memory_space_constraint(x, pltpu.VMEM) for x in xs]
+
+
 def local_pass(snapshots, basis, counts):
     vm = pl.BlockSpec(memory_space=pltpu.VMEM)
     hbm = pl.BlockSpec(memory_space=pl.ANY)
@@ -107,9 +114,9 @@
         in_specs=[pl.BlockSpec(memory_space=pltpu.SMEM), hbm, hbm],
         out_specs=[vm, vm, vm],
         out_shape=[
-            jax.ShapeDtypeStruct((NVAR, R, K), F32),
-            jax.ShapeDtypeStruct((NVAR, R, K), F32),
-            jax.ShapeDtypeStruct((128, 128), F32),
+            pltpu.VMEM((NVAR, R, K), F32),
+            pltpu.VMEM((NVAR, R, K), F32),
+            pltpu.VMEM((128, 128), F32),
         ],
         scratch_shapes=[
             pltpu.VMEM((COLS * NVAR, R, SLOTS), BF),
@@ -119,8 +126,9 @@
             pltpu.SemaphoreType.DMA((COLS * NVAR,)),
             pltpu.SemaphoreType.DMA((COLS * NVAR, CUTS)),
         ],
+        compiler_params=pltpu.CompilerParams(vmem_limit_bytes=ROOM),
         name="local",
-    )(counts, basis, snapshots)
+    )(*[pltpu.with_memory_space_constraint(x, pltpu.HBM) for x in (counts, basis, snapshots)])
 
 
 OWN = 328
@@ -396,9 +404,9 @@
     return pl.pallas_call(
         own_kernel,
         out_shape=[
-            jax.ShapeDtypeStruct((COLS, OWN, LANES), F32),
-            jax.ShapeDtypeStruct((COLS, R, K), F32),
-            jax.ShapeDtypeStruct((8, 128), F32),
+            pltpu.VMEM((COLS, OWN, LANES), F32),
+            pltpu.VMEM((COLS, R, K), F32),
+            pltpu.VMEM((8, 128), F32),
         ],
         scratch_shapes=[
             pltpu.VMEM((COLS, 2 * R, K), F32),
@@ -408,8 +416,9 @@
             pltpu.VMEM((COLS, OWN, LANES), F32),
             pltpu.VMEM((COLS, 128, 128), F32),
         ],
+        compiler_params=pltpu.CompilerParams(vmem_limit_bytes=ROOM),
         name="fit_own",
-    )(everyone, proj0, proj1)
+    )(*on_chip(everyone, proj0, proj1))
 
 
 def near_kernel(adjacency, scales, own, mid, up, down, solved, out, twice, fh, fm, fl, near, block, x, order, sems):
@@ -516,8 +525,9 @@
             pltpu.VMEM((COLS, 512, 128), F32),
             pltpu.SemaphoreType.DMA((COLS * NB,)),
         ],
+        compiler_params=pltpu.CompilerParams(vmem_limit_bytes=ROOM),
         name="fit_near",
-    )(adjacency, scales, own, mid, up, down, solved)
+    )(pltpu.with_memory_space_constraint(adjacency, pltpu.HBM), *on_chip(scales, own, mid, up, down, solved))
 
 
 def shifts(axis, x, y):

time: 78 us -> 73.5 us (0.942)
  Pallas kernels: 37.7 us -> 35.2 us
  other arithmetic: 1.08 us -> 0.06 us
    pallas_call x1, Pallas kernels: 17.1 us -> 15.1 us  [fit_own(): pl.pallas_call(own_kernel, out_shape=[pltpu.VMEM((COLS, OWN, LANES), F32)...]
    another operation x1, other arithmetic: 1.08 us -> 0.06 us  [body(): mid = jnp.stack([left, proj0, proj1, right])]
  transfers between devices with their start and end apart: 4 -> 4, of which waited for: 2 -> 2; matrix products, arithmetic and copies ran while one was open for 0% -> 1% of each run, Pallas kernels for 22% -> 21%
where the time goes in v4:
time: 73.5 us; the launch traced here: 72.3 us
  Pallas kernels  35.2 us (48%)
  blocking collectives  21.7 us (30%)
  starting transfers between devices  11.3 us (15%)
  waiting for transfers between devices  2.6 us (4%)
  between operations  0.85 us (1%)
    all_to_all x1, blocking collectives, body(): everyone = lax.all_to_all(stats, GX_GY, 0, 0, tiled=True)  21.7 us
    pallas_call x1, Pallas kernels, fit_own(): pl.pallas_call(own_kernel, out_shape=[pltpu.VMEM((COLS, OWN, LANES), F32)...  15.1 us
    pallas_call x1, Pallas kernels, fit_near(): pl.pallas_call(near_kernel, in_specs=[pl.BlockSpec(memory_space=pltpu.SME...  11.6 us
    pallas_call x1, Pallas kernels, local_pass(): pl.pallas_call(local_kernel, in_specs=[pl.BlockSpec(memory_space=pltpu.SM...  8.51 us
    ppermute x2, starting transfers between devices, shifts(): lax.ppermute(x, axis, [(i, i + 1) for i in range(n - 1)])  6.72 us
    ppermute x2, starting transfers between devices, shifts(): lax.ppermute(y, axis, [(i + 1, i) for i in range(n - 1)])  4.58 us
  transfers between devices with their start and end apart: 4, of which 2 were waited for; matrix products, arithmetic and copies ran while one was open for 1% of the time, Pallas kernels for 21%

profile of v4, /device:TPU:1, one launch (start us, length us, event | category | flops | bytes accessed | tf_op | source)
XLA Modules:
  0.0 72.3 jit_solution(13862496636705900368)
XLA Ops:
  0.6 8.5 %local.1 = (f32[4,24,512]{2,1,0:T(8,128)S(1)}, f32[4,24,512]{2,1,0:T(8,128)S(1)}, f32[128,128]{1,0:T(8,128)S(1)}) custom-call(s32[1,2]{1,0:T(1,128)} %counts.1, bf16[2,4,24,2048]{3,2,1,0:T(8,128)(2,1)} %bitcast.20, bf16[2,4,2048,512]{3,2,1,0:T(8,128)(2,1)} %bitcast.19), custom_call_target="tpu_custom_call" | custom-call | tf_op jit(solution)/shard_map/local/pallas_call | solution.py:112
  9.1 3.3 %collective-permute-start.1 = (f32[4,24,512]{2,1,0:T(8,128)S(1)}, f32[4,24,512]{2,1,0:T(8,128)S(1)}, u32[]{:S(2)}, u32[]{:S(2)}) collective-permute-start(f32[4,24,512]{2,1,0:T(8,128)S(1)} %get-tuple-element.9.proj0), channel_id=1, source_target_pairs={{1,0},{2,1},{3,2},{4,3},{5,4},{6,5},{7,6},{9,8},{10,9},{11,10},{12... | collective-permute-start | bytes 589832 | tf_op jit(solution)/shard_map/ppermute | solution.py:537
  12.4 3.1 %collective-permute-start = (f32[4,24,512]{2,1,0:T(8,128)S(1)}, f32[4,24,512]{2,1,0:T(8,128)S(1)}, u32[]{:S(2)}, u32[]{:S(2)}) collective-permute-start(f32[4,24,512]{2,1,0:T(8,128)S(1)} %get-tuple-element.10.proj1), channel_id=1, source_target_pairs={{0,1},{1,2},{2,3},{3,4},{4,5},{5,6},{6,7},{8,9},{9,10},{10,11},{11... | collective-permute-start | bytes 589832 | tf_op jit(solution)/shard_map/ppermute | solution.py:536
  15.6 1.4 %collective-permute-done.1 = f32[4,24,512]{2,1,0:T(8,128)S(1)} collective-permute-done((f32[4,24,512]{2,1,0:T(8,128)S(1)}, f32[4,24,512]{2,1,0:T(8,128)S(1)}, u32[]{:S(2)}, u32[]{:S(2)}) %collective-permute-start.1) | collective-permute-done | bytes 196640 | tf_op jit(solution)/shard_map/ppermute | solution.py:537
  17.0 1.2 %collective-permute-done = f32[4,24,512]{2,1,0:T(8,128)S(1)} collective-permute-done((f32[4,24,512]{2,1,0:T(8,128)S(1)}, f32[4,24,512]{2,1,0:T(8,128)S(1)}, u32[]{:S(2)}, u32[]{:S(2)}) %collective-permute-start) | collective-permute-done | bytes 196640 | tf_op jit(solution)/shard_map/ppermute | solution.py:536
  18.2 0.1 pad_maximum_fusion.mid
  18.2 3.6 %collective-permute-start.2 = (f32[4,4,24,512]{3,2,1,0:T(8,128)S(1)}, f32[4,4,24,512]{3,2,1,0:T(8,128)S(1)}, u32[]{:S(2)}, u32[]{:S(2)}) collective-permute-start(f32[4,4,24,512]{3,2,1,0:T(8,128)S(1)} %pad_maximum_fusion.mid), channel_id=1, source_target_pairs={{0,8},{8,16},{16,24},{24,32},{32,40},{40,48},{48,56},{56,64},{64,7... | collective-permute-start | bytes 2359304 | tf_op jit(solution)/shard_map/ppermute | solution.py:536
  21.8 1.3 %collective-permute-start.3 = (f32[4,4,24,512]{3,2,1,0:T(8,128)S(1)}, f32[4,4,24,512]{3,2,1,0:T(8,128)S(1)}, u32[]{:S(2)}, u32[]{:S(2)}) collective-permute-start(f32[4,4,24,512]{3,2,1,0:T(8,128)S(1)} %pad_maximum_fusion.mid), channel_id=1, source_target_pairs={{8,0},{16,8},{24,16},{32,24},{40,32},{48,40},{56,48},{64,56},{72,6... | collective-permute-start | bytes 2359304 | tf_op jit(solution)/shard_map/ppermute | solution.py:537
  23.1 21.7 %all_to_all.11 = f32[128,1,128]{2,1,0:T(1,128)S(1)} all-to-all(f32[128,1,128]{2,1,0:T(1,128)S(1)} %bitcast.18), channel_id=1, replica_groups=mesh['gx_0'=4,'gx_1'=4,'gy_0'=4,'gy_1'=2] {'gx_0','gx_1','gy_0','gy_1'}, dimensions={0} | all-to-all | bytes 131072 | tf_op jit(solution)/shard_map/all_to_all | solution.py:543
  44.8 15.1 %fit_own.1 = (f32[2,328,384]{2,1,0:T(8,128)S(1)}, f32[2,24,512]{2,1,0:T(8,128)S(1)}, f32[8,128]{1,0:T(8,128)S(1)}) custom-call(f32[128,128]{1,0:T(8,128)S(1)} %bitcast.17, f32[4,24,512]{2,1,0:T(8,128)S(1)} %get-tuple-element.9.proj0, f32[4,24,512]{2,1,0:T(8,128)S(1)} %get-tuple-element.10.proj1), custom_call_target="tpu_custom_call" | custom-call | tf_op jit(solution)/shard_map/fit_own/pallas_call | solution.py:404
  59.9 0.6 copy.7
  60.5 0.0 collective-permute-done.2.up
  60.5 0.0 collective-permute-done.3.down
  60.5 11.6 %fit_near.1 = f32[2,24,397]{2,1,0:T(8,128)} custom-call(s32[1,2,3]{2,1,0:T(2,128)} %adjacency.1, f32[8,128]{1,0:T(8,128)S(1)} %get-tuple-element.11.scales, f32[2,24,512]{2,1,0:T(8,128)S(1)} %get-tuple-element.12.own, f32[4,4,24,512]{3,2,1,0:T(8,128)S(1)} %pad_maximum_fusion.mid, f32[4,4,24,512]{3,2,1,0:T(8,128)S(1)} %collective-permute-done.2.up, ...), custom_call_target="tpu_custom_call" | custom-call | tf_op jit(solution)/shard_map/fit_near/pallas_call | solution.py:512
Async XLA Ops:
  9.1 7.8 %collective-permute-start.1 = (f32[4,24,512]{2,1,0:T(8,128)S(1)}, f32[4,24,512]{2,1,0:T(8,128)S(1)}, u32[]{:S(2)}, u32[]{:S(2)}) collective-permute-start(f32[4,24,512]{2,1,0:T(8,128)S(1)} %get-tuple-element.9.proj0), channel_id=1, source_target_pairs={{1,0},{2,1},{3,2},{4,3},{5,4},{6,5},{7,6},{9,8},{10,9},{11,10},{12... | collective-permute-start | bytes 589832 | tf_op jit(solution)/shard_map/ppermute | solution.py:537
  12.4 5.7 %collective-permute-start = (f32[4,24,512]{2,1,0:T(8,128)S(1)}, f32[4,24,512]{2,1,0:T(8,128)S(1)}, u32[]{:S(2)}, u32[]{:S(2)}) collective-permute-start(f32[4,24,512]{2,1,0:T(8,128)S(1)} %get-tuple-element.10.proj1), channel_id=1, source_target_pairs={{0,1},{1,2},{2,3},{3,4},{4,5},{5,6},{6,7},{8,9},{9,10},{10,11},{11... | collective-permute-start | bytes 589832 | tf_op jit(solution)/shard_map/ppermute | solution.py:536
  18.2 42.3 %collective-permute-start.2 = (f32[4,4,24,512]{3,2,1,0:T(8,128)S(1)}, f32[4,4,24,512]{3,2,1,0:T(8,128)S(1)}, u32[]{:S(2)}, u32[]{:S(2)}) collective-permute-start(f32[4,4,24,512]{3,2,1,0:T(8,128)S(1)} %pad_maximum_fusion.mid), channel_id=1, source_target_pairs={{0,8},{8,16},{16,24},{24,32},{32,40},{40,48},{48,56},{56,64},{64,7... | collective-permute-start | bytes 2359304 | tf_op jit(solution)/shard_map/ppermute | solution.py:536
  21.8 38.7 %collective-permute-start.3 = (f32[4,4,24,512]{3,2,1,0:T(8,128)S(1)}, f32[4,4,24,512]{3,2,1,0:T(8,128)S(1)}, u32[]{:S(2)}, u32[]{:S(2)}) collective-permute-start(f32[4,4,24,512]{3,2,1,0:T(8,128)S(1)} %pad_maximum_fusion.mid), channel_id=1, source_target_pairs={{8,0},{16,8},{24,16},{32,24},{40,32},{48,40},{56,48},{64,56},{72,6... | collective-permute-start | bytes 2359304 | tf_op jit(solution)/shard_map/ppermute | solution.py:537

commit v5 on v4

--- a/solution.py
+++ b/solution.py
@@ -20,7 +20,6 @@
 HALF = 0.5
 F32 = jnp.float32
 BF = jnp.bfloat16
-HI = lax.Precision.HIGHEST
 
 
 def iotas(shape):
@@ -159,7 +158,31 @@
 
 
 def mm(a, b):
-    return jnp.dot(a, b, precision=HI, preferred_element_type=F32)
+    ah, am, al = split3(a)
+    bh, bm, bl = split3(b)
+    n = b.shape[1]
+    w = jnp.concatenate([bh, bm], axis=1)
+    p = dot(jnp.concatenate([ah, am], axis=1), jnp.concatenate([w, w], axis=0))
+    q = dot(jnp.concatenate([ah, al], axis=1), jnp.concatenate([bl, bh], axis=0))
+    return p[:, :n] + (p[:, n:] + q)
+
+
+def mm_thirds(a, b):
+    bh, bm, bl = split3(b)
+    n = b.shape[1]
+    w = jnp.concatenate([bh, bm], axis=1)
+    p = dot(a[0], w)
+    q = dot(a[1], w)
+    r = dot(a[0], bl) + dot(a[2], bh)
+    return p[:, :n] + ((p[:, n:] + q[:, :n]) + (q[:, n:] + r))
+
+
+def first_lanes(x):
+    return jnp.where(iotas(x.shape)[1] < NEAR, x, 0.0)
+
+
+def to_rows(x, rows):
+    return jnp.concatenate([x, jnp.zeros((rows - x.shape[0], x.shape[1]), F32)], axis=0)
 
 
 def tree(terms):
@@ -179,7 +202,24 @@
     return u[:, :128] + (u[:, 128:] + v)
 
 
-def invert(block, tiles, strip=4, look=2):
+def pivots(col, riders, sub):
+    recips = jnp.zeros((8, 128), F32)
+    diag = sub_copy(col[0], 0)
+    for j in range(8):
+        r = 1.0 / diag
+        bare = jnp.where(sub == j, 0.0, col[j])
+        recips = jnp.where(sub == j, r, recips)
+        heads = {k: sub_copy(col[k], j) for k in range(j + 1, 8)}
+        if j < 7:
+            diag = sub_copy(col[j + 1], j + 1) - (sub_copy(col[j], j + 1) * heads[j + 1]) * r
+        mult = bare * r
+        for k in range(j + 1, 8):
+            col[k] = col[k] - mult * heads[k]
+        riders = [x - mult * sub_copy(x, j) for x in riders]
+    return [x * recips for x in riders]
+
+
+def invert(block, tiles, strip=4, look=1):
     sub, lane = iotas((8, 128))
     for s in range(0, tiles, strip):
         own = list(range(s, min(s + strip, tiles)))
@@ -192,16 +232,7 @@
             for m in range(COLS):
                 tile = block[m, base : base + 8, :]
                 col = [lane_copy(tile, base + k) for k in range(8)]
-                x = jnp.where(inside, unit, tile)
-                recips = jnp.zeros((8, 128), F32)
-                for j in range(8):
-                    r = 1.0 / sub_copy(col[j], j)
-                    mult = jnp.where(sub == j, 0.0, col[j]) * r
-                    recips = jnp.where(sub == j, r, recips)
-                    for k in range(j + 1, 8):
-                        col[k] = col[k] - mult * sub_copy(col[k], j)
-                    x = x - mult * sub_copy(x, j)
-                w = x * recips
+                w = pivots(col, [jnp.where(inside, unit, tile)], sub)[0]
                 block[m, base : base + 8, :] = w
                 ws.append([sub_copy(w, j) for j in range(8)])
             for t in [t for t in own + ahead if t > p] + [t for t in own if t < p]:
@@ -216,8 +247,8 @@
             for m in range(COLS):
                 rest = [block[m, a:b, :] for a, b in ranges]
                 rest = jnp.concatenate(rest, axis=0) if len(rest) > 1 else rest[0]
-                _, wide = iotas(rest.shape)
-                kept = jnp.where((wide >= lo) & (wide < hi), 0.0, rest)
+                _, wide_l = iotas(rest.shape)
+                kept = jnp.where((wide_l >= lo) & (wide_l < hi), 0.0, rest)
                 new = kept - padded_dot(rest, block[m, lo:hi, :], lo)
                 at = 0
                 for a, b in ranges:
@@ -235,6 +266,23 @@
             done += 1
     for f in work[done:]:
         f()
+
+
+def states_kernel(everyone, left, proj0, proj1, right, mid, gnorm):
+    found = global_scales(everyone)
+    gnorm[...] = jnp.broadcast_to(found[NVAR], (8, 128))
+    inv = [x[:, 0:1] for x in found]
+    for c, proj in enumerate((left, proj0, proj1, right)):
+        mid[c] = scaled_sum(proj, inv)
+
+
+def global_states(everyone, left, proj0, proj1, right):
+    return pl.pallas_call(
+        states_kernel,
+        out_shape=[pltpu.VMEM((4, R, K), F32), pltpu.VMEM((8, 128), F32)],
+        compiler_params=pltpu.CompilerParams(vmem_limit_bytes=ROOM),
+        name="states",
+    )(*on_chip(everyone, left, proj0, proj1, right))
 
 
 def own_features(feats, twice, m, state, keep):
@@ -285,21 +333,16 @@
     return lax.dot_general(a, b, (((1,), (1,)), ((), ())), preferred_element_type=F32)
 
 
-def own_kernel(everyone, proj0, proj1, out, own, scales, twice, fh, fm, fl, h, block):
+def own_kernel(gnorm, mid, fh, fm, fl, ah, am, al, tail, twice, h, block):
     keep = past_mask()
-    found = global_scales(everyone)
-    scales[...] = jnp.concatenate(found + [jnp.zeros((3, 128), F32)], axis=0)
-    for m, proj in enumerate((proj0, proj1)):
-        own[m] = scaled_sum(proj, [x[:, 0:1] for x in found])
     for m in range(COLS):
 
         def put(at, x, m=m):
-            a, b, c = split3(x)
             n = x.shape[0]
-            fh[m, at : at + n], fm[m, at : at + n], fl[m, at : at + n] = a, b, c
-
-        own_features(put, twice, m, own[m], keep)
-    lin, quad = ridge(found[NVAR])
+            fh[m, at : at + n], fm[m, at : at + n], fl[m, at : at + n] = split3(x)
+
+        own_features(put, twice, m, mid[1 + m], keep)
+    lin, quad = ridge(gnorm[0:1])
     sub, lane = iotas((8, 128))
 
     def gram(m, r0, r1, c0, c1):
@@ -389,104 +432,89 @@
         return go
 
     spread(invert(block, 9), 8, [after1(m, k) for k in range(4) for m in range(COLS)])
-    _, wide = iotas((256, 128))
-    for m in range(COLS):
+    _, _ = iotas((256, 128))
+    for m in range(COLS):
+
+        def put(rows, lanes, x, m=m):
+            ah[m, rows, lanes], am[m, rows, lanes], al[m, rows, lanes] = split3(x)
+
         last = block[m, 0:NEAR]
-        w = mm(last[:, 0:NEAR], h[m, 256:OWN, 0:256])
+        w = mm(first_lanes(last), to_rows(h[m, 256:OWN, 0:256], 128))
         part = h[m, 0:256, 256:LANES]
-        out[m, 0:256, 0:256] = h[m, 0:256, 0:256] - mm(part[:, 0:NEAR], w)
-        out[m, 0:256, 256:LANES] = jnp.where(wide < NEAR, 0.0, part) - mm(part[:, 0:NEAR], last)
-        out[m, 256:OWN, 0:256] = w
-        out[m, 256:OWN, 256:LANES] = last
-
-
-def fit_own(everyone, proj0, proj1):
+        lead = first_lanes(part)
+        top, low = slice(0, 256), slice(256, OWN)
+        left, right = slice(0, 256), slice(256, LANES)
+        put(top, left, h[m, 0:256, 0:256] - mm(lead, to_rows(w, 128)))
+        end = (part - lead) - mm(lead, to_rows(last, 128))
+        put(top, right, end)
+        tail[m, top] = end
+        put(low, left, w)
+        put(low, right, last)
+        tail[m, low] = last
+
+
+def fit_own(gnorm, mid):
+    thirds = [pltpu.VMEM((COLS, OWN + R, K), BF)] * 3 + [pltpu.VMEM((COLS, OWN, LANES), BF)] * 3
     return pl.pallas_call(
         own_kernel,
-        out_shape=[
-            pltpu.VMEM((COLS, OWN, LANES), F32),
-            pltpu.VMEM((COLS, R, K), F32),
-            pltpu.VMEM((8, 128), F32),
-        ],
+        out_shape=thirds + [pltpu.VMEM((COLS, OWN, 128), F32)],
         scratch_shapes=[
             pltpu.VMEM((COLS, 2 * R, K), F32),
-            pltpu.VMEM((COLS, OWN + R, K), BF),
-            pltpu.VMEM((COLS, OWN + R, K), BF),
-            pltpu.VMEM((COLS, OWN + R, K), BF),
             pltpu.VMEM((COLS, OWN, LANES), F32),
             pltpu.VMEM((COLS, 128, 128), F32),
         ],
         compiler_params=pltpu.CompilerParams(vmem_limit_bytes=ROOM),
         name="fit_own",
-    )(*on_chip(everyone, proj0, proj1))
-
-
-def near_kernel(adjacency, scales, own, mid, up, down, solved, out, twice, fh, fm, fl, near, block, x, order, sems):
+    )(*on_chip(gnorm, mid))
+
+
+def near_kernel(
+    adjacency, gnorm, mid, up, down, fh, fm, fl, ah, am, al, tail, out, own, links, patch, block, x, order, sem
+):
+    fetch = pltpu.make_async_copy(adjacency, links, sem)
+    fetch.start()
     row0 = lax.axis_index("gx_0") * 4 + lax.axis_index("gx_1")
     col0 = (lax.axis_index("gy_0") * 2 + lax.axis_index("gy_1")) * COLS
-    for m in range(COLS):
-        for b in range(NB):
-            link = adjacency[0, m, b]
-            row = (link >> 4) - row0 + 1
-            col = (link & 15) - col0 + 1
-            slot = m * NB + b
-            for r, source in enumerate((up, mid, down)):
-
-                @pl.when(row == r)
-                def _():
-                    pltpu.make_async_copy(source.at[col], near.at[slot], sems.at[slot]).start()
-
     keep = past_mask()
-    lin, _ = ridge(scales[NVAR : NVAR + 1, :])
-    inv = [scales[v : v + 1, 0:1] for v in range(NVAR)]
+    lin, _ = ridge(gnorm[0:1])
     sub, lane = iotas((8, 128))
-    for m in range(COLS):
-
-        def put(at, v, m=m):
-            n = v.shape[0]
-            fh[m, at : at + n], fm[m, at : at + n], fl[m, at : at + n] = split3(v)
-
-        own_features(put, twice, m, own[m], keep)
+    for c in range(4):
+        for r, source in enumerate((up, mid, down)):
+            patch[4 * r + c] = jnp.where(keep, source[c], 0.0)
+    own[0] = mid[1]
+    own[1] = mid[2]
+    gap = jnp.zeros((128 - NEAR, K), F32)
+    fetch.wait()
     for m in range(COLS):
         rows = []
         for b in range(NB):
-            slot = m * NB + b
-            pltpu.make_async_copy(mid.at[0], near.at[slot], sems.at[slot]).wait()
-            rows.append(jnp.where(keep, scaled_sum(near.at[slot], inv), 0.0))
-        nh, nm, nl = split3(jnp.concatenate(rows, axis=0))
-        thirds = jnp.concatenate([nh, nm, nl], axis=0)
-        p = nt(fh[m], thirds)
-        q = nt(fm[m], thirds[0 : 2 * NEAR])
-        g = (p[:, 2 * NEAR : 3 * NEAR] + q[:, NEAR : 2 * NEAR] + nt(fl[m], nh)) + (p[:, NEAR : 2 * NEAR] + q[:, 0:NEAR])
-        cross = g + p[:, 0:NEAR]
-        p = nt(nh, thirds)
-        q = nt(nm, thirds[0 : 2 * NEAR])
-        g = (p[:, 2 * NEAR : 3 * NEAR] + q[:, NEAR : 2 * NEAR] + nt(nl, nh)) + (p[:, NEAR : 2 * NEAR] + q[:, 0:NEAR])
-        square = g + p[:, 0:NEAR]
-        wide = jnp.concatenate([cross, jnp.zeros((LANES - OWN - R, NEAR), F32)], axis=0)
-        wide = jnp.concatenate([wide, jnp.zeros((LANES, 128 - NEAR), F32)], axis=1)
-        turned = wide.T[0:NEAR]
-        z = mm(solved[m, :, 0:256], cross[0:256]) + mm(solved[m, :, 256:OWN], cross[256:OWN])
-        tail = solved[m, :, 256:LANES]
-        _, lane_o = iotas((OWN, 128))
-        z = jnp.concatenate([z, jnp.zeros((OWN, 128 - NEAR), F32)], axis=1)
-        both = jnp.where(lane_o < NEAR, z, tail)
+            link = links[0, m, b]
+            rows.append(patch[((link >> 4) - row0 + 1) * 4 + ((link & 15) - col0 + 1)])
+        nh, nm, nl = split3(jnp.concatenate(rows + [gap], axis=0))
+        pair = jnp.concatenate([nh, nm], axis=0)
+        a = [jnp.concatenate([f[m], n[0:80]], axis=0) for f, n in ((fh, nh), (fm, nm), (fl, nl))]
+        p = nt(a[0], pair)
+        q = nt(a[1], pair)
+        r = nt(a[0], nl) + nt(a[2], nh)
+        cross = p[:, 0:128] + ((p[:, 128:256] + q[:, 0:128]) + (q[:, 128:256] + r))
+        turned = to_rows(cross[0 : OWN + R], LANES).T[0:NEAR]
+        z = mm_thirds([t[m] for t in (ah, am, al)], to_rows(cross[0:OWN], LANES))
+        both = jnp.where(iotas((OWN, 128))[1] < NEAR, z, tail[m])
         x[m, 0:OWN] = both
         _, lane_n = iotas((NEAR, 128))
-        square = jnp.concatenate([square, jnp.zeros((NEAR, 128 - NEAR), F32)], axis=1)
-        start = jnp.where(lane_n < NEAR, square, turned[:, 256:LANES])
+        start = jnp.where(lane_n < NEAR, cross[OWN + R : OWN + R + NEAR], turned[:, 256:LANES])
         start = jnp.where(lane_n < NEAR + R, start, 0.0)
-        for i in range(NEAR // 8):
-            rows8 = slice(8 * i, 8 * i + 8)
-            block[m, rows8] = start[rows8] + jnp.where(lane == sub + 8 * i, lin, 0.0)
-        block[m, 0:NEAR] = block[m, 0:NEAR] - mm(turned[:, 0:OWN], both)
+        start = jnp.concatenate(
+            [start[8 * i : 8 * i + 8] + jnp.where(lane == sub + 8 * i, lin, 0.0) for i in range(NEAR // 8)], axis=0
+        )
+        turned = jnp.where(iotas((NEAR, LANES))[1] < OWN, turned, 0.0)
+        block[m, 0:NEAR] = start - mm_thirds(split3(turned), to_rows(both, LANES))
     for _ in invert(block, 9):
         pass
     for m in range(COLS):
         last = block[m, 0:NEAR]
         both = x[m, 0:OWN]
-        x[m, 0:OWN] = both - mm(both[:, 0:NEAR], last)
-        x[m, OWN : OWN + NEAR] = last
+        x[m, 0:OWN] = both - mm(first_lanes(both), to_rows(last, 128))
         order[m, 0:1] = x[m, MIXED + 12 : MIXED + 13]
         order[m, 1:25] = x[m, NQ : NQ + R]
         order[m, 25:97] = last
@@ -506,28 +534,27 @@
         out[m] = flat[NEAR : NEAR + R, 0:NF]
 
 
-def fit_near(adjacency, scales, own, mid, up, down, solved):
+def fit_near(adjacency, *rest):
     vm = pl.BlockSpec(memory_space=pltpu.VMEM)
-    far = pl.BlockSpec(memory_space=pl.ANY)
     return pl.pallas_call(
         near_kernel,
-        in_specs=[pl.BlockSpec(memory_space=pltpu.SMEM), vm, vm, far, far, far, vm],
-        out_specs=vm,
-        out_shape=jax.ShapeDtypeStruct((COLS, R, NF), F32),
+        in_specs=[pl.BlockSpec(memory_space=pl.ANY)] + [vm] * len(rest),
+        out_specs=[vm, vm],
+        out_shape=[
+            jax.ShapeDtypeStruct((COLS, R, NF), F32),
+            jax.ShapeDtypeStruct((COLS, R, K), F32),
+        ],
         scratch_shapes=[
-            pltpu.VMEM((COLS, 2 * R, K), F32),
-            pltpu.VMEM((COLS, OWN + R, K), BF),
-            pltpu.VMEM((COLS, OWN + R, K), BF),
-            pltpu.VMEM((COLS, OWN + R, K), BF),
-            pltpu.VMEM((COLS * NB, NVAR, R, K), F32),
+            pltpu.SMEM((1, COLS, NB), jnp.int32),
+            pltpu.VMEM((12, R, K), F32),
             pltpu.VMEM((COLS, 128, 128), F32),
-            pltpu.VMEM((COLS, OWN + NEAR, 128), F32),
+            pltpu.VMEM((COLS, OWN, 128), F32),
             pltpu.VMEM((COLS, 512, 128), F32),
-            pltpu.SemaphoreType.DMA((COLS * NB,)),
+            pltpu.SemaphoreType.DMA,
         ],
         compiler_params=pltpu.CompilerParams(vmem_limit_bytes=ROOM),
         name="fit_near",
-    )(pltpu.with_memory_space_constraint(adjacency, pltpu.HBM), *on_chip(scales, own, mid, up, down, solved))
+    )(pltpu.with_memory_space_constraint(adjacency, pltpu.HBM), *on_chip(*rest))
 
 
 def shifts(axis, x, y):
@@ -542,10 +569,10 @@
     proj0, proj1, stats = local_pass(snapshots[0], basis[0], node_counts)
     everyone = lax.all_to_all(stats, GX_GY, 0, 0, tiled=True)
     left, right = shifts(GY, proj1, proj0)
-    mid = jnp.stack([left, proj0, proj1, right])
+    mid, gnorm = global_states(everyone, left, proj0, proj1, right)
     up, down = shifts(GX, mid, mid)
-    solved, own, scales = fit_own(everyone, proj0, proj1)
-    operator = fit_near(adjacency, scales, own, mid, up, down, solved)
+    parts = fit_own(gnorm, mid)
+    operator, own = fit_near(adjacency, gnorm, mid, up, down, *parts)
     return (jnp.swapaxes(operator, 1, 2)[None], own[None])
 
 

time: 73.5 us -> 64.1 us (0.87); the launches traced: 72.3 us -> 63.9 us
  Pallas kernels: 35.2 us -> 31.3 us
  waiting for transfers between devices: 2.6 us -> 0.01 us
  blocking collectives: 21.7 us -> 20 us
    pallas_call x2 -> x3, Pallas kernels: 26.7 us -> 22.8 us  [the longest x1 14 us: fit_own(): pl.pallas_call(own_kernel, out_shape=thirds + [pltpu.VMEM((COLS, OWN, 128...]
    ppermute x2, starting transfers between devices: 6.72 us -> 8.5 us  [shifts(): lax.ppermute(x, axis, [(i, i + 1) for i in range(n - 1)])]
    all_to_all x1, blocking collectives: 21.7 us -> 20 us  [body(): everyone = lax.all_to_all(stats, GX_GY, 0, 0, tiled=True)]
    ppermute x2, waiting for transfers between devices: 1.41 us -> 0.01 us  [shifts(): lax.ppermute(y, axis, [(i + 1, i) for i in range(n - 1)])]
    ppermute x2, starting transfers between devices: 4.58 us -> 3.21 us  [shifts(): lax.ppermute(y, axis, [(i + 1, i) for i in range(n - 1)])]
    ppermute x2, waiting for transfers between devices: 1.18 us -> 0.01 us  [shifts(): lax.ppermute(x, axis, [(i, i + 1) for i in range(n - 1)])]
  transfers between devices with their start and end apart: 4 -> 4, of which waited for: 2 -> 0; matrix products, arithmetic and copies ran while one was open for 1% -> 0% of each run, Pallas kernels for 21% -> 22%
where the time goes in v5:
time: 64.1 us; the launch traced here: 63.9 us
  Pallas kernels  31.3 us (49%)
  blocking collectives  20 us (31%)
  starting transfers between devices  11.7 us (18%)
  between operations  0.86 us (1%)
    all_to_all x1, blocking collectives, body(): everyone = lax.all_to_all(stats, GX_GY, 0, 0, tiled=True)  20 us
    pallas_call x1, Pallas kernels, fit_own(): pl.pallas_call(own_kernel, out_shape=thirds + [pltpu.VMEM((COLS, OWN, 128...  14 us
    pallas_call x1, Pallas kernels, local_pass(): pl.pallas_call(local_kernel, in_specs=[pl.BlockSpec(memory_space=pltpu.SM...  8.51 us
    ppermute x2, starting transfers between devices, shifts(): lax.ppermute(x, axis, [(i, i + 1) for i in range(n - 1)])  8.5 us
    pallas_call x1, Pallas kernels, fit_near(): pl.pallas_call(near_kernel, in_specs=[pl.BlockSpec(memory_space=pl.ANY)]...  8.33 us
    ppermute x2, starting transfers between devices, shifts(): lax.ppermute(y, axis, [(i + 1, i) for i in range(n - 1)])  3.21 us
  transfers between devices with their start and end apart: 4, of which 0 were waited for; matrix products, arithmetic and copies ran while one was open for 0% of the time, Pallas kernels for 22%

profile of v5, /device:TPU:1, one launch (start us, length us, event | category | flops | bytes accessed | tf_op | source)
XLA Modules:
  0.0 63.9 jit_solution(8774435674658849431)
XLA Ops:
  0.6 8.5 %local.1 = (f32[4,24,512]{2,1,0:T(8,128)S(1)}, f32[4,24,512]{2,1,0:T(8,128)S(1)}, f32[128,128]{1,0:T(8,128)S(1)}) custom-call(s32[1,2]{1,0:T(1,128)} %counts.1, bf16[2,4,24,2048]{3,2,1,0:T(8,128)(2,1)} %bitcast.13, bf16[2,4,2048,512]{3,2,1,0:T(8,128)(2,1)} %bitcast.12), custom_call_target="tpu_custom_call" | custom-call | tf_op jit(solution)/shard_map/local/pallas_call | solution.py:111
  9.1 4.5 %collective-permute-start = (f32[4,24,512]{2,1,0:T(8,128)S(1)}, f32[4,24,512]{2,1,0:T(8,128)S(1)}, u32[]{:S(2)}, u32[]{:S(2)}) collective-permute-start(f32[4,24,512]{2,1,0:T(8,128)S(1)} %get-tuple-element.17.proj1), channel_id=1, source_target_pairs={{0,1},{1,2},{2,3},{3,4},{4,5},{5,6},{6,7},{8,9},{9,10},{10,11},{11... | collective-permute-start | bytes 589832 | tf_op jit(solution)/shard_map/ppermute | solution.py:563
  13.7 1.9 %collective-permute-start.1 = (f32[4,24,512]{2,1,0:T(8,128)S(1)}, f32[4,24,512]{2,1,0:T(8,128)S(1)}, u32[]{:S(2)}, u32[]{:S(2)}) collective-permute-start(f32[4,24,512]{2,1,0:T(8,128)S(1)} %get-tuple-element.18.proj0), channel_id=1, source_target_pairs={{1,0},{2,1},{3,2},{4,3},{5,4},{6,5},{7,6},{9,8},{10,9},{11,10},{12... | collective-permute-start | bytes 589832 | tf_op jit(solution)/shard_map/ppermute | solution.py:564
  15.6 20.0 %all_to_all.11 = f32[128,1,128]{2,1,0:T(1,128)S(1)} all-to-all(f32[128,1,128]{2,1,0:T(1,128)S(1)} %bitcast.11), channel_id=1, replica_groups=mesh['gx_0'=4,'gx_1'=4,'gy_0'=4,'gy_1'=2] {'gx_0','gx_1','gy_0','gy_1'}, dimensions={0} | all-to-all | bytes 131072 | tf_op jit(solution)/shard_map/all_to_all | solution.py:570
  35.5 0.0 collective-permute-done.left
  35.5 0.0 collective-permute-done.1.right
  35.6 0.4 states.1
  36.0 1.3 %collective-permute-start.3 = (f32[4,24,512]{2,1,0:T(8,128)S(1)}, f32[4,24,512]{2,1,0:T(8,128)S(1)}, u32[]{:S(2)}, u32[]{:S(2)}) collective-permute-start(f32[4,24,512]{2,1,0:T(8,128)S(1)} %get-tuple-element.20.mid), channel_id=1, source_target_pairs={{8,0},{16,8},{24,16},{32,24},{40,32},{48,40},{56,48},{64,56},{72,6... | collective-permute-start | bytes 589832 | tf_op jit(solution)/shard_map/ppermute | solution.py:564
  37.3 4.0 %collective-permute-start.2 = (f32[4,24,512]{2,1,0:T(8,128)S(1)}, f32[4,24,512]{2,1,0:T(8,128)S(1)}, u32[]{:S(2)}, u32[]{:S(2)}) collective-permute-start(f32[4,24,512]{2,1,0:T(8,128)S(1)} %get-tuple-element.20.mid), channel_id=1, source_target_pairs={{0,8},{8,16},{16,24},{24,32},{32,40},{40,48},{48,56},{56,64},{64,7... | collective-permute-start | bytes 589832 | tf_op jit(solution)/shard_map/ppermute | solution.py:563
  41.3 14.0 %fit_own.1 = (bf16[2,352,512]{2,1,0:T(8,128)(2,1)S(1)}, bf16[2,352,512]{2,1,0:T(8,128)(2,1)S(1)}, bf16[2,352,512]{2,1,0:T(8,128)(2,1)S(1)}, bf16[2,328,384]{2,1,...) custom-call(f32[8,128]{1,0:T(8,128)S(1)} %get-tuple-element.19.gnorm, ...), custom_call_target="tpu_custom_call" | custom-call | tf_op jit(solution)/shard_map/fit_own/pallas_call | solution.py:458
  55.3 0.0 collective-permute-done.3.down
  55.4 0.0 collective-permute-done.2.up
  55.4 8.3 %fit_near.1 = (f32[2,24,397]{2,1,0:T(8,128)}, f32[2,24,512]{2,1,0:T(8,128)}) custom-call(s32[1,2,3]{2,1,0:T(2,128)} %adjacency.1, f32[8,128]{1,0:T(8,128)S(1)} %get-tuple-element.19.gnorm, f32[4,24,512]{2,1,0:T(8,128)S(1)} %get-tuple-element.20.mid, f32[4,24,512]{2,1,0:T(8,128)S(1)} %collective-permute-done.2.up, ...), custom_call_target="tpu_custom_call" | custom-call | tf_op jit(solution)/shard_map/fit_near/pallas_call | solution.py:539
Async XLA Ops:
  9.1 26.4 %collective-permute-start = (f32[4,24,512]{2,1,0:T(8,128)S(1)}, f32[4,24,512]{2,1,0:T(8,128)S(1)}, u32[]{:S(2)}, u32[]{:S(2)}) collective-permute-start(f32[4,24,512]{2,1,0:T(8,128)S(1)} %get-tuple-element.17.proj1), channel_id=1, source_target_pairs={{0,1},{1,2},{2,3},{3,4},{4,5},{5,6},{6,7},{8,9},{9,10},{10,11},{11... | collective-permute-start | bytes 589832 | tf_op jit(solution)/shard_map/ppermute | solution.py:563
  13.7 21.9 %collective-permute-start.1 = (f32[4,24,512]{2,1,0:T(8,128)S(1)}, f32[4,24,512]{2,1,0:T(8,128)S(1)}, u32[]{:S(2)}, u32[]{:S(2)}) collective-permute-start(f32[4,24,512]{2,1,0:T(8,128)S(1)} %get-tuple-element.18.proj0), channel_id=1, source_target_pairs={{1,0},{2,1},{3,2},{4,3},{5,4},{6,5},{7,6},{9,8},{10,9},{11,10},{12... | collective-permute-start | bytes 589832 | tf_op jit(solution)/shard_map/ppermute | solution.py:564
  36.0 19.4 %collective-permute-start.3 = (f32[4,24,512]{2,1,0:T(8,128)S(1)}, f32[4,24,512]{2,1,0:T(8,128)S(1)}, u32[]{:S(2)}, u32[]{:S(2)}) collective-permute-start(f32[4,24,512]{2,1,0:T(8,128)S(1)} %get-tuple-element.20.mid), channel_id=1, source_target_pairs={{8,0},{16,8},{24,16},{32,24},{40,32},{48,40},{56,48},{64,56},{72,6... | collective-permute-start | bytes 589832 | tf_op jit(solution)/shard_map/ppermute | solution.py:564
  37.3 18.1 %collective-permute-start.2 = (f32[4,24,512]{2,1,0:T(8,128)S(1)}, f32[4,24,512]{2,1,0:T(8,128)S(1)}, u32[]{:S(2)}, u32[]{:S(2)}) collective-permute-start(f32[4,24,512]{2,1,0:T(8,128)S(1)} %get-tuple-element.20.mid), channel_id=1, source_target_pairs={{0,8},{8,16},{16,24},{24,32},{32,40},{40,48},{48,56},{56,64},{64,7... | collective-permute-start | bytes 589832 | tf_op jit(solution)/shard_map/ppermute | solution.py:563

commit v6 on v5

--- a/solution.py
+++ b/solution.py
@@ -219,7 +219,7 @@
     return [x * recips for x in riders]
 
 
-def invert(block, tiles, strip=4, look=1):
+def invert(block, tiles, strip=2, look=1):
     sub, lane = iotas((8, 128))
     for s in range(0, tiles, strip):
         own = list(range(s, min(s + strip, tiles)))
@@ -345,11 +345,27 @@
     lin, quad = ridge(gnorm[0:1])
     sub, lane = iotas((8, 128))
 
+    def thirds(m, lo, hi):
+        return [f[m, lo:hi] for f in (fh, fm, fl)]
+
     def gram(m, r0, r1, c0, c1):
-        a = [f[m, r0:r1] for f in (fh, fm, fl)]
-        b = [f[m, c0:c1] for f in (fh, fm, fl)]
-        g = ((nt(a[1], b[1]) + nt(a[0], b[2])) + nt(a[2], b[0])) + (nt(a[0], b[1]) + nt(a[1], b[0]))
-        return g + nt(a[0], b[0])
+        want = r1 - r0
+        size = -(-want // 16) * 16
+        a, b = thirds(m, r0, r0 + size), thirds(m, c0, c1)
+        n = c1 - c0
+        top, mid, low = slice(0, size), slice(size, 2 * size), slice(2 * size, 3 * size)
+        if n > 128:
+            x = nt(jnp.concatenate(a, axis=0), b[0])
+            y = nt(jnp.concatenate(a[:2], axis=0), b[1])
+            g = (((y[mid] + nt(a[0], b[2])) + x[low]) + (y[top] + x[mid])) + x[top]
+            return g[0:want]
+        gap = [jnp.zeros((128 - n, K), BF)] * (n < 128)
+        pair = jnp.concatenate([b[0]] + gap + [b[1]] + gap, axis=0)
+        p = nt(jnp.concatenate(a[:2], axis=0), pair)
+        r = nt(a[0], b[2]) + nt(a[2], b[0])
+        one, two = slice(0, n), slice(128, 128 + n)
+        g = p[top, one] + ((p[top, two] + p[mid, one]) + (p[mid, two] + r))
+        return g[0:want]
 
     def reg(row):
         if row < NQ or row == MIXED:
@@ -370,22 +386,22 @@
     def piece(m, kind):
         def go():
             if kind == 0:
-                h[m, 0:128, 128:256] = gram(m, 0, 128, 128, 256)
+                h[m, 0:128, 256:LANES] = jnp.zeros((128, 128), F32)
+                h[m, 0:128, 128 : OWN + R] = gram(m, 0, 128, 128, OWN + R)
             elif kind == 1:
-                h[m, 128:OWN, 0:128] = gram(m, 128, OWN, 0, 128)
+                g = gram(m, 128, 256, 0, 256)
+                h[m, 128:256, 0:128] = g[:, 0:128]
+                h[m, 128:256, 128:256] = ridged(g[:, 128:256], 128)
             elif kind == 2:
-                h[m, 128:256, 128:256] = ridged(gram(m, 128, 256, 128, 256), 128)
-            elif kind == 3:
-                h[m, 256:OWN, 128:256] = gram(m, 256, OWN, 128, 256)
+                h[m, 256:OWN, 0:256] = gram(m, 256, OWN, 0, 256)
             else:
-                h[m, :, 256:LANES] = jnp.zeros((OWN, 128), F32)
-                h[m, 0:256, 256 : OWN + R] = gram(m, 0, 256, 256, OWN + R)
-                h[m, 256:OWN, 256 : OWN + R] = gram(m, 256, OWN, 256, OWN + R)
+                h[m, 128:OWN, 256:LANES] = jnp.zeros((OWN - 128, 128), F32)
+                h[m, 128:OWN, 256 : OWN + R] = gram(m, 128, OWN, 256, OWN + R)
                 h[m, 256:OWN, 256:LANES] = ridged(h[m, 256:OWN, 256:LANES], 256)
 
         return go
 
-    spread(invert(block, 16), 14, [piece(m, k) for k in range(5) for m in range(COLS)])
+    spread(invert(block, 16), 14, [piece(m, k) for k in range(4) for m in range(COLS)])
     inv0 = [block[m] for m in range(COLS)]
     for m in range(COLS):
         w = mm(inv0[m], h[m, 0:128, 128:256])
@@ -493,10 +509,11 @@
         nh, nm, nl = split3(jnp.concatenate(rows + [gap], axis=0))
         pair = jnp.concatenate([nh, nm], axis=0)
         a = [jnp.concatenate([f[m], n[0:80]], axis=0) for f, n in ((fh, nh), (fm, nm), (fl, nl))]
-        p = nt(a[0], pair)
-        q = nt(a[1], pair)
+        size = OWN + R + 80
+        p = nt(jnp.concatenate(a[:2], axis=0), pair)
         r = nt(a[0], nl) + nt(a[2], nh)
-        cross = p[:, 0:128] + ((p[:, 128:256] + q[:, 0:128]) + (q[:, 128:256] + r))
+        top, mid_rows = slice(0, size), slice(size, 2 * size)
+        cross = p[top, 0:128] + ((p[top, 128:256] + p[mid_rows, 0:128]) + (p[mid_rows, 128:256] + r))
         turned = to_rows(cross[0 : OWN + R], LANES).T[0:NEAR]
         z = mm_thirds([t[m] for t in (ah, am, al)], to_rows(cross[0:OWN], LANES))
         both = jnp.where(iotas((OWN, 128))[1] < NEAR, z, tail[m])

time: 64.1 us -> 61.5 us (0.959)
  Pallas kernels: 31.3 us -> 28.8 us
    pallas_call x1, Pallas kernels: 14 us -> 12.8 us  [fit_own(): pl.pallas_call(own_kernel, out_shape=thirds + [pltpu.VMEM((COLS, OWN, 128...]
    pallas_call x1, Pallas kernels: 8.33 us -> 7.1 us  [fit_near(): pl.pallas_call(near_kernel, in_specs=[pl.BlockSpec(memory_space=pl.ANY)]...]
  transfers between devices with their start and end apart: 4 -> 4, of which waited for: 0 -> 0; matrix products, arithmetic and copies ran while one was open for 0% -> 0% of each run, Pallas kernels for 22% -> 21%
where the time goes in v6:
time: 61.5 us; the launch traced here: 61.2 us
  Pallas kernels  28.8 us (47%)
  blocking collectives  20 us (33%)
  starting transfers between devices  11.7 us (19%)
  between operations  0.7 us (1%)
    all_to_all x1, blocking collectives, body(): everyone = lax.all_to_all(stats, GX_GY, 0, 0, tiled=True)  20 us
    pallas_call x1, Pallas kernels, fit_own(): pl.pallas_call(own_kernel, out_shape=thirds + [pltpu.VMEM((COLS, OWN, 128...  12.8 us
    pallas_call x1, Pallas kernels, local_pass(): pl.pallas_call(local_kernel, in_specs=[pl.BlockSpec(memory_space=pltpu.SM...  8.51 us
    ppermute x2, starting transfers between devices, shifts(): lax.ppermute(x, axis, [(i, i + 1) for i in range(n - 1)])  8.49 us
    pallas_call x1, Pallas kernels, fit_near(): pl.pallas_call(near_kernel, in_specs=[pl.BlockSpec(memory_space=pl.ANY)]...  7.1 us
    ppermute x2, starting transfers between devices, shifts(): lax.ppermute(y, axis, [(i + 1, i) for i in range(n - 1)])  3.21 us
  transfers between devices with their start and end apart: 4, of which 0 were waited for; matrix products, arithmetic and copies ran while one was open for 0% of the time, Pallas kernels for 21%

profile of v6, /device:TPU:1, one launch (start us, length us, event | category | flops | bytes accessed | tf_op | source)
XLA Modules:
  0.0 61.2 jit_solution(5511524059532293781)
XLA Ops:
  0.6 8.5 %local.1 = (f32[4,24,512]{2,1,0:T(8,128)S(1)}, f32[4,24,512]{2,1,0:T(8,128)S(1)}, f32[128,128]{1,0:T(8,128)S(1)}) custom-call(s32[1,2]{1,0:T(1,128)} %counts.1, bf16[2,4,24,2048]{3,2,1,0:T(8,128)(2,1)} %bitcast.13, bf16[2,4,2048,512]{3,2,1,0:T(8,128)(2,1)} %bitcast.12), custom_call_target="tpu_custom_call" | custom-call | tf_op jit(solution)/shard_map/local/pallas_call | solution.py:111
  9.1 4.5 %collective-permute-start = (f32[4,24,512]{2,1,0:T(8,128)S(1)}, f32[4,24,512]{2,1,0:T(8,128)S(1)}, u32[]{:S(2)}, u32[]{:S(2)}) collective-permute-start(f32[4,24,512]{2,1,0:T(8,128)S(1)} %get-tuple-element.17.proj1), channel_id=1, source_target_pairs={{0,1},{1,2},{2,3},{3,4},{4,5},{5,6},{6,7},{8,9},{9,10},{10,11},{11... | collective-permute-start | bytes 589832 | tf_op jit(solution)/shard_map/ppermute | solution.py:580
  13.7 1.9 %collective-permute-start.1 = (f32[4,24,512]{2,1,0:T(8,128)S(1)}, f32[4,24,512]{2,1,0:T(8,128)S(1)}, u32[]{:S(2)}, u32[]{:S(2)}) collective-permute-start(f32[4,24,512]{2,1,0:T(8,128)S(1)} %get-tuple-element.18.proj0), channel_id=1, source_target_pairs={{1,0},{2,1},{3,2},{4,3},{5,4},{6,5},{7,6},{9,8},{10,9},{11,10},{12... | collective-permute-start | bytes 589832 | tf_op jit(solution)/shard_map/ppermute | solution.py:581
  15.6 20.0 %all_to_all.11 = f32[128,1,128]{2,1,0:T(1,128)S(1)} all-to-all(f32[128,1,128]{2,1,0:T(1,128)S(1)} %bitcast.11), channel_id=1, replica_groups=mesh['gx_0'=4,'gx_1'=4,'gy_0'=4,'gy_1'=2] {'gx_0','gx_1','gy_0','gy_1'}, dimensions={0} | all-to-all | bytes 131072 | tf_op jit(solution)/shard_map/all_to_all | solution.py:587
  35.5 0.0 collective-permute-done.left
  35.5 0.0 collective-permute-done.1.right
  35.6 0.4 states.1
  36.0 1.3 %collective-permute-start.3 = (f32[4,24,512]{2,1,0:T(8,128)S(1)}, f32[4,24,512]{2,1,0:T(8,128)S(1)}, u32[]{:S(2)}, u32[]{:S(2)}) collective-permute-start(f32[4,24,512]{2,1,0:T(8,128)S(1)} %get-tuple-element.20.mid), channel_id=1, source_target_pairs={{8,0},{16,8},{24,16},{32,24},{40,32},{48,40},{56,48},{64,56},{72,6... | collective-permute-start | bytes 589832 | tf_op jit(solution)/shard_map/ppermute | solution.py:581
  37.3 4.0 %collective-permute-start.2 = (f32[4,24,512]{2,1,0:T(8,128)S(1)}, f32[4,24,512]{2,1,0:T(8,128)S(1)}, u32[]{:S(2)}, u32[]{:S(2)}) collective-permute-start(f32[4,24,512]{2,1,0:T(8,128)S(1)} %get-tuple-element.20.mid), channel_id=1, source_target_pairs={{0,8},{8,16},{16,24},{24,32},{32,40},{40,48},{48,56},{56,64},{64,7... | collective-permute-start | bytes 589832 | tf_op jit(solution)/shard_map/ppermute | solution.py:580
  41.3 12.8 %fit_own.1 = (bf16[2,352,512]{2,1,0:T(8,128)(2,1)S(1)}, bf16[2,352,512]{2,1,0:T(8,128)(2,1)S(1)}, bf16[2,352,512]{2,1,0:T(8,128)(2,1)S(1)}, bf16[2,328,384]{2,1,...) custom-call(f32[8,128]{1,0:T(8,128)S(1)} %get-tuple-element.19.gnorm, ...), custom_call_target="tpu_custom_call" | custom-call | tf_op jit(solution)/shard_map/fit_own/pallas_call | solution.py:474
  54.1 0.0 collective-permute-done.3.down
  54.1 0.0 collective-permute-done.2.up
  54.1 7.1 %fit_near.1 = (f32[2,24,397]{2,1,0:T(8,128)}, f32[2,24,512]{2,1,0:T(8,128)}) custom-call(s32[1,2,3]{2,1,0:T(2,128)} %adjacency.1, f32[8,128]{1,0:T(8,128)S(1)} %get-tuple-element.19.gnorm, f32[4,24,512]{2,1,0:T(8,128)S(1)} %get-tuple-element.20.mid, f32[4,24,512]{2,1,0:T(8,128)S(1)} %collective-permute-done.2.up, ...), custom_call_target="tpu_custom_call" | custom-call | tf_op jit(solution)/shard_map/fit_near/pallas_call | solution.py:556
Async XLA Ops:
  9.1 26.4 %collective-permute-start = (f32[4,24,512]{2,1,0:T(8,128)S(1)}, f32[4,24,512]{2,1,0:T(8,128)S(1)}, u32[]{:S(2)}, u32[]{:S(2)}) collective-permute-start(f32[4,24,512]{2,1,0:T(8,128)S(1)} %get-tuple-element.17.proj1), channel_id=1, source_target_pairs={{0,1},{1,2},{2,3},{3,4},{4,5},{5,6},{6,7},{8,9},{9,10},{10,11},{11... | collective-permute-start | bytes 589832 | tf_op jit(solution)/shard_map/ppermute | solution.py:580
  13.7 21.9 %collective-permute-start.1 = (f32[4,24,512]{2,1,0:T(8,128)S(1)}, f32[4,24,512]{2,1,0:T(8,128)S(1)}, u32[]{:S(2)}, u32[]{:S(2)}) collective-permute-start(f32[4,24,512]{2,1,0:T(8,128)S(1)} %get-tuple-element.18.proj0), channel_id=1, source_target_pairs={{1,0},{2,1},{3,2},{4,3},{5,4},{6,5},{7,6},{9,8},{10,9},{11,10},{12... | collective-permute-start | bytes 589832 | tf_op jit(solution)/shard_map/ppermute | solution.py:581
  36.0 18.1 %collective-permute-start.3 = (f32[4,24,512]{2,1,0:T(8,128)S(1)}, f32[4,24,512]{2,1,0:T(8,128)S(1)}, u32[]{:S(2)}, u32[]{:S(2)}) collective-permute-start(f32[4,24,512]{2,1,0:T(8,128)S(1)} %get-tuple-element.20.mid), channel_id=1, source_target_pairs={{8,0},{16,8},{24,16},{32,24},{40,32},{48,40},{56,48},{64,56},{72,6... | collective-permute-start | bytes 589832 | tf_op jit(solution)/shard_map/ppermute | solution.py:581
  37.3 16.8 %collective-permute-start.2 = (f32[4,24,512]{2,1,0:T(8,128)S(1)}, f32[4,24,512]{2,1,0:T(8,128)S(1)}, u32[]{:S(2)}, u32[]{:S(2)}) collective-permute-start(f32[4,24,512]{2,1,0:T(8,128)S(1)} %get-tuple-element.20.mid), channel_id=1, source_target_pairs={{0,8},{8,16},{16,24},{24,32},{32,40},{40,48},{48,56},{56,64},{64,7... | collective-permute-start | bytes 589832 | tf_op jit(solution)/shard_map/ppermute | solution.py:580

commit v7 on v6

--- a/solution.py
+++ b/solution.py
@@ -333,7 +333,7 @@
     return lax.dot_general(a, b, (((1,), (1,)), ((), ())), preferred_element_type=F32)
 
 
-def own_kernel(gnorm, mid, fh, fm, fl, ah, am, al, tail, twice, h, block):
+def own_kernel(gnorm, mid, fh, fm, fl, h, block, twice):
     keep = past_mask()
     for m in range(COLS):
 
@@ -426,11 +426,51 @@
         return go
 
     spread(invert(block, 16), 14, [after0(m, k) for k in range(4) for m in range(COLS)])
+
+
+def fit_own(gnorm, mid):
+    return pl.pallas_call(
+        own_kernel,
+        out_shape=[pltpu.VMEM((COLS, OWN + R, K), BF)] * 3
+        + [pltpu.VMEM((COLS, OWN, LANES), F32), pltpu.VMEM((COLS, 128, 128), F32)],
+        scratch_shapes=[pltpu.VMEM((COLS, 2 * R, K), F32)],
+        compiler_params=pltpu.CompilerParams(vmem_limit_bytes=ROOM),
+        name="fit_own",
+    )(*on_chip(gnorm, mid))
+
+
+def near_kernel(
+    adjacency, gnorm, mid, up, down, fh, fm, fl, h_in, block_in, out, own,
+    links, patch, h, block, nb, cross, turned, x, order, sem,
+):
+    fetch = pltpu.make_async_copy(adjacency, links, sem)
+    fetch.start()
+    row0 = lax.axis_index("gx_0") * 4 + lax.axis_index("gx_1")
+    col0 = (lax.axis_index("gy_0") * 2 + lax.axis_index("gy_1")) * COLS
+    keep = past_mask()
+    lin, _ = ridge(gnorm[0:1])
+    sub, lane = iotas((8, 128))
     for m in range(COLS):
-        h[m, 128:256, 128:256] = block[m]
-        w = mm(block[m], h[m, 128:256, 256:LANES])
-        block[m, 0:NEAR] = h[m, 256:OWN, 256:LANES] - mm(h[m, 256:OWN, 128:256], w)
+        w = mm(block_in[m], h_in[m, 128:256, 256:LANES])
+        block[m, 0:NEAR] = h_in[m, 256:OWN, 256:LANES] - mm(h_in[m, 256:OWN, 128:256], w)
         h[m, 128:256, 256:LANES] = w
+        h[m, 128:256, 128:256] = block_in[m]
+        h[m, 128:256, 0:128] = h_in[m, 128:256, 0:128]
+        h[m, 0:128] = h_in[m, 0:128]
+        h[m, 256:OWN] = h_in[m, 256:OWN]
+    for c in range(4):
+        for r, source in enumerate((up, mid, down)):
+            patch[4 * r + c] = jnp.where(keep, source[c], 0.0)
+    own[0] = mid[1]
+    own[1] = mid[2]
+    gap = jnp.zeros((128 - NEAR, K), F32)
+    fetch.wait()
+    for m in range(COLS):
+        rows = []
+        for b in range(NB):
+            link = links[0, m, b]
+            rows.append(patch[((link >> 4) - row0 + 1) * 4 + ((link & 15) - col0 + 1)])
+        nb[m, 0:128], nb[m, 128:256], nb[m, 256:384] = split3(jnp.concatenate(rows + [gap], axis=0))
 
     def after1(m, kind):
         def go():
@@ -447,85 +487,62 @@
 
         return go
 
-    spread(invert(block, 9), 8, [after1(m, k) for k in range(4) for m in range(COLS)])
-    _, _ = iotas((256, 128))
+    def near_products(m, part):
+        def go():
+            nh, nm, nl = (nb[m, 128 * i : 128 * i + 128] for i in range(3))
+            if part == 0:
+                a = [f[m, 0:176] for f in (fh, fm, fl)]
+            else:
+                pieces = ((fh, nh), (fm, nm), (fl, nl))
+                a = [jnp.concatenate([f[m, 176 : OWN + R], n[0:80]], axis=0) for f, n in pieces]
+            size = a[0].shape[0]
+            p = nt(jnp.concatenate(a[:2], axis=0), nb[m, 0:256])
+            r = nt(a[0], nl) + nt(a[2], nh)
+            top, low = slice(0, size), slice(size, 2 * size)
+            g = p[top, 0:128] + ((p[top, 128:256] + p[low, 0:128]) + (p[low, 128:256] + r))
+            cross[m, 176 * part : 176 * part + size] = g
+
+        return go
+
+    def turn(m):
+        def go():
+            turned[m] = to_rows(cross[m, 0 : OWN + R], LANES).T[0:NEAR]
+
+        return go
+
+    def near_columns(m):
+        def go():
+            g = mm_thirds(split3(h[m, :, 0:256]), cross[m, 0:256])
+            x[m, 0:256] = g[0:256]
+            x[m, 256:OWN] = cross[m, 256:OWN] + g[256:OWN]
+
+        return go
+
+    work = []
+    for k in range(4):
+        for m in range(COLS):
+            work.append(after1(m, k))
+            if k < 2:
+                work.append(near_products(m, k))
+            else:
+                work.append(turn(m) if k == 2 else near_columns(m))
+    spread(invert(block, 9), 8, work)
+    _, wide = iotas((256, 128))
+    _, lane_n = iotas((NEAR, 128))
     for m in range(COLS):
-
-        def put(rows, lanes, x, m=m):
-            ah[m, rows, lanes], am[m, rows, lanes], al[m, rows, lanes] = split3(x)
-
         last = block[m, 0:NEAR]
-        w = mm(first_lanes(last), to_rows(h[m, 256:OWN, 0:256], 128))
+        low = jnp.where(lane_n < NEAR, mm(first_lanes(last), to_rows(x[m, 256:OWN], 128)), last)
         part = h[m, 0:256, 256:LANES]
-        lead = first_lanes(part)
-        top, low = slice(0, 256), slice(256, OWN)
-        left, right = slice(0, 256), slice(256, LANES)
-        put(top, left, h[m, 0:256, 0:256] - mm(lead, to_rows(w, 128)))
-        end = (part - lead) - mm(lead, to_rows(last, 128))
-        put(top, right, end)
-        tail[m, top] = end
-        put(low, left, w)
-        put(low, right, last)
-        tail[m, low] = last
-
-
-def fit_own(gnorm, mid):
-    thirds = [pltpu.VMEM((COLS, OWN + R, K), BF)] * 3 + [pltpu.VMEM((COLS, OWN, LANES), BF)] * 3
-    return pl.pallas_call(
-        own_kernel,
-        out_shape=thirds + [pltpu.VMEM((COLS, OWN, 128), F32)],
-        scratch_shapes=[
-            pltpu.VMEM((COLS, 2 * R, K), F32),
-            pltpu.VMEM((COLS, OWN, LANES), F32),
-            pltpu.VMEM((COLS, 128, 128), F32),
-        ],
-        compiler_params=pltpu.CompilerParams(vmem_limit_bytes=ROOM),
-        name="fit_own",
-    )(*on_chip(gnorm, mid))
-
-
-def near_kernel(
-    adjacency, gnorm, mid, up, down, fh, fm, fl, ah, am, al, tail, out, own, links, patch, block, x, order, sem
-):
-    fetch = pltpu.make_async_copy(adjacency, links, sem)
-    fetch.start()
-    row0 = lax.axis_index("gx_0") * 4 + lax.axis_index("gx_1")
-    col0 = (lax.axis_index("gy_0") * 2 + lax.axis_index("gy_1")) * COLS
-    keep = past_mask()
-    lin, _ = ridge(gnorm[0:1])
-    sub, lane = iotas((8, 128))
-    for c in range(4):
-        for r, source in enumerate((up, mid, down)):
-            patch[4 * r + c] = jnp.where(keep, source[c], 0.0)
-    own[0] = mid[1]
-    own[1] = mid[2]
-    gap = jnp.zeros((128 - NEAR, K), F32)
-    fetch.wait()
-    for m in range(COLS):
-        rows = []
-        for b in range(NB):
-            link = links[0, m, b]
-            rows.append(patch[((link >> 4) - row0 + 1) * 4 + ((link & 15) - col0 + 1)])
-        nh, nm, nl = split3(jnp.concatenate(rows + [gap], axis=0))
-        pair = jnp.concatenate([nh, nm], axis=0)
-        a = [jnp.concatenate([f[m], n[0:80]], axis=0) for f, n in ((fh, nh), (fm, nm), (fl, nl))]
-        size = OWN + R + 80
-        p = nt(jnp.concatenate(a[:2], axis=0), pair)
-        r = nt(a[0], nl) + nt(a[2], nh)
-        top, mid_rows = slice(0, size), slice(size, 2 * size)
-        cross = p[top, 0:128] + ((p[top, 128:256] + p[mid_rows, 0:128]) + (p[mid_rows, 128:256] + r))
-        turned = to_rows(cross[0 : OWN + R], LANES).T[0:NEAR]
-        z = mm_thirds([t[m] for t in (ah, am, al)], to_rows(cross[0:OWN], LANES))
-        both = jnp.where(iotas((OWN, 128))[1] < NEAR, z, tail[m])
-        x[m, 0:OWN] = both
-        _, lane_n = iotas((NEAR, 128))
-        start = jnp.where(lane_n < NEAR, cross[OWN + R : OWN + R + NEAR], turned[:, 256:LANES])
+        top = jnp.where(wide < NEAR, x[m, 0:256], part) - mm(first_lanes(part), to_rows(low, 128))
+        both = jnp.concatenate([top, low], axis=0)
+        x[m] = both
+        start = jnp.where(lane_n < NEAR, cross[m, OWN + R : OWN + R + NEAR], turned[m, :, 256:LANES])
         start = jnp.where(lane_n < NEAR + R, start, 0.0)
         start = jnp.concatenate(
             [start[8 * i : 8 * i + 8] + jnp.where(lane == sub + 8 * i, lin, 0.0) for i in range(NEAR // 8)], axis=0
         )
-        turned = jnp.where(iotas((NEAR, LANES))[1] < OWN, turned, 0.0)
-        block[m, 0:NEAR] = start - mm_thirds(split3(turned), to_rows(both, LANES))
+        flat = jnp.where(iotas((NEAR, LANES))[1] < OWN, turned[m], 0.0)
+        block[m, 0:NEAR] = start - mm_thirds(split3(flat), to_rows(both, LANES))
     for _ in invert(block, 9):
         pass
     for m in range(COLS):
@@ -564,7 +581,11 @@
         scratch_shapes=[
             pltpu.SMEM((1, COLS, NB), jnp.int32),
             pltpu.VMEM((12, R, K), F32),
+            pltpu.VMEM((COLS, OWN, LANES), F32),
             pltpu.VMEM((COLS, 128, 128), F32),
+            pltpu.VMEM((COLS, 384, K), BF),
+            pltpu.VMEM((COLS, OWN + R + 80, 128), F32),
+            pltpu.VMEM((COLS, NEAR, LANES), F32),
             pltpu.VMEM((COLS, OWN, 128), F32),
             pltpu.VMEM((COLS, 512, 128), F32),
             pltpu.SemaphoreType.DMA,

time: 61.5 us -> 57.8 us (0.940)
  Pallas kernels: 28.8 us -> 25.1 us
    pallas_call x1, Pallas kernels: 12.8 us -> 8.43 us  [fit_own(): pl.pallas_call(own_kernel, out_shape=[pltpu.VMEM((COLS, OWN + R, K), BF)]...]
    pallas_call x1, Pallas kernels: 7.1 us -> 7.78 us  [fit_near(): pl.pallas_call(near_kernel, in_specs=[pl.BlockSpec(memory_space=pl.ANY)]...]
  transfers between devices with their start and end apart: 4 -> 4, of which waited for: 0 -> 0; matrix products, arithmetic and copies ran while one was open for 0% -> 0% of each run, Pallas kernels for 21% -> 15%
where the time goes in v7:
time: 57.8 us; the launch traced here: 57.5 us
  Pallas kernels  25.1 us (43%)
  blocking collectives  20 us (35%)
  starting transfers between devices  11.7 us (20%)
  between operations  0.7 us (1%)
    all_to_all x1, blocking collectives, body(): everyone = lax.all_to_all(stats, GX_GY, 0, 0, tiled=True)  20 us
    pallas_call x1, Pallas kernels, local_pass(): pl.pallas_call(local_kernel, in_specs=[pl.BlockSpec(memory_space=pltpu.SM...  8.51 us
    ppermute x2, starting transfers between devices, shifts(): lax.ppermute(x, axis, [(i, i + 1) for i in range(n - 1)])  8.49 us
    pallas_call x1, Pallas kernels, fit_own(): pl.pallas_call(own_kernel, out_shape=[pltpu.VMEM((COLS, OWN + R, K), BF)]...  8.43 us
    pallas_call x1, Pallas kernels, fit_near(): pl.pallas_call(near_kernel, in_specs=[pl.BlockSpec(memory_space=pl.ANY)]...  7.78 us
    ppermute x2, starting transfers between devices, shifts(): lax.ppermute(y, axis, [(i + 1, i) for i in range(n - 1)])  3.21 us
  transfers between devices with their start and end apart: 4, of which 0 were waited for; matrix products, arithmetic and copies ran while one was open for 0% of the time, Pallas kernels for 15%

profile of v7, /device:TPU:1, one launch (start us, length us, event | category | flops | bytes accessed | tf_op | source)
XLA Modules:
  0.0 57.5 jit_solution(83727630317416563)
XLA Ops:
  0.6 8.5 %local.1 = (f32[4,24,512]{2,1,0:T(8,128)S(1)}, f32[4,24,512]{2,1,0:T(8,128)S(1)}, f32[128,128]{1,0:T(8,128)S(1)}) custom-call(s32[1,2]{1,0:T(1,128)} %counts.1, bf16[2,4,24,2048]{3,2,1,0:T(8,128)(2,1)} %bitcast.13, bf16[2,4,2048,512]{3,2,1,0:T(8,128)(2,1)} %bitcast.12), custom_call_target="tpu_custom_call" | custom-call | tf_op jit(solution)/shard_map/local/pallas_call | solution.py:111
  9.1 4.5 %collective-permute-start = (f32[4,24,512]{2,1,0:T(8,128)S(1)}, f32[4,24,512]{2,1,0:T(8,128)S(1)}, u32[]{:S(2)}, u32[]{:S(2)}) collective-permute-start(f32[4,24,512]{2,1,0:T(8,128)S(1)} %get-tuple-element.15.proj1), channel_id=1, source_target_pairs={{0,1},{1,2},{2,3},{3,4},{4,5},{5,6},{6,7},{8,9},{9,10},{10,11},{11... | collective-permute-start | bytes 589832 | tf_op jit(solution)/shard_map/ppermute | solution.py:601
  13.7 1.9 %collective-permute-start.1 = (f32[4,24,512]{2,1,0:T(8,128)S(1)}, f32[4,24,512]{2,1,0:T(8,128)S(1)}, u32[]{:S(2)}, u32[]{:S(2)}) collective-permute-start(f32[4,24,512]{2,1,0:T(8,128)S(1)} %get-tuple-element.16.proj0), channel_id=1, source_target_pairs={{1,0},{2,1},{3,2},{4,3},{5,4},{6,5},{7,6},{9,8},{10,9},{11,10},{12... | collective-permute-start | bytes 589832 | tf_op jit(solution)/shard_map/ppermute | solution.py:602
  15.6 20.0 %all_to_all.11 = f32[128,1,128]{2,1,0:T(1,128)S(1)} all-to-all(f32[128,1,128]{2,1,0:T(1,128)S(1)} %bitcast.11), channel_id=1, replica_groups=mesh['gx_0'=4,'gx_1'=4,'gy_0'=4,'gy_1'=2] {'gx_0','gx_1','gy_0','gy_1'}, dimensions={0} | all-to-all | bytes 131072 | tf_op jit(solution)/shard_map/all_to_all | solution.py:608
  35.5 0.0 collective-permute-done.left
  35.5 0.0 collective-permute-done.1.right
  35.6 0.4 states.1
  36.0 1.3 %collective-permute-start.3 = (f32[4,24,512]{2,1,0:T(8,128)S(1)}, f32[4,24,512]{2,1,0:T(8,128)S(1)}, u32[]{:S(2)}, u32[]{:S(2)}) collective-permute-start(f32[4,24,512]{2,1,0:T(8,128)S(1)} %get-tuple-element.18.mid), channel_id=1, source_target_pairs={{8,0},{16,8},{24,16},{32,24},{40,32},{48,40},{56,48},{64,56},{72,6... | collective-permute-start | bytes 589832 | tf_op jit(solution)/shard_map/ppermute | solution.py:602
  37.3 4.0 %collective-permute-start.2 = (f32[4,24,512]{2,1,0:T(8,128)S(1)}, f32[4,24,512]{2,1,0:T(8,128)S(1)}, u32[]{:S(2)}, u32[]{:S(2)}) collective-permute-start(f32[4,24,512]{2,1,0:T(8,128)S(1)} %get-tuple-element.18.mid), channel_id=1, source_target_pairs={{0,8},{8,16},{16,24},{24,32},{32,40},{40,48},{48,56},{56,64},{64,7... | collective-permute-start | bytes 589832 | tf_op jit(solution)/shard_map/ppermute | solution.py:601
  41.3 8.4 %fit_own.1 = (bf16[2,352,512]{2,1,0:T(8,128)(2,1)S(1)}, bf16[2,352,512]{2,1,0:T(8,128)(2,1)S(1)}, bf16[2,352,512]{2,1,0:T(8,128)(2,1)S(1)}, f32[2,328,384]{2,1,0:T(8,128)S(1)}, f32[2,128,128]{2,1,0:T(8,128)S(1)}) custom-call(f32[8,128]{1,0:T(8,128)S(1)} %get-tuple-element.17.gnorm, f32[4,24,512]{2,1,0:T(8,128)S(1)} %get-tuple-element.18.mid), custom_call_target="tpu_custom_call" | custom-call | tf_op jit(solution)/shard_map/fit_own/pallas_call | solution.py:432
  49.7 0.0 collective-permute-done.3.down
  49.7 0.0 collective-permute-done.2.up
  49.7 7.8 %fit_near.1 = (f32[2,24,397]{2,1,0:T(8,128)}, f32[2,24,512]{2,1,0:T(8,128)}) custom-call(s32[1,2,3]{2,1,0:T(2,128)} %adjacency.1, f32[8,128]{1,0:T(8,128)S(1)} %get-tuple-element.17.gnorm, f32[4,24,512]{2,1,0:T(8,128)S(1)} %get-tuple-element.18.mid, f32[4,24,512]{2,1,0:T(8,128)S(1)} %collective-permute-done.2.up, ...), custom_call_target="tpu_custom_call" | custom-call | tf_op jit(solution)/shard_map/fit_near/pallas_call | solution.py:573
Async XLA Ops:
  9.1 26.4 %collective-permute-start = (f32[4,24,512]{2,1,0:T(8,128)S(1)}, f32[4,24,512]{2,1,0:T(8,128)S(1)}, u32[]{:S(2)}, u32[]{:S(2)}) collective-permute-start(f32[4,24,512]{2,1,0:T(8,128)S(1)} %get-tuple-element.15.proj1), channel_id=1, source_target_pairs={{0,1},{1,2},{2,3},{3,4},{4,5},{5,6},{6,7},{8,9},{9,10},{10,11},{11... | collective-permute-start | bytes 589832 | tf_op jit(solution)/shard_map/ppermute | solution.py:601
  13.7 21.9 %collective-permute-start.1 = (f32[4,24,512]{2,1,0:T(8,128)S(1)}, f32[4,24,512]{2,1,0:T(8,128)S(1)}, u32[]{:S(2)}, u32[]{:S(2)}) collective-permute-start(f32[4,24,512]{2,1,0:T(8,128)S(1)} %get-tuple-element.16.proj0), channel_id=1, source_target_pairs={{1,0},{2,1},{3,2},{4,3},{5,4},{6,5},{7,6},{9,8},{10,9},{11,10},{12... | collective-permute-start | bytes 589832 | tf_op jit(solution)/shard_map/ppermute | solution.py:602
  36.0 13.7 %collective-permute-start.3 = (f32[4,24,512]{2,1,0:T(8,128)S(1)}, f32[4,24,512]{2,1,0:T(8,128)S(1)}, u32[]{:S(2)}, u32[]{:S(2)}) collective-permute-start(f32[4,24,512]{2,1,0:T(8,128)S(1)} %get-tuple-element.18.mid), channel_id=1, source_target_pairs={{8,0},{16,8},{24,16},{32,24},{40,32},{48,40},{56,48},{64,56},{72,6... | collective-permute-start | bytes 589832 | tf_op jit(solution)/shard_map/ppermute | solution.py:602
  37.3 12.4 %collective-permute-start.2 = (f32[4,24,512]{2,1,0:T(8,128)S(1)}, f32[4,24,512]{2,1,0:T(8,128)S(1)}, u32[]{:S(2)}, u32[]{:S(2)}) collective-permute-start(f32[4,24,512]{2,1,0:T(8,128)S(1)} %get-tuple-element.18.mid), channel_id=1, source_target_pairs={{0,8},{8,16},{16,24},{24,32},{32,40},{40,48},{48,56},{56,64},{64,7... | collective-permute-start | bytes 589832 | tf_op jit(solution)/shard_map/ppermute | solution.py:601

commit v8 on v7

--- a/solution.py
+++ b/solution.py
@@ -389,11 +389,10 @@
                 h[m, 0:128, 256:LANES] = jnp.zeros((128, 128), F32)
                 h[m, 0:128, 128 : OWN + R] = gram(m, 0, 128, 128, OWN + R)
             elif kind == 1:
-                g = gram(m, 128, 256, 0, 256)
-                h[m, 128:256, 0:128] = g[:, 0:128]
-                h[m, 128:256, 128:256] = ridged(g[:, 128:256], 128)
-            elif kind == 2:
-                h[m, 256:OWN, 0:256] = gram(m, 256, OWN, 0, 256)
+                g = gram(m, 128, OWN, 0, 256)
+                h[m, 128:256, 0:128] = g[0:128, 0:128]
+                h[m, 128:256, 128:256] = ridged(g[0:128, 128:256], 128)
+                h[m, 256:OWN, 0:256] = g[128:]
             else:
                 h[m, 128:OWN, 256:LANES] = jnp.zeros((OWN - 128, 128), F32)
                 h[m, 128:OWN, 256 : OWN + R] = gram(m, 128, OWN, 256, OWN + R)
@@ -401,7 +400,7 @@
 
         return go
 
-    spread(invert(block, 16), 14, [piece(m, k) for k in range(4) for m in range(COLS)])
+    spread(invert(block, 16), 14, [piece(m, k) for k in range(2) for m in range(COLS)])
     inv0 = [block[m] for m in range(COLS)]
     for m in range(COLS):
         w = mm(inv0[m], h[m, 0:128, 128:256])
@@ -425,7 +424,8 @@
 
         return go
 
-    spread(invert(block, 16), 14, [after0(m, k) for k in range(4) for m in range(COLS)])
+    late = [piece(m, 2) for m in range(COLS)]
+    spread(invert(block, 16), 14, late + [after0(m, k) for k in range(4) for m in range(COLS)])
 
 
 def fit_own(gnorm, mid):
@@ -441,10 +441,12 @@
 
 def near_kernel(
     adjacency, gnorm, mid, up, down, fh, fm, fl, h_in, block_in, out, own,
-    links, patch, h, block, nb, cross, turned, x, order, sem,
+    links, patch, h, block, nb, cross, turned, x, order, flat_out, sem, own_sem, out_sems,
 ):
     fetch = pltpu.make_async_copy(adjacency, links, sem)
     fetch.start()
+    save = pltpu.make_async_copy(mid.at[pl.ds(1, COLS)], own, own_sem)
+    save.start()
     row0 = lax.axis_index("gx_0") * 4 + lax.axis_index("gx_1")
     col0 = (lax.axis_index("gy_0") * 2 + lax.axis_index("gy_1")) * COLS
     keep = past_mask()
@@ -461,8 +463,6 @@
     for c in range(4):
         for r, source in enumerate((up, mid, down)):
             patch[4 * r + c] = jnp.where(keep, source[c], 0.0)
-    own[0] = mid[1]
-    own[1] = mid[2]
     gap = jnp.zeros((128 - NEAR, K), F32)
     fetch.wait()
     for m in range(COLS):
@@ -554,18 +554,18 @@
         order[m, 25:97] = last
         dst = 97
         for a in range(R):
-            for b in range(a, R):
-                d = b - a
-                if d == 12:
-                    src = MIXED + a
-                elif d < 12:
-                    src = R * d + a
-                else:
-                    src = R * (R - d) + b
+            near_count = min(12, R - a)
+            order[m, dst : dst + near_count] = x[m, pl.ds(a, near_count, stride=R), :]
+            dst += near_count
+            for b in range(a + 12, R):
+                src = MIXED + a if b - a == 12 else R * (R - b + a) + b
                 order[m, dst : dst + 1] = x[m, src : src + 1]
                 dst += 1
-        flat = order[m].T
-        out[m] = flat[NEAR : NEAR + R, 0:NF]
+        flat_out[m] = order[m].T[NEAR : NEAR + R, 0:NF]
+        pltpu.make_async_copy(flat_out.at[m], out.at[m], out_sems.at[m]).start()
+    for m in range(COLS):
+        pltpu.make_async_copy(flat_out.at[m], out.at[m], out_sems.at[m]).wait()
+    save.wait()
 
 
 def fit_near(adjacency, *rest):
@@ -573,7 +573,7 @@
     return pl.pallas_call(
         near_kernel,
         in_specs=[pl.BlockSpec(memory_space=pl.ANY)] + [vm] * len(rest),
-        out_specs=[vm, vm],
+        out_specs=[pl.BlockSpec(memory_space=pl.ANY)] * 2,
         out_shape=[
             jax.ShapeDtypeStruct((COLS, R, NF), F32),
             jax.ShapeDtypeStruct((COLS, R, K), F32),
@@ -588,7 +588,10 @@
             pltpu.VMEM((COLS, NEAR, LANES), F32),
             pltpu.VMEM((COLS, OWN, 128), F32),
             pltpu.VMEM((COLS, 512, 128), F32),
+            pltpu.VMEM((COLS, R, NF), F32),
             pltpu.SemaphoreType.DMA,
+            pltpu.SemaphoreType.DMA,
+            pltpu.SemaphoreType.DMA((COLS,)),
         ],
         compiler_params=pltpu.CompilerParams(vmem_limit_bytes=ROOM),
         name="fit_near",

time: 57.8 us -> 57.7 us (level)
  transfers between devices with their start and end apart: 4 -> 4, of which waited for: 0 -> 0; matrix products, arithmetic and copies ran while one was open for 0% -> 0% of each run, Pallas kernels for 15% -> 14%
where the time goes in v8:
time: 57.7 us; the launch traced here: 57.4 us
  Pallas kernels  25 us (43%)
  blocking collectives  20 us (35%)
  starting transfers between devices  11.7 us (20%)
  between operations  0.7 us (1%)
    all_to_all x1, blocking collectives, body(): everyone = lax.all_to_all(stats, GX_GY, 0, 0, tiled=True)  20 us
    pallas_call x1, Pallas kernels, local_pass(): pl.pallas_call(local_kernel, in_specs=[pl.BlockSpec(memory_space=pltpu.SM...  8.51 us
    ppermute x2, starting transfers between devices, shifts(): lax.ppermute(x, axis, [(i, i + 1) for i in range(n - 1)])  8.49 us
    pallas_call x1, Pallas kernels, fit_own(): pl.pallas_call(own_kernel, out_shape=[pltpu.VMEM((COLS, OWN + R, K), BF)]...  8.32 us
    pallas_call x1, Pallas kernels, fit_near(): pl.pallas_call(near_kernel, in_specs=[pl.BlockSpec(memory_space=pl.ANY)]...  7.75 us
    ppermute x2, starting transfers between devices, shifts(): lax.ppermute(y, axis, [(i + 1, i) for i in range(n - 1)])  3.21 us
  transfers between devices with their start and end apart: 4, of which 0 were waited for; matrix products, arithmetic and copies ran while one was open for 0% of the time, Pallas kernels for 14%

profile of v8, /device:TPU:1, one launch (start us, length us, event | category | flops | bytes accessed | tf_op | source)
XLA Modules:
  0.0 57.4 jit_solution(5834221345777540664)
XLA Ops:
  0.6 8.5 %local.1 = (f32[4,24,512]{2,1,0:T(8,128)S(1)}, f32[4,24,512]{2,1,0:T(8,128)S(1)}, f32[128,128]{1,0:T(8,128)S(1)}) custom-call(s32[1,2]{1,0:T(1,128)} %counts.1, bf16[2,4,24,2048]{3,2,1,0:T(8,128)(2,1)} %bitcast.13, bf16[2,4,2048,512]{3,2,1,0:T(8,128)(2,1)} %bitcast.12), custom_call_target="tpu_custom_call" | custom-call | tf_op jit(solution)/shard_map/local/pallas_call | solution.py:111
  9.1 4.5 %collective-permute-start = (f32[4,24,512]{2,1,0:T(8,128)S(1)}, f32[4,24,512]{2,1,0:T(8,128)S(1)}, u32[]{:S(2)}, u32[]{:S(2)}) collective-permute-start(f32[4,24,512]{2,1,0:T(8,128)S(1)} %get-tuple-element.15.proj1), channel_id=1, source_target_pairs={{0,1},{1,2},{2,3},{3,4},{4,5},{5,6},{6,7},{8,9},{9,10},{10,11},{11... | collective-permute-start | bytes 589832 | tf_op jit(solution)/shard_map/ppermute | solution.py:604
  13.7 1.9 %collective-permute-start.1 = (f32[4,24,512]{2,1,0:T(8,128)S(1)}, f32[4,24,512]{2,1,0:T(8,128)S(1)}, u32[]{:S(2)}, u32[]{:S(2)}) collective-permute-start(f32[4,24,512]{2,1,0:T(8,128)S(1)} %get-tuple-element.16.proj0), channel_id=1, source_target_pairs={{1,0},{2,1},{3,2},{4,3},{5,4},{6,5},{7,6},{9,8},{10,9},{11,10},{12... | collective-permute-start | bytes 589832 | tf_op jit(solution)/shard_map/ppermute | solution.py:605
  15.6 20.0 %all_to_all.11 = f32[128,1,128]{2,1,0:T(1,128)S(1)} all-to-all(f32[128,1,128]{2,1,0:T(1,128)S(1)} %bitcast.11), channel_id=1, replica_groups=mesh['gx_0'=4,'gx_1'=4,'gy_0'=4,'gy_1'=2] {'gx_0','gx_1','gy_0','gy_1'}, dimensions={0} | all-to-all | bytes 131072 | tf_op jit(solution)/shard_map/all_to_all | solution.py:611
  35.5 0.0 collective-permute-done.left
  35.5 0.0 collective-permute-done.1.right
  35.6 0.4 states.1
  36.0 1.3 %collective-permute-start.3 = (f32[4,24,512]{2,1,0:T(8,128)S(1)}, f32[4,24,512]{2,1,0:T(8,128)S(1)}, u32[]{:S(2)}, u32[]{:S(2)}) collective-permute-start(f32[4,24,512]{2,1,0:T(8,128)S(1)} %get-tuple-element.18.mid), channel_id=1, source_target_pairs={{8,0},{16,8},{24,16},{32,24},{40,32},{48,40},{56,48},{64,56},{72,6... | collective-permute-start | bytes 589832 | tf_op jit(solution)/shard_map/ppermute | solution.py:605
  37.3 4.0 %collective-permute-start.2 = (f32[4,24,512]{2,1,0:T(8,128)S(1)}, f32[4,24,512]{2,1,0:T(8,128)S(1)}, u32[]{:S(2)}, u32[]{:S(2)}) collective-permute-start(f32[4,24,512]{2,1,0:T(8,128)S(1)} %get-tuple-element.18.mid), channel_id=1, source_target_pairs={{0,8},{8,16},{16,24},{24,32},{32,40},{40,48},{48,56},{56,64},{64,7... | collective-permute-start | bytes 589832 | tf_op jit(solution)/shard_map/ppermute | solution.py:604
  41.3 8.3 %fit_own.1 = (bf16[2,352,512]{2,1,0:T(8,128)(2,1)S(1)}, bf16[2,352,512]{2,1,0:T(8,128)(2,1)S(1)}, bf16[2,352,512]{2,1,0:T(8,128)(2,1)S(1)}, f32[2,328,384]{2,1,0:T(8,128)S(1)}, f32[2,128,128]{2,1,0:T(8,128)S(1)}) custom-call(f32[8,128]{1,0:T(8,128)S(1)} %get-tuple-element.17.gnorm, f32[4,24,512]{2,1,0:T(8,128)S(1)} %get-tuple-element.18.mid), custom_call_target="tpu_custom_call" | custom-call | tf_op jit(solution)/shard_map/fit_own/pallas_call | solution.py:432
  49.6 0.0 collective-permute-done.3.down
  49.6 0.0 collective-permute-done.2.up
  49.6 7.8 %fit_near.1 = (f32[2,24,397]{2,1,0:T(8,128)}, f32[2,24,512]{2,1,0:T(8,128)}) custom-call(s32[1,2,3]{2,1,0:T(2,128)} %adjacency.1, f32[8,128]{1,0:T(8,128)S(1)} %get-tuple-element.17.gnorm, f32[4,24,512]{2,1,0:T(8,128)S(1)} %get-tuple-element.18.mid, f32[4,24,512]{2,1,0:T(8,128)S(1)} %collective-permute-done.2.up, ...), custom_call_target="tpu_custom_call" | custom-call | tf_op jit(solution)/shard_map/fit_near/pallas_call | solution.py:573
Async XLA Ops:
  9.1 26.4 %collective-permute-start = (f32[4,24,512]{2,1,0:T(8,128)S(1)}, f32[4,24,512]{2,1,0:T(8,128)S(1)}, u32[]{:S(2)}, u32[]{:S(2)}) collective-permute-start(f32[4,24,512]{2,1,0:T(8,128)S(1)} %get-tuple-element.15.proj1), channel_id=1, source_target_pairs={{0,1},{1,2},{2,3},{3,4},{4,5},{5,6},{6,7},{8,9},{9,10},{10,11},{11... | collective-permute-start | bytes 589832 | tf_op jit(solution)/shard_map/ppermute | solution.py:604
  13.7 21.9 %collective-permute-start.1 = (f32[4,24,512]{2,1,0:T(8,128)S(1)}, f32[4,24,512]{2,1,0:T(8,128)S(1)}, u32[]{:S(2)}, u32[]{:S(2)}) collective-permute-start(f32[4,24,512]{2,1,0:T(8,128)S(1)} %get-tuple-element.16.proj0), channel_id=1, source_target_pairs={{1,0},{2,1},{3,2},{4,3},{5,4},{6,5},{7,6},{9,8},{10,9},{11,10},{12... | collective-permute-start | bytes 589832 | tf_op jit(solution)/shard_map/ppermute | solution.py:605
  36.0 13.6 %collective-permute-start.3 = (f32[4,24,512]{2,1,0:T(8,128)S(1)}, f32[4,24,512]{2,1,0:T(8,128)S(1)}, u32[]{:S(2)}, u32[]{:S(2)}) collective-permute-start(f32[4,24,512]{2,1,0:T(8,128)S(1)} %get-tuple-element.18.mid), channel_id=1, source_target_pairs={{8,0},{16,8},{24,16},{32,24},{40,32},{48,40},{56,48},{64,56},{72,6... | collective-permute-start | bytes 589832 | tf_op jit(solution)/shard_map/ppermute | solution.py:605
  37.3 12.3 %collective-permute-start.2 = (f32[4,24,512]{2,1,0:T(8,128)S(1)}, f32[4,24,512]{2,1,0:T(8,128)S(1)}, u32[]{:S(2)}, u32[]{:S(2)}) collective-permute-start(f32[4,24,512]{2,1,0:T(8,128)S(1)} %get-tuple-element.18.mid), channel_id=1, source_target_pairs={{0,8},{8,16},{16,24},{24,32},{32,40},{40,48},{48,56},{56,64},{64,7... | collective-permute-start | bytes 589832 | tf_op jit(solution)/shard_map/ppermute | solution.py:604

commit v9 on v8

--- a/solution.py
+++ b/solution.py
@@ -464,13 +464,18 @@
         for r, source in enumerate((up, mid, down)):
             patch[4 * r + c] = jnp.where(keep, source[c], 0.0)
     gap = jnp.zeros((128 - NEAR, K), F32)
-    fetch.wait()
-    for m in range(COLS):
-        rows = []
-        for b in range(NB):
-            link = links[0, m, b]
-            rows.append(patch[((link >> 4) - row0 + 1) * 4 + ((link & 15) - col0 + 1)])
-        nb[m, 0:128], nb[m, 128:256], nb[m, 256:384] = split3(jnp.concatenate(rows + [gap], axis=0))
+
+    def select(m):
+        def go():
+            if m == 0:
+                fetch.wait()
+            rows = []
+            for b in range(NB):
+                link = links[0, m, b]
+                rows.append(patch[((link >> 4) - row0 + 1) * 4 + ((link & 15) - col0 + 1)])
+            nb[m, 0:128], nb[m, 128:256], nb[m, 256:384] = split3(jnp.concatenate(rows + [gap], axis=0))
+
+        return go
 
     def after1(m, kind):
         def go():
@@ -518,14 +523,11 @@
 
         return go
 
-    work = []
-    for k in range(4):
-        for m in range(COLS):
-            work.append(after1(m, k))
-            if k < 2:
-                work.append(near_products(m, k))
-            else:
-                work.append(turn(m) if k == 2 else near_columns(m))
+    both = range(COLS)
+    work = [after1(m, k) for k in (0, 1) for m in both] + [select(m) for m in both]
+    work += [near_products(m, 0) for m in both] + [after1(m, 2) for m in both]
+    work += [near_products(m, 1) for m in both] + [after1(m, 3) for m in both]
+    work += [turn(m) for m in both] + [near_columns(m) for m in both]
     spread(invert(block, 9), 8, work)
     _, wide = iotas((256, 128))
     _, lane_n = iotas((NEAR, 128))

time: 57.7 us -> 57.6 us (level)
  transfers between devices with their start and end apart: 4 -> 4, of which waited for: 0 -> 0; matrix products, arithmetic and copies ran while one was open for 0% -> 0% of each run, Pallas kernels for 14% -> 15%
where the time goes in v9:
time: 57.6 us; the launch traced here: 57.3 us
  Pallas kernels  25 us (43%)
  blocking collectives  20 us (35%)
  starting transfers between devices  11.7 us (20%)
  between operations  0.7 us (1%)
    all_to_all x1, blocking collectives, body(): everyone = lax.all_to_all(stats, GX_GY, 0, 0, tiled=True)  20 us
    pallas_call x1, Pallas kernels, local_pass(): pl.pallas_call(local_kernel, in_specs=[pl.BlockSpec(memory_space=pltpu.SM...  8.51 us
    ppermute x2, starting transfers between devices, shifts(): lax.ppermute(x, axis, [(i, i + 1) for i in range(n - 1)])  8.49 us
    pallas_call x1, Pallas kernels, fit_own(): pl.pallas_call(own_kernel, out_shape=[pltpu.VMEM((COLS, OWN + R, K), BF)]...  8.32 us
    pallas_call x1, Pallas kernels, fit_near(): pl.pallas_call(near_kernel, in_specs=[pl.BlockSpec(memory_space=pl.ANY)]...  7.71 us
    ppermute x2, starting transfers between devices, shifts(): lax.ppermute(y, axis, [(i + 1, i) for i in range(n - 1)])  3.21 us
  transfers between devices with their start and end apart: 4, of which 0 were waited for; matrix products, arithmetic and copies ran while one was open for 0% of the time, Pallas kernels for 15%

profile of v9, /device:TPU:1, one launch (start us, length us, event | category | flops | bytes accessed | tf_op | source)
XLA Modules:
  0.0 57.3 jit_solution(374707169255094813)
XLA Ops:
  0.6 8.5 %local.1 = (f32[4,24,512]{2,1,0:T(8,128)S(1)}, f32[4,24,512]{2,1,0:T(8,128)S(1)}, f32[128,128]{1,0:T(8,128)S(1)}) custom-call(s32[1,2]{1,0:T(1,128)} %counts.1, bf16[2,4,24,2048]{3,2,1,0:T(8,128)(2,1)} %bitcast.13, bf16[2,4,2048,512]{3,2,1,0:T(8,128)(2,1)} %bitcast.12), custom_call_target="tpu_custom_call" | custom-call | tf_op jit(solution)/shard_map/local/pallas_call | solution.py:111
  9.1 4.5 %collective-permute-start = (f32[4,24,512]{2,1,0:T(8,128)S(1)}, f32[4,24,512]{2,1,0:T(8,128)S(1)}, u32[]{:S(2)}, u32[]{:S(2)}) collective-permute-start(f32[4,24,512]{2,1,0:T(8,128)S(1)} %get-tuple-element.15.proj1), channel_id=1, source_target_pairs={{0,1},{1,2},{2,3},{3,4},{4,5},{5,6},{6,7},{8,9},{9,10},{10,11},{11... | collective-permute-start | bytes 589832 | tf_op jit(solution)/shard_map/ppermute | solution.py:606
  13.7 1.9 %collective-permute-start.1 = (f32[4,24,512]{2,1,0:T(8,128)S(1)}, f32[4,24,512]{2,1,0:T(8,128)S(1)}, u32[]{:S(2)}, u32[]{:S(2)}) collective-permute-start(f32[4,24,512]{2,1,0:T(8,128)S(1)} %get-tuple-element.16.proj0), channel_id=1, source_target_pairs={{1,0},{2,1},{3,2},{4,3},{5,4},{6,5},{7,6},{9,8},{10,9},{11,10},{12... | collective-permute-start | bytes 589832 | tf_op jit(solution)/shard_map/ppermute | solution.py:607
  15.6 20.0 %all_to_all.11 = f32[128,1,128]{2,1,0:T(1,128)S(1)} all-to-all(f32[128,1,128]{2,1,0:T(1,128)S(1)} %bitcast.11), channel_id=1, replica_groups=mesh['gx_0'=4,'gx_1'=4,'gy_0'=4,'gy_1'=2] {'gx_0','gx_1','gy_0','gy_1'}, dimensions={0} | all-to-all | bytes 131072 | tf_op jit(solution)/shard_map/all_to_all | solution.py:613
  35.5 0.0 collective-permute-done.left
  35.5 0.0 collective-permute-done.1.right
  35.6 0.4 states.1
  36.0 1.3 %collective-permute-start.3 = (f32[4,24,512]{2,1,0:T(8,128)S(1)}, f32[4,24,512]{2,1,0:T(8,128)S(1)}, u32[]{:S(2)}, u32[]{:S(2)}) collective-permute-start(f32[4,24,512]{2,1,0:T(8,128)S(1)} %get-tuple-element.18.mid), channel_id=1, source_target_pairs={{8,0},{16,8},{24,16},{32,24},{40,32},{48,40},{56,48},{64,56},{72,6... | collective-permute-start | bytes 589832 | tf_op jit(solution)/shard_map/ppermute | solution.py:607
  37.3 4.0 %collective-permute-start.2 = (f32[4,24,512]{2,1,0:T(8,128)S(1)}, f32[4,24,512]{2,1,0:T(8,128)S(1)}, u32[]{:S(2)}, u32[]{:S(2)}) collective-permute-start(f32[4,24,512]{2,1,0:T(8,128)S(1)} %get-tuple-element.18.mid), channel_id=1, source_target_pairs={{0,8},{8,16},{16,24},{24,32},{32,40},{40,48},{48,56},{56,64},{64,7... | collective-permute-start | bytes 589832 | tf_op jit(solution)/shard_map/ppermute | solution.py:606
  41.3 8.3 %fit_own.1 = (bf16[2,352,512]{2,1,0:T(8,128)(2,1)S(1)}, bf16[2,352,512]{2,1,0:T(8,128)(2,1)S(1)}, bf16[2,352,512]{2,1,0:T(8,128)(2,1)S(1)}, f32[2,328,384]{2,1,0:T(8,128)S(1)}, f32[2,128,128]{2,1,0:T(8,128)S(1)}) custom-call(f32[8,128]{1,0:T(8,128)S(1)} %get-tuple-element.17.gnorm, f32[4,24,512]{2,1,0:T(8,128)S(1)} %get-tuple-element.18.mid), custom_call_target="tpu_custom_call" | custom-call | tf_op jit(solution)/shard_map/fit_own/pallas_call | solution.py:432
  49.6 0.0 collective-permute-done.3.down
  49.6 0.0 collective-permute-done.2.up
  49.6 7.7 %fit_near.1 = (f32[2,24,397]{2,1,0:T(8,128)}, f32[2,24,512]{2,1,0:T(8,128)}) custom-call(s32[1,2,3]{2,1,0:T(2,128)} %adjacency.1, f32[8,128]{1,0:T(8,128)S(1)} %get-tuple-element.17.gnorm, f32[4,24,512]{2,1,0:T(8,128)S(1)} %get-tuple-element.18.mid, f32[4,24,512]{2,1,0:T(8,128)S(1)} %collective-permute-done.2.up, ...), custom_call_target="tpu_custom_call" | custom-call | tf_op jit(solution)/shard_map/fit_near/pallas_call | solution.py:575
Async XLA Ops:
  9.1 26.4 %collective-permute-start = (f32[4,24,512]{2,1,0:T(8,128)S(1)}, f32[4,24,512]{2,1,0:T(8,128)S(1)}, u32[]{:S(2)}, u32[]{:S(2)}) collective-permute-start(f32[4,24,512]{2,1,0:T(8,128)S(1)} %get-tuple-element.15.proj1), channel_id=1, source_target_pairs={{0,1},{1,2},{2,3},{3,4},{4,5},{5,6},{6,7},{8,9},{9,10},{10,11},{11... | collective-permute-start | bytes 589832 | tf_op jit(solution)/shard_map/ppermute | solution.py:606
  13.7 21.9 %collective-permute-start.1 = (f32[4,24,512]{2,1,0:T(8,128)S(1)}, f32[4,24,512]{2,1,0:T(8,128)S(1)}, u32[]{:S(2)}, u32[]{:S(2)}) collective-permute-start(f32[4,24,512]{2,1,0:T(8,128)S(1)} %get-tuple-element.16.proj0), channel_id=1, source_target_pairs={{1,0},{2,1},{3,2},{4,3},{5,4},{6,5},{7,6},{9,8},{10,9},{11,10},{12... | collective-permute-start | bytes 589832 | tf_op jit(solution)/shard_map/ppermute | solution.py:607
  36.0 13.6 %collective-permute-start.3 = (f32[4,24,512]{2,1,0:T(8,128)S(1)}, f32[4,24,512]{2,1,0:T(8,128)S(1)}, u32[]{:S(2)}, u32[]{:S(2)}) collective-permute-start(f32[4,24,512]{2,1,0:T(8,128)S(1)} %get-tuple-element.18.mid), channel_id=1, source_target_pairs={{8,0},{16,8},{24,16},{32,24},{40,32},{48,40},{56,48},{64,56},{72,6... | collective-permute-start | bytes 589832 | tf_op jit(solution)/shard_map/ppermute | solution.py:607
  37.3 12.3 %collective-permute-start.2 = (f32[4,24,512]{2,1,0:T(8,128)S(1)}, f32[4,24,512]{2,1,0:T(8,128)S(1)}, u32[]{:S(2)}, u32[]{:S(2)}) collective-permute-start(f32[4,24,512]{2,1,0:T(8,128)S(1)} %get-tuple-element.18.mid), channel_id=1, source_target_pairs={{0,8},{8,16},{16,24},{24,32},{32,40},{40,48},{48,56},{56,64},{64,7... | collective-permute-start | bytes 589832 | tf_op jit(solution)/shard_map/ppermute | solution.py:606
